TPU v7x, 32 devices: a 4x4x1 block of a 4x4x8 slice. The times are simulated.
32 devices in a mesh: dp: 1 (over z), tp: 4 (over y), ep: 8 (over x, core).
Axes of the slice: x: 4, y: 4, z: 1, core: 2. Of those that a mesh axis runs over, the one named last changes fastest.
The devices are a block of a 4x4x8 slice.
Arguments:
- x: bfloat16 [64, 1024, 768], P(('dp', 'ep'))
- src_len: int32 [64], P(('dp', 'ep'))
- expert_idx: int32 [64, 1024, 2], P(('dp', 'ep'))
- ln_gain: float32 [4, 768], replicated
- ln_bias: float32 [4, 768], replicated
- w_query: bfloat16 [2, 768, 12, 64], P(None, None, 'tp')
- b_query: float32 [2, 12, 64], P(None, 'tp')
- w_key: bfloat16 [2, 768, 12, 64], P(None, None, 'tp')
- w_value: bfloat16 [2, 768, 12, 64], P(None, None, 'tp')
- b_value: float32 [2, 12, 64], P(None, 'tp')
- w_attn_out: bfloat16 [2, 12, 64, 768], P(None, 'tp')
- b_attn_out: float32 [2, 768], replicated
- w_fc1: bfloat16 [768, 3072], P(None, 'tp')
- b_fc1: float32 [3072], P('tp')
- w_fc2: bfloat16 [3072, 768], P('tp')
- b_fc2: float32 [768], replicated
- w_router: float32 [768, 128], replicated
- w_exp_in: bfloat16 [128, 768, 3072], P('ep', None, 'tp')
- b_exp_in: float32 [128, 3072], P('ep', 'tp')
- w_exp_out: bfloat16 [128, 3072, 768], P('ep', 'tp')
- b_exp_out: float32 [128, 768], P('ep')
Outputs:
- output: bfloat16 [64, 1024, 768], P(('dp', 'ep'))
All inputs are finite; a program needn't handle non-finite values.
Results may differ from a plain program's by a relative error of at most 0.0144607.
Values are sent between devices in bfloat16 or wider.
A program may use at most 768 MiB of HBM per device.

v0:
```python
import jax
import jax.numpy as jnp
from jax import lax
from jax.sharding import PartitionSpec as P

LN_EPS = 1e-5


def layer_norm(hidden, gain, shift):
    hidden = hidden.astype(jnp.float32)
    centered = hidden - jnp.mean(hidden, axis=-1, keepdims=True)
    variance = jnp.mean(centered * centered, axis=-1, keepdims=True)
    return centered * lax.rsqrt(variance + LN_EPS) * gain + shift


def attention_layer(residual, key_ok, gain, shift, w_q, b_q, w_k, w_v, b_v, w_o, b_o):
    normed = layer_norm(residual, gain, shift).astype(jnp.bfloat16)
    query = (jnp.einsum('rsd,dhk->rshk', normed, w_q, preferred_element_type=jnp.float32) + b_q).astype(jnp.bfloat16)
    keys = jnp.einsum('rsd,dhk->rshk', normed, w_k, preferred_element_type=jnp.float32).astype(jnp.bfloat16)
    values = (jnp.einsum('rsd,dhk->rshk', normed, w_v, preferred_element_type=jnp.float32) + b_v).astype(jnp.bfloat16)
    scores = jnp.einsum('rqhk,rshk->rhqs', query, keys, preferred_element_type=jnp.float32) * (w_q.shape[-1] ** -0.5)
    scores = jnp.where(key_ok[:, None, None, :], scores, -1e30)
    attn_probs = jax.nn.softmax(scores, axis=-1).astype(jnp.bfloat16)
    context = jnp.einsum('rhqs,rshk->rqhk', attn_probs, values, preferred_element_type=jnp.float32).astype(jnp.bfloat16)
    partial = jnp.einsum('rqhk,hkd->rqd', context, w_o, preferred_element_type=jnp.float32).astype(jnp.bfloat16)
    total = lax.psum(partial, 'tp')
    return (residual.astype(jnp.float32) + total.astype(jnp.float32) + b_o).astype(jnp.bfloat16)


def dense_ffn(residual, gain, shift, w_in, b_in, w_out, b_out):
    normed = layer_norm(residual, gain, shift).astype(jnp.bfloat16)
    inner = jax.nn.relu(jnp.einsum('rsd,df->rsf', normed, w_in, preferred_element_type=jnp.float32) + b_in).astype(jnp.bfloat16)
    partial = jnp.einsum('rsf,fd->rsd', inner, w_out, preferred_element_type=jnp.float32).astype(jnp.bfloat16)
    total = lax.psum(partial, 'tp')
    return (residual.astype(jnp.float32) + total.astype(jnp.float32) + b_out).astype(jnp.bfloat16)


def route_tokens(normed_f32, key_ok, expert_idx, w_router, capacity):
    tokens = key_ok.size
    num_experts = w_router.shape[1]
    logits = jnp.dot(normed_f32.reshape(tokens, -1), w_router, preferred_element_type=jnp.float32)
    valid = key_ok.reshape(tokens)
    first = expert_idx[..., 0].reshape(tokens)
    second = expert_idx[..., 1].reshape(tokens)
    logit_first = jnp.take_along_axis(logits, first[:, None], axis=1)[:, 0]
    logit_second = jnp.take_along_axis(logits, second[:, None], axis=1)[:, 0]
    gate_first = jax.nn.sigmoid(logit_first - logit_second)
    gate_second = jax.nn.sigmoid(logit_second - logit_first)
    expert_ids = jnp.arange(num_experts, dtype=jnp.int32)
    hot_first = ((first[:, None] == expert_ids) & valid[:, None]).astype(jnp.int32)
    hot_second = ((second[:, None] == expert_ids) & valid[:, None]).astype(jnp.int32)
    rank_first = jnp.cumsum(hot_first, axis=0) - 1
    rank_second = jnp.cumsum(hot_second, axis=0) - 1 + jnp.sum(hot_first, axis=0)
    slot_first = jnp.sum(rank_first * hot_first, axis=1)
    slot_second = jnp.sum(rank_second * hot_second, axis=1)
    dump_slot = num_experts * capacity
    dest_first = jnp.where(valid & (slot_first < capacity), first * capacity + slot_first, dump_slot)
    dest_second = jnp.where(valid & (slot_second < capacity), second * capacity + slot_second, dump_slot)
    return gate_first, gate_second, dest_first, dest_second


def slot_table(dest_first, dest_second, dump_slot):
    tokens = dest_first.shape[0]
    token_ids = jnp.arange(tokens, dtype=jnp.int32)
    table = jnp.full((dump_slot + 1,), tokens, jnp.int32)
    table = table.at[dest_first].set(token_ids).at[dest_second].set(token_ids)
    return table[:dump_slot]


def solution(mesh):
    ep_size = mesh.shape['ep']

    def local_fn(x, src_len, expert_idx, ln_gain, ln_bias, w_query, b_query, w_key, w_value, b_value, w_attn_out, b_attn_out, w_fc1, b_fc1, w_fc2, b_fc2, w_router, w_exp_in, b_exp_in, w_exp_out, b_exp_out):
        rows, seq_len, d_model = x.shape
        tokens = rows * seq_len
        num_experts = w_router.shape[1]
        capacity = 2 * (-(-tokens // num_experts))
        dump_slot = num_experts * capacity
        local_experts = w_exp_in.shape[0]
        key_ok = jnp.arange(seq_len)[None, :] < src_len[:, None]
        hidden = attention_layer(x, key_ok, ln_gain[0], ln_bias[0], w_query[0], b_query[0], w_key[0], w_value[0], b_value[0], w_attn_out[0], b_attn_out[0])
        hidden = dense_ffn(hidden, ln_gain[1], ln_bias[1], w_fc1, b_fc1, w_fc2, b_fc2)
        hidden = attention_layer(hidden, key_ok, ln_gain[2], ln_bias[2], w_query[1], b_query[1], w_key[1], w_value[1], b_value[1], w_attn_out[1], b_attn_out[1])
        normed_f32 = layer_norm(hidden, ln_gain[3], ln_bias[3])
        gate_first, gate_second, dest_first, dest_second = route_tokens(normed_f32, key_ok, expert_idx, w_router, capacity)
        table = slot_table(dest_first, dest_second, dump_slot)
        padded = jnp.concatenate([normed_f32.astype(jnp.bfloat16).reshape(tokens, d_model), jnp.zeros((1, d_model), jnp.bfloat16)], axis=0)
        dispatch = padded[table].reshape(num_experts, capacity, d_model)
        received = lax.all_to_all(dispatch, 'ep', 0, 0, tiled=True).reshape(ep_size, local_experts, capacity, d_model)
        inner = jax.nn.relu(jnp.einsum('gecd,edf->gecf', received, w_exp_in, preferred_element_type=jnp.float32) + b_exp_in[None, :, None, :]).astype(jnp.bfloat16)
        partial = jnp.einsum('gecf,efd->gecd', inner, w_exp_out, preferred_element_type=jnp.float32).astype(jnp.bfloat16)
        summed = lax.psum(partial, 'tp')
        expert_out = (summed.astype(jnp.float32) + b_exp_out[None, :, None, :]).astype(jnp.bfloat16)
        returned = lax.all_to_all(expert_out.reshape(num_experts, capacity, d_model), 'ep', 0, 0, tiled=True)
        flat = jnp.concatenate([returned.reshape(dump_slot, d_model), jnp.zeros((1, d_model), jnp.bfloat16)], axis=0)
        combined = gate_first[:, None] * flat[dest_first].astype(jnp.float32) + gate_second[:, None] * flat[dest_second].astype(jnp.float32)
        result = hidden.reshape(tokens, d_model).astype(jnp.float32) + combined
        return result.astype(jnp.bfloat16).reshape(rows, seq_len, d_model)

    in_specs = (P(('dp', 'ep'), None, None), P(('dp', 'ep')), P(('dp', 'ep'), None, None), P(), P(), P(None, None, 'tp', None), P(None, 'tp', None), P(None, None, 'tp', None), P(None, None, 'tp', None), P(None, 'tp', None), P(None, 'tp', None, None), P(), P(None, 'tp'), P('tp'), P('tp', None), P(), P(), P('ep', None, 'tp'), P('ep', 'tp'), P('ep', 'tp', None), P('ep', None))
    return jax.shard_map(local_fn, mesh=mesh, in_specs=in_specs, out_specs=P(('dp', 'ep'), None, None), check_vma=False)
```

profile of v0, /device:TPU:97, one launch (start us, length us, event | category | flops | bytes accessed | tf_op | source)
XLA Modules:
  0.0 2315.2 jit_solution(4886192389071423402)
XLA Ops:
  9.3 6.4 convert_reduce_fusion.3
  15.7 8.1 fusion.31
  24.5 11.1 convolution_convert_fusion.1
  35.6 10.9 fusion.124
  47.0 8.0 add_convert_fusion.3
  55.0 41.3 %fusion.168 = (f32[8,3,1024]{2,1,0:T(4,128)S(1)}, f32[8,3,1024,1024]{2,3,1,0:T(8,128)}) fusion(pred[8,1024]{1,0:T(8,128)(4,1)S(1)} %get-tuple-element.40, bf16[8,1024,3,64]{1,3,2,0:T(8,128)(2,1)} %add_convert_fusion.3, bf16[8,1024,3,64]{1,3,2,0:T(8,128)(2,1)} %convolution_convert_fusion.1), kind=kOutput, calls=%fused_computation.223 | convolution fusion | flops 3321889792 | bytes 107061248 | tf_op jit(solution)/shard_map/sub | solution.py:23
  96.4 35.3 %fusion.202 = bf16[8,1024,3,64]{1,3,2,0:T(8,128)(2,1)} fusion(f32[8,3,1024,1024]{2,3,1,0:T(8,128)} %get-tuple-element.42, f32[8,3,1024]{2,1,0:T(4,128)S(1)} %get-tuple-element.41, f32[8,1024,3,64]{1,3,2,0:T(8,128)} %fusion.124, f32[3,64]{1,0:T(4,128)S(1)} %bitcast.226), kind=kOutput, calls=%fused_computation.121.clone.2 | convolution fusion | flops 3276275712 | bytes 110199552 | tf_op jit(solution)/shard_map/rhqs,rshk->rqhk/dot_general | solution.py:24
  131.7 10.2 bitcast_convert_fusion.1
  143.2 225.3 %all-reduce.7.cloned.1.call-done = bf16[8,1024,768]{2,1,0:T(8,128)(2,1)} async-done(((bf16[8,1024,768]{2,1,0:T(8,128)(2,1)}), bf16[8,1024,768]{2,1,0:T(8,128)(2,1)}) %all-reduce.7.cloned.1.call-update) | async-done | bytes 12582928 | tf_op jit(solution)/shard_map/psum | solution.py:26
  368.5 16.0 convert_reduce_fusion.2
  384.5 8.2 fusion.27
  392.7 25.7 %fusion.86 = bf16[8,1024,768]{2,1,0:T(8,128)(2,1)} fusion(bf16[8,1024,768]{2,1,0:T(8,128)(2,1)} %get-tuple-element.25, f32[768]{0:T(1024)S(1)} %copy-done.54, f32[768]{0:T(1024)S(1)} %copy-done.40, f32[768]{0:T(1024)S(1)} %copy-done.41, f32[8,1024]{1,0:T(8,128)S(1)} %add_rsqrt_fusion.2, f32[8,1024]{1,0:T(8,128)S(1)} %broadcast_multiply_fusion.2, ...), kind=kOutput, calls=%fused_computation.96 | convolution fusion | flops 19390267392 | bytes 27599872 | tf_op jit(solution)/shard_map/rsf,fd->rsd/dot_general | solution.py:33
  419.1 222.2 %all-reduce.9.cloned.1.call-done = bf16[8,1024,768]{2,1,0:T(8,128)(2,1)} async-done(((bf16[8,1024,768]{2,1,0:T(8,128)(2,1)}), bf16[8,1024,768]{2,1,0:T(8,128)(2,1)}) %all-reduce.9.cloned.1.call-update) | async-done | bytes 12582928 | tf_op jit(solution)/shard_map/psum | solution.py:34
  641.2 15.8 convert_reduce_fusion.1
  657.0 8.2 fusion.23
  665.2 11.3 convolution_convert_fusion
  676.5 8.8 fusion.119
  685.3 7.9 add_convert_fusion.1
  693.2 41.5 %fusion.169 = (f32[8,3,1024]{2,1,0:T(4,128)S(1)}, f32[8,3,1024,1024]{2,3,1,0:T(8,128)}) fusion(pred[8,1024]{1,0:T(8,128)(4,1)S(1)} %copy-done.33, bf16[8,1024,3,64]{1,3,2,0:T(8,128)(2,1)} %add_convert_fusion.1, bf16[8,1024,3,64]{1,3,2,0:T(8,128)(2,1)} %convolution_convert_fusion), kind=kOutput, calls=%fused_computation.224 | convolution fusion | flops 3321889792 | bytes 107061248 | tf_op jit(solution)/shard_map/sub | solution.py:23
  734.8 33.9 %fusion.200 = bf16[8,1024,3,64]{1,3,2,0:T(8,128)(2,1)S(1)} fusion(f32[8,3,1024,1024]{2,3,1,0:T(8,128)} %get-tuple-element.44, f32[8,3,1024]{2,1,0:T(4,128)S(1)} %get-tuple-element.43, f32[8,1024,3,64]{1,3,2,0:T(8,128)} %fusion.119, f32[3,64]{1,0:T(4,128)S(1)} %bitcast.223), kind=kOutput, calls=%fused_computation.120.clone.2 | convolution fusion | flops 3276275712 | bytes 110199552 | tf_op jit(solution)/shard_map/rhqs,rshk->rqhk/dot_general | solution.py:24
  768.7 6.5 bitcast_convert_fusion
  783.6 4.4 copy.44
  792.4 2.8 add_add_fusion.1
  797.7 4.5 convert_reduce_fusion.4
  802.3 4.1 fusion.90
  807.3 30.5 %scatter_custom_fusion = s32[16385]{0:T(1024)S(1)} fusion(s32[8192]{0:T(1024)S(1)} %bitcast.217, s32[8192]{0:T(1024)S(1)} %iota.26, s32[]{:T(128)} %constant.56.clone.1), kind=kCustom, calls=%fused_computation.167 | custom fusion | bytes 65544 | tf_op jit(solution)/shard_map/scatter | solution.py:66
  837.8 30.5 %scatter_fusion = s32[16385]{0:T(1024)S(1)} fusion(s32[16385]{0:T(1024)S(1)} %scatter_custom_fusion, s32[8192]{0:T(1024)S(1)} %bitcast.212, s32[8192]{0:T(1024)S(1)} %iota.27), kind=kCustom, calls=%fused_computation.6 | custom fusion | bytes 131072 | tf_op jit(solution)/shard_map/scatter | solution.py:66
  868.3 129.7 %all-reduce.11.cloned.1.call-done = bf16[8,1024,768]{2,1,0:T(8,128)(2,1)} async-done(((bf16[8,1024,768]{2,1,0:T(8,128)(2,1)}), bf16[8,1024,768]{2,1,0:T(8,128)(2,1)}) %all-reduce.11.cloned.1.call-update) | async-done | bytes 12582928 | tf_op jit(solution)/shard_map/psum | solution.py:26
  998.0 15.6 convert_reduce_fusion
  1013.6 8.1 fusion.20
  1021.8 8.5 fusion.134
  1030.3 5.2 concatenate.6
  1035.5 79.3 %gather_fusion = bf16[16384,768]{1,0:T(8,128)(2,1)} fusion(bf16[8193,768]{1,0:T(8,128)(2,1)} %concatenate.6, s32[16384]{0:T(1024)S(1)} %fusion.137), kind=kCustom, calls=%fused_computation.2 | custom fusion | bytes 50397184 | tf_op jit(solution)/shard_map/gather | solution.py:88
  1114.8 283.9 %all_to_all.10 = bf16[128,128,768]{2,1,0:T(8,128)(2,1)} all-to-all(bf16[128,128,768]{2,1,0:T(8,128)(2,1)} %bitcast.197), channel_id=1, replica_groups=mesh['dp'=1,'tp'=4,'ep'=8] {'ep'}, dimensions={0} | all-to-all | bytes 50331648 | tf_op jit(solution)/shard_map/all_to_all | solution.py:89
  1398.7 45.5 %convert_bitcast_fusion = bf16[8,16,128,768]{3,2,0,1:T(8,128)(2,1)} fusion(bf16[16,768,768]{2,1,0:T(8,128)(2,1)} %param.42, f32[16,768]{1,0:T(8,128)S(1)} %copy-done.53, bf16[8,16,128,768]{3,2,1,0:T(8,128)(2,1)} %bitcast.202, bf16[16,768,768]{2,1,0:T(8,128)(2,1)} %param.40), kind=kOutput, calls=%fused_computation.78 | convolution fusion | flops 38705037312 | bytes 88129536 | tf_op jit(solution)/shard_map/gecf,efd->gecd/dot_general | solution.py:91
  1444.3 423.3 %all-reduce.13.cloned.1.call-done = bf16[8,16,128,768]{3,2,0,1:T(8,128)(2,1)} async-done(((bf16[8,16,128,768]{3,2,0,1:T(8,128)(2,1)}), bf16[8,16,128,768]{3,2,0,1:T(8,128)(2,1)}) %all-reduce.13.cloned.1.call-update) | async-done | bytes 25165840 | tf_op jit(solution)/shard_map/psum | solution.py:92
  1867.6 14.7 add_convert_fusion
  1882.3 8.6 copy.46
  1891.0 7.5 all-to-all-start.1
  1898.9 8.6 fusion.22
  1907.5 5.0 fusion.170
  1912.5 126.4 %gather_fusion.3 = f32[8192]{0:T(1024)S(1)} fusion(f32[8192,128]{1,0:T(8,128)} %fusion.170, s32[8192]{0:T(1024)S(1)} %bitcast.193), kind=kCustom, calls=%fused_computation.clone | custom fusion | bytes 131072 | tf_op jit(solution)/shard_map/jit(take_along_axis)/gather | solution.py:45
  2039.0 126.5 %gather_fusion.4 = f32[8192]{0:T(1024)S(1)} fusion(f32[8192,128]{1,0:T(8,128)} %fusion.170, s32[8192]{0:T(1024)S(1)} %bitcast.192), kind=kCustom, calls=%fused_computation.1.clone | custom fusion | bytes 131072 | tf_op jit(solution)/shard_map/jit(take_along_axis)/gather | solution.py:46
  2165.9 6.0 all-to-all-done.1
  2171.8 20.5 concatenate.7
  2192.3 48.8 %gather_fusion.2 = bf16[8192,768]{1,0:T(8,128)(2,1)} fusion(bf16[16385,768]{1,0:T(8,128)(2,1)} %concatenate.7, s32[8192]{0:T(1024)S(1)} %broadcast_clamp_fusion), kind=kCustom, calls=%fused_computation.4 | custom fusion | bytes 25198592 | tf_op jit(solution)/shard_map/gather | solution.py:96
  2241.2 48.7 %gather_fusion.1 = bf16[8192,768]{1,0:T(8,128)(2,1)} fusion(bf16[16385,768]{1,0:T(8,128)(2,1)} %concatenate.7, s32[8192]{0:T(1024)S(1)} %broadcast_clamp_fusion.1), kind=kCustom, calls=%fused_computation.3 | custom fusion | bytes 25198592 | tf_op jit(solution)/shard_map/gather | solution.py:96
  2289.9 18.4 fusion.41
  (175 shorter events, 22.9 us)
Async XLA Ops:
  6.5 386.1 %copy-start = (bf16[768,768]{1,0:T(8,128)(2,1)S(1)}, bf16[768,768]{1,0:T(8,128)(2,1)}, u32[]{:S(2)}) copy-start(bf16[768,768]{1,0:T(8,128)(2,1)} %param.37) | copy-start | bytes 3538948
  6.6 361.9 %all-reduce.7.cloned.1.call-start = ((), (), s32[]{:S(2)}) async-start(), calls=%async_computation.2 | async-start | bytes 25165824 | tf_op jit(solution)/shard_map/psum | solution.py:26
  8.0 47.0 %copy-start.32 = (pred[8,1024]{1,0:T(8,128)(4,1)}, pred[8,1024]{1,0:T(8,128)(4,1)S(1)}, u32[]{:S(2)}) copy-start(pred[8,1024]{1,0:T(8,128)(4,1)S(1)} %get-tuple-element.40) | copy-start | bytes 24580
  9.3 14.5 copy-start.30
  9.3 14.5 copy-start.31
  9.3 15.2 copy-start.45
  24.5 11.1 copy-start.47
  24.5 22.5 slice-start
  24.5 22.5 slice-start.1
  35.6 10.9 copy-start.42
  35.6 11.5 slice-start.2
  35.6 11.5 copy-start.49
  96.3 35.3 %copy-start.51 = (bf16[2,3,64,768]{3,2,1,0:T(8,128)(2,1)S(1)}, bf16[2,3,64,768]{3,2,1,0:T(8,128)(2,1)}, u32[]{:S(2)}) copy-start(bf16[2,3,64,768]{3,2,1,0:T(8,128)(2,1)} %param.33) | copy-start | bytes 1769476
  141.9 499.3 %all-reduce.9.cloned.1.call-start = ((), (), s32[]{:S(2)}) async-start(), calls=%async_computation.3 | async-start | bytes 25165824 | tf_op jit(solution)/shard_map/psum | solution.py:34
  384.4 8.3 copy-start.40
  384.4 8.3 copy-start.41
  384.4 8.3 copy-start.44
  384.4 8.3 copy-start.54
  418.4 222.8 %copy-start.37 = (f32[768]{0:T(1024)S(1)}, f32[768]{0:T(1024)}, u32[]{:S(2)}) copy-start(f32[768]{0:T(1024)} %param.38) | copy-start | bytes 9220
  418.5 579.5 %all-reduce.11.cloned.1.call-start = ((), (), s32[]{:S(2)}) async-start(), calls=%async_computation.4 | async-start | bytes 25165824 | tf_op jit(solution)/shard_map/psum | solution.py:26
  657.0 8.2 copy-start.38
  657.0 8.2 copy-start.39
  657.0 8.2 copy-start.46
  665.2 11.3 copy-start.2
  665.2 11.3 copy-start.48
  676.5 8.8 copy-start.50
  734.8 33.9 %copy-start.52 = (bf16[2,3,64,768]{3,2,1,0:T(8,128)(2,1)S(1)}, bf16[2,3,64,768]{3,2,1,0:T(8,128)(2,1)}, u32[]{:S(2)}) copy-start(bf16[2,3,64,768]{3,2,1,0:T(8,128)(2,1)} %param.33) | copy-start | bytes 1769476
  775.2 12.8 copy-start.28
  775.2 1092.4 %all-reduce.13.cloned.1.call-start = ((), (), s32[]{:S(2)}) async-start(), calls=%async_computation.5 | async-start | bytes 50331648 | tf_op jit(solution)/shard_map/psum | solution.py:92
  776.1 30.3 %copy-start.6 = (s32[8,1024,1]{1,2,0:T(1,128)}, s32[8,1024,1]{1,2,0:T(1,128)S(1)}, u32[]{:S(2)}) copy-start(s32[8,1024,1]{1,2,0:T(1,128)S(1)} %get-tuple-element.26) | copy-start | bytes 98308
  776.1 30.3 %copy-start.8 = (s32[8,1024,1]{1,2,0:T(1,128)}, s32[8,1024,1]{1,2,0:T(1,128)S(1)}, u32[]{:S(2)}) copy-start(s32[8,1024,1]{1,2,0:T(1,128)S(1)} %get-tuple-element.27) | copy-start | bytes 98308
  788.0 9.7 copy-start.27
  792.4 9.9 copy-start.5
  807.3 61.0 %copy-start.13 = (s32[8192,1]{0,1:T(1,128)}, s32[8192,1]{0,1:T(1,128)S(1)}, u32[]{:S(2)}) copy-start(s32[8192,1]{0,1:T(1,128)S(1)} %get-tuple-element.31) | copy-start | bytes 98308
  807.3 61.0 %copy-start.19 = (s32[8192,1]{0,1:T(1,128)}, s32[8192,1]{0,1:T(1,128)S(1)}, u32[]{:S(2)}) copy-start(s32[8192,1]{0,1:T(1,128)S(1)} %get-tuple-element.32) | copy-start | bytes 98308
  837.8 160.2 %copy-start.29 = (f32[768]{0:T(1024)S(1)}, f32[768]{0:T(1024)}, u32[]{:S(2)}) copy-start(f32[768]{0:T(1024)} %get-tuple-element.18) | copy-start | bytes 9220
  1013.6 8.2 copy-start.23
  1013.6 8.2 copy-start.25
  1013.6 16.7 copy-start.10
  1021.7 8.6 copy-start.15
  1114.8 283.9 %copy-start.53 = (f32[16,768]{1,0:T(8,128)S(1)}, f32[16,768]{1,0:T(8,128)}, u32[]{:S(2)}) copy-start(f32[16,768]{1,0:T(8,128)} %param.41) | copy-start | bytes 147460
  1444.3 423.3 %copy-start.22 = (f32[16,768]{1,0:T(8,128)S(1)}, f32[16,768]{1,0:T(8,128)}, u32[]{:S(2)}) copy-start(f32[16,768]{1,0:T(8,128)} %param.43) | copy-start | bytes 147460
  1890.9 7.9 copy-start.11
  1891.0 280.9 %all-to-all-start.1 = ((bf16[128,128,768]{2,1,0:T(8,128)(2,1)}), bf16[128,128,768]{2,1,0:T(8,128)(2,1)}, u32[]{:S(2)}, u32[]{:S(2)}) async-start(bf16[128,128,768]{2,1,0:T(8,128)(2,1)} %bitcast.196), calls=%async_computation.1 | async-start | bytes 50331648 | tf_op jit(solution)/shard_map/all_to_all | solution.py:94
  1898.9 8.6 copy-start.12
  2039.0 126.5 %copy-start.7 = (s32[8,1024,1]{1,2,0:T(1,128)S(1)}, s32[8,1024,1]{1,2,0:T(1,128)}, u32[]{:S(2)}) copy-start(s32[8,1024,1]{1,2,0:T(1,128)} %copy-done.6) | copy-start | bytes 98308
  2039.0 126.5 %copy-start.9 = (s32[8,1024,1]{1,2,0:T(1,128)S(1)}, s32[8,1024,1]{1,2,0:T(1,128)}, u32[]{:S(2)}) copy-start(s32[8,1024,1]{1,2,0:T(1,128)} %copy-done.8) | copy-start | bytes 98308
  2289.9 18.4 copy-start.1
  (15 other events, 69.8 us)
Sparse Core Ops, SparseCore 0:
  142.1 226.3 all-reduce.6
  418.6 222.5 all-reduce.8
  775.4 222.5 all-reduce.10
  1444.4 423.1 all-reduce.12
where the time goes:
time: 2330 us; the launch traced here: 2320 us
  waiting for transfers between devices  1010 us (43%)
  local copies, waits for them, and re-layouts  541 us (23%)
  matrix products  303 us (13%)
  blocking collectives  284 us (12%)
  other arithmetic  158 us (7%)
    psum x1, waiting for transfers between devices, local_fn(): summed = lax.psum(partial, 'tp')  423 us
    psum x2, waiting for transfers between devices, attention_layer(): total = lax.psum(partial, 'tp')  355 us
    all_to_all x1, blocking collectives, local_fn(): lax.all_to_all(dispatch, 'ep', 0, 0, tiled=True)  284 us
    psum x1, waiting for transfers between devices, dense_ffn(): total = lax.psum(partial, 'tp')  222 us
    gather x1, local copies, waits for them, and re-layouts, route_tokens(): logit_second = jnp.take_along_axis(logits, second[:, None], axis=1)[:, 0]  126 us
    gather x1, local copies, waits for them, and re-layouts, route_tokens(): logit_first = jnp.take_along_axis(logits, first[:, None], axis=1)[:, 0]  126 us
    sub x2, matrix products, attention_layer(): attn_probs = jax.nn.softmax(scores, axis=-1).astype(jnp.bfloat16)  82.9 us
    gather x1, local copies, waits for them, and re-layouts, local_fn(): dispatch = padded[table].reshape(num_experts, capacity, d_model)  79.3 us
  transfers between devices with their start and end apart: 5, of which 5 were waited for; matrix products, arithmetic and copies ran while one was open for 15% of the time, Pallas kernels for 0%

commit v1 on v0

v1 whole, which is shorter than its diff:
```python
import functools

import jax
import jax.numpy as jnp
from jax import lax
from jax.experimental import pallas as pl
from jax.experimental.pallas import tpu as pltpu
from jax.sharding import PartitionSpec as P

LN_EPS = 1e-5
BF16 = jnp.bfloat16
F32 = jnp.float32
LOG2E = 1.4426950408889634


def dot_t(lhs, rhs_t):
    return lax.dot_general(lhs, rhs_t, (((1,), (1,)), ((), ())), preferred_element_type=F32)


HBM = pltpu.HBM


def norm_rows(value, gain, shift):
    centered = value - jnp.mean(value, axis=-1, keepdims=True)
    variance = jnp.mean(centered * centered, axis=-1, keepdims=True)
    return centered * lax.rsqrt(variance + LN_EPS) * gain + shift


def away(axis, size, distance):
    return lax.rem(lax.axis_index(axis) + distance, size)


def enter(groups):
    barrier = pltpu.get_barrier_semaphore()
    count = 0
    for axis, size in groups:
        for distance in range(1, size):
            pl.semaphore_signal(barrier, inc=1, device_id={axis: away(axis, size, distance)}, device_id_type=pl.DeviceIdType.MESH)
            count += 1
    pl.semaphore_wait(barrier, count)


def exchange(tp_size, weight_ref, chunk, landing_ref, send_sem, recv_sem):
    return [pltpu.make_async_remote_copy(
        src_ref=weight_ref.at[chunk * tp_size + away('tp', tp_size, distance)], dst_ref=landing_ref.at[distance - 1],
        send_sem=send_sem.at[distance - 1], recv_sem=recv_sem.at[distance - 1],
        device_id={'tp': away('tp', tp_size, distance)}, device_id_type=pl.DeviceIdType.MESH)
        for distance in sorted(range(1, tp_size), key=lambda d: (min(d, tp_size - d), d))]


def attention_body(tp_size, chunk, head_dim, block_q, lens_ref, x_ref, gain_ref, shift_ref, w_qkv_ref, b_qkv_ref, w_out_ref, b_out_ref, gain2_ref, shift2_ref, w_move_ref,
                   hidden_ref, normed_ref, moved_ref, qkv_ref, context_ref, send_sem, recv_sem):
    row = pl.program_id(0)
    block = pl.program_id(1)
    seq, width = x_ref.shape
    copies = exchange(tp_size, w_move_ref, chunk, moved_ref, send_sem, recv_sem)

    @pl.when((row == 0) & (block == 0))
    def _():
        enter([('tp', tp_size)])
        for copy in copies:
            copy.start()

    @pl.when(block == 0)
    def _():
        def project(index, carry):
            rows = pl.ds(pl.multiple_of(index * block_q, block_q), block_q)
            normed = norm_rows(x_ref[rows, :].astype(F32), gain_ref[...], shift_ref[...]).astype(BF16)
            qkv_ref[rows, :] = (dot_t(normed, w_qkv_ref[...]) + b_qkv_ref[...]).astype(BF16)
            return carry
        lax.fori_loop(0, seq // block_q, project, 0)

    length = lens_ref[row]
    pair = 2 * head_dim
    key_ok = lax.broadcasted_iota(jnp.int32, (1, seq), 1) < length
    lane_head = lax.broadcasted_iota(jnp.int32, (1, pair), 1) // head_dim
    factor = (head_dim ** -0.5) * LOG2E
    rows = pl.ds(pl.multiple_of(block * block_q, block_q), block_q)

    def heads(index, carry):
        lanes = pl.multiple_of(index * pair, pair)
        query = qkv_ref[rows, pl.ds(lanes, pair)]
        keys = qkv_ref[:, pl.ds(pl.multiple_of(lanes + width, pair), pair)]
        values = qkv_ref[:, pl.ds(pl.multiple_of(lanes + 2 * width, pair), pair)]
        result = None
        for head in range(2):
            scores = dot_t(jnp.where(lane_head == head, query, jnp.zeros_like(query)), keys)
            scores = jnp.where(key_ok, scores, -1e30)
            top = jnp.max(scores, axis=-1, keepdims=True)
            weights = jnp.exp2((scores - top) * factor)
            scale = 1.0 / jnp.sum(weights, axis=-1, keepdims=True)
            part = jnp.dot((weights * scale).astype(BF16), values, preferred_element_type=F32)
            result = part if result is None else jnp.where(lane_head == head, part, result)
        context_ref[:, pl.ds(lanes, pair)] = result.astype(BF16)
        return carry

    lax.fori_loop(0, width // pair, heads, 0)
    projected = jnp.dot(context_ref[...], w_out_ref[...], preferred_element_type=F32)
    hidden = (x_ref[rows, :].astype(F32) + projected + b_out_ref[...]).astype(BF16)
    hidden_ref[...] = hidden
    normed_ref[...] = norm_rows(hidden.astype(F32), gain2_ref[...], shift2_ref[...]).astype(BF16)

    @pl.when((row == pl.num_programs(0) - 1) & (block == pl.num_programs(1) - 1))
    def _():
        for copy in copies:
            copy.wait()


def attention_layer(x, lens, seq, head_dim, norm, w_qkv, b_qkv, w_out, b_out, norm2, w_move, tp_size, chunk, call_id):
    tokens, width = x.shape
    block_q = min(256, seq)
    blocks = seq // block_q
    fixed = lambda shape: pl.BlockSpec(shape, lambda r, q: (0,) * len(shape), pipeline_mode=pl.Buffered(1))
    moved = (tp_size - 1,) + w_move.shape[1:]
    return pl.pallas_call(
        functools.partial(attention_body, tp_size, chunk, head_dim, block_q),
        out_shape=(jax.ShapeDtypeStruct((tokens, width), BF16), jax.ShapeDtypeStruct((tokens, width), BF16), jax.ShapeDtypeStruct(moved, BF16)),
        grid=(tokens // seq, blocks),
        in_specs=[pl.BlockSpec(memory_space=pltpu.SMEM), pl.BlockSpec((seq, width), lambda r, q: (r, 0)), fixed((1, width)), fixed((1, width)),
                  fixed(w_qkv.shape), fixed((1, 3 * width)), fixed(w_out.shape), fixed((1, width)), fixed((1, width)), fixed((1, width)), pl.BlockSpec(memory_space=HBM)],
        out_specs=(pl.BlockSpec((block_q, width), lambda r, q: (r * blocks + q, 0)), pl.BlockSpec((block_q, width), lambda r, q: (r * blocks + q, 0)), pl.BlockSpec(memory_space=HBM)),
        scratch_shapes=[pltpu.VMEM((seq, 3 * width), BF16), pltpu.VMEM((block_q, width), BF16), pltpu.SemaphoreType.DMA((tp_size - 1,)), pltpu.SemaphoreType.DMA((tp_size - 1,))],
        compiler_params=pltpu.CompilerParams(dimension_semantics=('arbitrary', 'arbitrary'), collective_id=call_id, has_side_effects=True, vmem_limit_bytes=52 * 1024 * 1024),
        cost_estimate=pl.CostEstimate(flops=30_000_000_000, transcendentals=0, bytes_accessed=40_000_000),
        name='attention_layer')(lens, x, *norm, w_qkv, b_qkv, w_out, b_out, *norm2, w_move)


def dense_body(tp_size, chunk, parts, x_ref, normed_ref, w_in_ref, b_in_ref, w_out_ref, b_out_ref, w_move_ref, o_ref, moved_ref, send_sem, recv_sem):
    block = pl.program_id(0)
    copies = exchange(tp_size, w_move_ref, chunk, moved_ref, send_sem, recv_sem)

    @pl.when(block == 0)
    def _():
        enter([('tp', tp_size)])
        for copy in copies:
            copy.start()

    size = w_in_ref.shape[0] // parts
    total = x_ref[...].astype(F32) + b_out_ref[...]
    for part in range(parts):
        cols = pl.ds(part * size, size)
        inner = jnp.maximum(dot_t(normed_ref[...], w_in_ref[cols, :]) + b_in_ref[:, cols], 0.0).astype(BF16)
        total += jnp.dot(inner, w_out_ref[cols, :], preferred_element_type=F32)
    o_ref[...] = total.astype(BF16)

    @pl.when(block == pl.num_programs(0) - 1)
    def _():
        for copy in copies:
            copy.wait()


def dense_layer(x, normed, w_in, b_in, w_out, b_out, w_move, tp_size, chunk, call_id):
    tokens, width = x.shape
    block_n = min(256, tokens)
    fixed = lambda shape: pl.BlockSpec(shape, lambda i: (0,) * len(shape), pipeline_mode=pl.Buffered(1))
    moved = (tp_size - 1,) + w_move.shape[1:]
    return pl.pallas_call(
        functools.partial(dense_body, tp_size, chunk, 4),
        out_shape=(jax.ShapeDtypeStruct((tokens, width), BF16), jax.ShapeDtypeStruct(moved, BF16)), grid=(tokens // block_n,),
        in_specs=[pl.BlockSpec((block_n, width), lambda i: (i, 0)), pl.BlockSpec((block_n, width), lambda i: (i, 0)), fixed(w_in.shape), fixed(b_in.shape), fixed(w_out.shape), fixed((1, width)), pl.BlockSpec(memory_space=HBM)],
        out_specs=(pl.BlockSpec((block_n, width), lambda i: (i, 0)), pl.BlockSpec(memory_space=HBM)),
        scratch_shapes=[pltpu.SemaphoreType.DMA((tp_size - 1,)), pltpu.SemaphoreType.DMA((tp_size - 1,))],
        compiler_params=pltpu.CompilerParams(dimension_semantics=('arbitrary',), collective_id=call_id, has_side_effects=True, vmem_limit_bytes=52 * 1024 * 1024),
        cost_estimate=pl.CostEstimate(flops=20_000_000_000, transcendentals=0, bytes_accessed=30_000_000),
        name='dense_layer')(x, normed, w_in, b_in, w_out, b_out, w_move)


def experts_body(tp_size, ep_size, early, dispatch_ref, early_refs, w_in_ref, w_out_ref, b_in_ref, b_out_ref, returned_ref,
                 arrived_ref, late_ref, early_buf, own_buf, out_buf, local_sem, send_sem, recv_sem, back_send, back_recv, move_send, move_recv):
    chunks, _, slots, width = arrived_ref.shape
    me = lax.axis_index('ep')
    mine = lax.axis_index('tp')
    weights = (w_in_ref, w_out_ref)
    units = [(chunk, which) for chunk in range(chunks) for which in range(2)]
    late = units[early:]

    sends = {}
    for chunk in range(chunks):
        for distance in range(1, ep_size):
            peer = away('ep', ep_size, distance)
            sends[chunk, distance] = pltpu.make_async_remote_copy(
                src_ref=dispatch_ref.at[chunk, peer], dst_ref=arrived_ref.at[chunk, me], send_sem=send_sem.at[chunk, distance], recv_sem=recv_sem.at[chunk, distance],
                device_id={'ep': peer}, device_id_type=pl.DeviceIdType.MESH)
    moves = {unit: exchange(tp_size, weights[unit[1]], unit[0], late_ref.at[index], move_send.at[index], move_recv.at[index]) for index, unit in enumerate(late)}
    kept = [pltpu.make_async_copy(dispatch_ref.at[chunk, me], arrived_ref.at[chunk, me], local_sem.at[0, chunk]) for chunk in range(chunks)]
    owns = {unit: pltpu.make_async_copy(weights[unit[1]].at[unit[0] * tp_size + mine], own_buf.at[unit[0], unit[1]], local_sem.at[1 + unit[1], unit[0]]) for unit in units}
    earlies = {unit: pltpu.make_async_copy(early_refs[index], early_buf.at[index], local_sem.at[3, index]) for index, unit in enumerate(units[:early])}

    enter([('tp', tp_size), ('ep', ep_size)])
    for unit in late:
        for copy in moves[unit]:
            copy.start()
    for chunk in range(chunks):
        for distance in range(1, ep_size):
            sends[chunk, distance].start()
        kept[chunk].start()
    for unit in units:
        owns[unit].start()
        if unit in earlies:
            earlies[unit].start()

    def part_ref(unit, part):
        if part == 0:
            return own_buf.at[unit[0], unit[1]]
        index = units.index(unit)
        return early_buf.at[index, part - 1] if index < early else late_ref.at[index - early, part - 1]

    backs = {}
    for chunk in range(chunks):
        slot = chunk % out_buf.shape[0]
        for distance in range(1, ep_size):
            sends[chunk, distance].wait_recv()
        kept[chunk].wait()
        for which in range(2):
            unit = (chunk, which)
            owns[unit].wait()
            if unit in earlies:
                earlies[unit].wait()
            else:
                for copy in moves[unit]:
                    copy.wait_recv()
        before = chunk - out_buf.shape[0]
        if before >= 0:
            for copy in backs[before][:-1]:
                copy.wait_send()
            backs[before][-1].wait()

        def rows(index, carry):
            tokens = arrived_ref[chunk, pl.ds(2 * index, 2)].reshape(2 * slots, width)
            total = jnp.zeros((2 * slots, width), F32)
            for part in range(tp_size):
                inner = jnp.dot(tokens, part_ref((chunk, 0), part)[...], preferred_element_type=F32) + b_in_ref[chunk, pl.ds(part, 1), :]
                total += jnp.dot(jnp.maximum(inner, 0.0).astype(BF16), part_ref((chunk, 1), part)[...], preferred_element_type=F32)
            out_buf[slot, pl.ds(2 * index, 2)] = (total + b_out_ref[pl.ds(chunk, 1), :]).astype(BF16).reshape(2, slots, width)
            return carry

        lax.fori_loop(0, ep_size // 2, rows, 0)
        backs[chunk] = []
        for distance in range(1, ep_size):
            peer = away('ep', ep_size, distance)
            backs[chunk].append(pltpu.make_async_remote_copy(
                src_ref=out_buf.at[slot, peer], dst_ref=returned_ref.at[chunk, me], send_sem=back_send.at[chunk, distance], recv_sem=back_recv.at[chunk, distance],
                device_id={'ep': peer}, device_id_type=pl.DeviceIdType.MESH))
        backs[chunk].append(pltpu.make_async_copy(out_buf.at[slot, me], returned_ref.at[chunk, me], local_sem.at[4, chunk]))
        for copy in backs[chunk]:
            copy.start()

    for chunk in range(chunks):
        for distance in range(1, ep_size):
            sends[chunk, distance].wait_send()
        for copy in backs[chunk][:-1]:
            copy.wait_recv()
            if chunk + out_buf.shape[0] >= chunks:
                copy.wait_send()
        if chunk + out_buf.shape[0] >= chunks:
            backs[chunk][-1].wait()
    for unit in late:
        for copy in moves[unit]:
            copy.wait_send()


def experts(dispatch, early_weights, w_in, w_out, b_in, b_out, tp_size, ep_size, call_id):
    chunks, _, slots, width = dispatch.shape
    hidden = w_in.shape[2]
    early = len(early_weights)
    late = 2 * chunks - early
    hbm = pl.BlockSpec(memory_space=HBM)
    vmem = pl.BlockSpec(memory_space=pltpu.VMEM)

    def body(dispatch_ref, *refs):
        experts_body(tp_size, ep_size, early, dispatch_ref, refs[:early], *refs[early:])

    dma = pltpu.SemaphoreType.DMA
    return pl.pallas_call(
        body, out_shape=jax.ShapeDtypeStruct(dispatch.shape, BF16),
        in_specs=[hbm] * (3 + early) + [vmem, vmem], out_specs=hbm,
        scratch_shapes=[pltpu.VMEM(dispatch.shape, BF16), pltpu.VMEM((late, tp_size - 1, width, hidden), BF16), pltpu.VMEM((early, tp_size - 1, width, hidden), BF16),
                        pltpu.VMEM((chunks, 2, width, hidden), BF16), pltpu.VMEM((2, ep_size, slots, width), BF16),
                        dma((5, max(chunks, early))), dma((chunks, ep_size)), dma((chunks, ep_size)), dma((chunks, ep_size)), dma((chunks, ep_size)),
                        dma((late, tp_size - 1)), dma((late, tp_size - 1))],
        compiler_params=pltpu.CompilerParams(collective_id=call_id, has_side_effects=True, vmem_limit_bytes=62 * 1024 * 1024),
        cost_estimate=pl.CostEstimate(flops=4 * chunks * ep_size * slots * width * hidden * tp_size, transcendentals=0, bytes_accessed=60_000_000),
        name='experts')(dispatch, *early_weights, w_in, w_out, b_in, b_out)


def combine_body(block_t, token_ref, gate_at_ref, gates_ref, slots_ref, o_ref, acc_ref, wide_ref):
    block = pl.program_id(0)
    slots, width = wide_ref.shape
    tokens = o_ref.shape[0]

    @pl.when(block == 0)
    def _():
        def clear(index, carry):
            rows = pl.ds(pl.multiple_of(index * block_t, block_t), block_t)
            acc_ref[rows, :] = jnp.zeros((block_t, width), F32)
            return carry
        lax.fori_loop(0, tokens // block_t, clear, 0)
        acc_ref[pl.ds(tokens, 8), :] = jnp.zeros((8, width), F32)

    wide_ref[...] = slots_ref[...].astype(F32)
    base = block * slots

    def step(index, carry):
        first = index * 8
        places = [token_ref[base + first + u] for u in range(8)]
        gates = [gates_ref[gate_at_ref[base + first + u]] for u in range(8)]
        old = [acc_ref[pl.ds(places[u], 1), :] for u in range(8)]
        new = [wide_ref[pl.ds(first + u, 1), :] for u in range(8)]
        for u in range(8):
            acc_ref[pl.ds(places[u], 1), :] = old[u] + gates[u] * new[u]
        return carry

    lax.fori_loop(0, slots // 8, step, 0)

    @pl.when(block == pl.num_programs(0) - 1)
    def _():
        def write(index, carry):
            rows = pl.ds(pl.multiple_of(index * block_t, block_t), block_t)
            o_ref[rows, :] = acc_ref[rows, :].astype(BF16)
            return carry
        lax.fori_loop(0, tokens // block_t, write, 0)


def combine(token_of, gate_at, gates, outputs, tokens):
    blocks, slots, width = outputs.shape
    block_t = min(256, tokens)
    grid_spec = pltpu.PrefetchScalarGridSpec(
        num_scalar_prefetch=3, grid=(blocks,),
        in_specs=[pl.BlockSpec((None, slots, width), lambda b, *_: (b, 0, 0))],
        out_specs=pl.BlockSpec((tokens, width), lambda b, *_: (0, 0)),
        scratch_shapes=[pltpu.VMEM((tokens + 8, width), F32), pltpu.VMEM((slots, width), F32)])
    return pl.pallas_call(
        functools.partial(combine_body, block_t),
        out_shape=jax.ShapeDtypeStruct((tokens, width), BF16), grid_spec=grid_spec,
        compiler_params=pltpu.CompilerParams(dimension_semantics=('arbitrary',), vmem_limit_bytes=56 * 1024 * 1024),
        cost_estimate=pl.CostEstimate(flops=30_000_000_000, transcendentals=0, bytes_accessed=2 * tokens * width + 2 * blocks * slots * width),
        name='combine')(token_of, gate_at, gates, outputs)


def route(key_ok, expert_idx, num_experts, capacity):
    tokens = key_ok.size
    valid = key_ok.reshape(tokens)
    first = expert_idx[..., 0].reshape(tokens)
    second = expert_idx[..., 1].reshape(tokens)
    expert_ids = jnp.arange(num_experts, dtype=jnp.int32)
    hot_first = ((first[:, None] == expert_ids) & valid[:, None]).astype(jnp.int32)
    hot_second = ((second[:, None] == expert_ids) & valid[:, None]).astype(jnp.int32)
    rank_first = jnp.cumsum(hot_first, axis=0) - 1
    rank_second = jnp.cumsum(hot_second, axis=0) - 1 + jnp.sum(hot_first, axis=0)
    slot_first = jnp.sum(rank_first * hot_first, axis=1)
    slot_second = jnp.sum(rank_second * hot_second, axis=1)
    dump = num_experts * capacity
    dest_first = jnp.where(valid & (slot_first < capacity), first * capacity + slot_first, dump)
    dest_second = jnp.where(valid & (slot_second < capacity), second * capacity + slot_second, dump)
    choice = jnp.full((dump + 1,), 2 * tokens, jnp.int32)
    ids = jnp.arange(tokens, dtype=jnp.int32)
    choice = choice.at[dest_first].set(ids).at[dest_second].set(ids + tokens)
    return choice[:dump].reshape(num_experts, capacity)


def solution(mesh):
    tp_size = mesh.shape['tp']
    ep_size = mesh.shape['ep']

    def gather_tp(value, axis=0, tiled=False):
        return lax.all_gather(value, 'tp', axis=axis, tiled=tiled)

    def local_fn(x, src_len, expert_idx, ln_gain, ln_bias, w_query, b_query, w_key, w_value, b_value, w_attn_out, b_attn_out, w_fc1, b_fc1, w_fc2, b_fc2, w_router, w_exp_in, b_exp_in, w_exp_out, b_exp_out):
        rows, seq, width = x.shape
        tokens = rows * seq
        num_experts = w_router.shape[1]
        capacity = 2 * (-(-tokens // num_experts))
        local_experts = w_exp_in.shape[0]
        own_experts = local_experts // tp_size
        _, _, local_heads, head_dim = w_query.shape
        heads = local_heads * tp_size
        head_cols = local_heads * head_dim
        hidden_cols = w_fc1.shape[1]
        tp_index = lax.axis_index('tp')
        ep_index = lax.axis_index('ep')
        own_rows = rows // tp_size
        own_tokens = own_rows * seq
        x_own = lax.dynamic_slice_in_dim(x, tp_index * own_rows, own_rows, 0).reshape(own_tokens, width)
        len_own = lax.dynamic_slice_in_dim(src_len, tp_index * own_rows, own_rows, 0)

        def pack_attention(j):
            columns = [w[j].reshape(width, head_cols).T for w in (w_query, w_key, w_value)]
            return jnp.concatenate(columns + [w_attn_out[j].reshape(head_cols, width)], axis=0)

        def unpack_attention(gathered):
            by_kind = gathered.reshape(tp_size, 4, head_cols, width).transpose(1, 0, 2, 3)
            return by_kind[:3].reshape(3 * heads * head_dim, width), by_kind[3].reshape(heads * head_dim, width)

        small = jnp.concatenate([b_query.reshape(-1), b_value.reshape(-1), b_fc1.reshape(-1), b_exp_in.reshape(-1)])
        small = gather_tp(small)
        attn_bias_size = 2 * head_cols
        b_query_all = small[:, :attn_bias_size].reshape(tp_size, 2, head_cols).transpose(1, 0, 2).reshape(2, -1)
        b_value_all = small[:, attn_bias_size:2 * attn_bias_size].reshape(tp_size, 2, head_cols).transpose(1, 0, 2).reshape(2, -1)
        b_fc1_all = small[:, 2 * attn_bias_size:2 * attn_bias_size + hidden_cols]
        b_exp_in_all = small[:, 2 * attn_bias_size + hidden_cols:].reshape(tp_size, local_experts, -1)
        b_qkv = jnp.concatenate([b_query_all, jnp.zeros_like(b_query_all), b_value_all], axis=1)

        first_pack = gather_tp(pack_attention(0))

        cut = hidden_cols // ep_size

        def own_slice(value):
            size = value.shape[0] // ep_size
            return lax.dynamic_slice_in_dim(value, ep_index * size, size, 0)

        later = jnp.concatenate([own_slice(w_fc1.T), own_slice(w_fc2), own_slice(pack_attention(1))], axis=0)
        later, first_pack = lax.optimization_barrier((later, first_pack))
        later = gather_tp(later)
        fc1_all = lax.all_gather(later[:, :cut], 'ep').reshape(-1, width)
        fc2_all = lax.all_gather(later[:, cut:2 * cut], 'ep').reshape(-1, width)
        second_pack = lax.all_gather(later[:, 2 * cut:], 'ep').transpose(1, 0, 2, 3).reshape(tp_size, -1, width)
        b_fc1_all = b_fc1_all.reshape(tp_size, ep_size, cut).transpose(1, 0, 2).reshape(-1)

        key_ok = jnp.arange(seq)[None, :] < src_len[:, None]
        choice_all = route(key_ok, expert_idx, num_experts, capacity)
        choice = choice_all.reshape(ep_size, own_experts, tp_size, capacity)
        choice = lax.dynamic_index_in_dim(choice, tp_index, 2, keepdims=False)
        source = jnp.where(choice < tokens, choice, choice - tokens)
        dispatch_at = jnp.where(choice == 2 * tokens, 0, source)

        def norm(i):
            return ln_gain[i].reshape(1, width), ln_bias[i].reshape(1, width)

        def row(value):
            return value.reshape(1, -1)

        w_qkv, w_out = unpack_attention(first_pack)
        hidden, normed, moved_0 = attention_layer(x_own, len_own, seq, head_dim, norm(0), w_qkv, row(b_qkv[0]), w_out, row(b_attn_out[0]), norm(1), w_exp_in, tp_size, 0, 0)
        hidden, moved_1 = dense_layer(hidden, normed, fc1_all, row(b_fc1_all), fc2_all, row(b_fc2), w_exp_out, tp_size, 0, 1)
        w_qkv, w_out = unpack_attention(second_pack)
        hidden, normed, moved_2 = attention_layer(hidden, len_own, seq, head_dim, norm(2), w_qkv, row(b_qkv[1]), w_out, row(b_attn_out[1]), norm(3), w_exp_in, tp_size, 1, 2)
        normed_all = gather_tp(normed, tiled=True)

        logits = jnp.dot(normed_all, w_router.astype(BF16), preferred_element_type=F32)
        expert_ids = jnp.arange(num_experts, dtype=jnp.int32)
        flat_idx = expert_idx.reshape(tokens, 2)
        picked = [jnp.sum(jnp.where(flat_idx[:, k:k + 1] == expert_ids, logits, 0.0), axis=1) for k in range(2)]
        gates = jnp.concatenate([jax.nn.sigmoid(picked[0] - picked[1]), jax.nn.sigmoid(picked[1] - picked[0]), jnp.zeros((128,), F32)])

        b_in_own = lax.dynamic_index_in_dim(b_exp_in_all.reshape(tp_size, own_experts, tp_size, -1), tp_index, 2, keepdims=False)
        part_order = lax.rem(tp_index - jnp.arange(tp_size) + tp_size, tp_size)
        b_in_own = b_in_own[part_order].transpose(1, 0, 2)
        b_out_own = lax.dynamic_index_in_dim(b_exp_out.reshape(own_experts, tp_size, width), tp_index, 1, keepdims=False)
        dispatch = normed_all[dispatch_at.transpose(1, 0, 2).reshape(-1)].reshape(own_experts, ep_size, capacity, width)
        outputs = experts(dispatch, [moved_0, moved_1, moved_2], w_exp_in, w_exp_out, b_in_own, b_out_own, tp_size, ep_size, 3)
        outputs = outputs.reshape(own_experts * ep_size, capacity, width)
        choice = choice.transpose(1, 0, 2).reshape(-1)
        token_of = jnp.where(choice == 2 * tokens, tokens, source.transpose(1, 0, 2).reshape(-1))
        partial = combine(token_of, choice, gates, outputs, tokens)
        summed = lax.psum_scatter(partial, 'tp', scatter_dimension=0, tiled=True)
        result = (hidden.astype(F32) + summed.astype(F32)).astype(BF16)
        return gather_tp(result, tiled=True).reshape(rows, seq, width)

    in_specs = (P(('dp', 'ep'), None, None), P(('dp', 'ep')), P(('dp', 'ep'), None, None), P(), P(), P(None, None, 'tp', None), P(None, 'tp', None), P(None, None, 'tp', None), P(None, None, 'tp', None), P(None, 'tp', None), P(None, 'tp', None, None), P(), P(None, 'tp'), P('tp'), P('tp', None), P(), P(), P('ep', None, 'tp'), P('ep', 'tp'), P('ep', 'tp', None), P('ep', None))
    return jax.shard_map(local_fn, mesh=mesh, in_specs=in_specs, out_specs=P(('dp', 'ep'), None, None), check_vma=False)
```

time: 2330 us -> 1100 us (0.47)
  waiting for transfers between devices: 1010 us -> 332 us
  Pallas kernels: 0 us -> 566 us
  local copies, waits for them, and re-layouts: 541 us -> 131 us
  matrix products: 303 us -> 9.27 us
  blocking collectives: 284 us -> 9.35 us
  other arithmetic: 158 us -> 28.8 us
    psum x4 -> x0, waiting for transfers between devices: 1000 us -> none  [the longest x1 423 us: local_fn(): summed = lax.psum(partial, 'tp')]
    pallas_call x0 -> x5, Pallas kernels: none -> 566 us  [the longest x1 293 us: experts(): pl.pallas_call(body, out_shape=jax.ShapeDtypeStruct(dispatch.shape, BF16)...]
    gather x5 -> x3, local copies, waits for them, and re-layouts: 430 us -> 26.7 us  [the longest x1 25.5 us: local_fn(): normed_all[dispatch_at.transpose(1, 0, 2).reshape(-1)]]
    all_to_all x1 -> x0, blocking collectives: 284 us -> none  [local_fn(): lax.all_to_all(dispatch, 'ep', 0, 0, tiled=True)]
    all_gather x0 -> x7, waiting for transfers between devices: none -> 221 us  [the longest x4 221 us: gather_tp(): return lax.all_gather(value, 'tp', axis=axis, tiled=tiled)]
    dot_general x13 -> x1, matrix products: 220 us -> 9.27 us  [local_fn(): jnp.dot(normed_all, w_router.astype(BF16), preferred_element_type=F32)]
    reduce_scatter x0 -> x1, waiting for transfers between devices: none -> 110 us  [local_fn(): summed = lax.psum_scatter(partial, 'tp', scatter_dimension=0, tiled=True)]
    reduce_sum x10 -> x2, other arithmetic: 94.9 us -> 8.66 us  [the longest x1 4.54 us: route(): jnp.sum(hot_first, axis=0)]
  transfers between devices with their start and end apart: 5 -> 8, of which waited for: 5 -> 5; matrix products, arithmetic and copies ran while one was open for 15% -> 10% of each run, Pallas kernels for 0% -> 8%
where the time goes in v1:
time: 1100 us; the launch traced here: 1090 us
  Pallas kernels  566 us (51%)
  waiting for transfers between devices  332 us (30%)
  local copies, waits for them, and re-layouts  131 us (12%)
  other arithmetic  28.8 us (3%)
  between operations  14.6 us (1%)
    pallas_call x1, Pallas kernels, experts(): pl.pallas_call(body, out_shape=jax.ShapeDtypeStruct(dispatch.shape, BF16)...  293 us
    all_gather x4, waiting for transfers between devices, gather_tp(): return lax.all_gather(value, 'tp', axis=axis, tiled=tiled)  221 us
    pallas_call x2, Pallas kernels, attention_layer(): pl.pallas_call(functools.partial(attention_body, tp_size, chunk, head_dim...  178 us
    reduce_scatter x1, waiting for transfers between devices, local_fn(): summed = lax.psum_scatter(partial, 'tp', scatter_dimension=0, tiled=True)  110 us
    scatter x2, local copies, waits for them, and re-layouts, route(): choice = choice.at[dest_first].set(ids).at[dest_second].set(ids + tokens)  60.9 us
    pallas_call x1, Pallas kernels, dense_layer(): pl.pallas_call(functools.partial(dense_body, tp_size, chunk, 4), out_shap...  55.1 us
    pallas_call x1, Pallas kernels, combine(): pl.pallas_call(functools.partial(combine_body, block_t), out_shape=jax.Sh...  39.4 us
    gather x1, local copies, waits for them, and re-layouts, local_fn(): normed_all[dispatch_at.transpose(1, 0, 2).reshape(-1)]  25.5 us
  transfers between devices with their start and end apart: 8, of which 5 were waited for; matrix products, arithmetic and copies ran while one was open for 10% of the time, Pallas kernels for 8%

profile of v1, /device:TPU:97, one launch (start us, length us, event | category | flops | bytes accessed | tf_op | source)
XLA Modules:
  0.0 1091.7 jit_solution(1304356706863210234)
XLA Ops:
  6.6 1.2 fusion.32
  7.7 1.1 fusion.31
  8.8 1.1 fusion.30
  9.9 1.1 fusion.29
  11.0 1.1 pad_maximum_fusion
  12.6 1.2 fusion.20
  13.8 0.8 pad_maximum_fusion.1
  14.6 51.3 %all-gather.19.cloned.1.call-done = bf16[3072,768]{1,0:T(8,128)(2,1)} async-done(((bf16[768,768]{1,0:T(8,128)(2,1)}), bf16[3072,768]{1,0:T(8,128)(2,1)}) %all-gather.19.cloned.1.call-update) | async-done | bytes 4718608 | tf_op jit(solution)/shard_map/all_gather | solution.py:366
  66.1 27.3 %all-gather.21.cloned.1.call-done = bf16[1152,768]{1,0:T(8,128)(2,1)} async-done(((bf16[288,768]{1,0:T(8,128)(2,1)}), bf16[1152,768]{1,0:T(8,128)(2,1)}) %all-gather.21.cloned.1.call-update) | async-done | bytes 1769488 | tf_op jit(solution)/shard_map/all_gather | solution.py:366
  93.4 2.7 fusion.28
  96.2 0.6 all-gather.23.cloned.1.call-update
  96.9 0.6 all-gather.25.cloned.1.call-update
  97.8 9.4 all-gather.6
  107.9 3.9 constant_dynamic-slice_fusion.5
  112.3 2.0 copy.81
  114.3 88.9 %attention_layer.2 = (bf16[2048,768]{1,0:T(8,128)(2,1)}, bf16[2048,768]{1,0:T(8,128)(2,1)}, bf16[3,768,768]{2,1,0:T(8,128)(2,1)}) custom-call(s32[2]{0:T(128)S(1)} %dynamic_slice.27.lens_ref, bf16[2048,768]{1,0:T(8,128)(2,1)} %bitcast.136, f32[1,768]{1,0:T(1,128)S(1)} %get-tuple-element.69.gain_ref, f32[1,768]{1,0:T(1,128)S(1)} %get-tuple-element.56.shift_ref, ...), custom_call_target="tpu_custom_call" | custom-call | flops 30000001024 | bytes 40000000 | tf_op jit(solution)/shard_map/attention_layer/pallas_call | solution.py:115
  203.2 2.7 copy.87
  205.9 0.2 slice.173
  206.2 2.0 copy.88
  208.3 55.1 %dense_layer.1 = (bf16[2048,768]{1,0:T(8,128)(2,1)}, bf16[3,768,768]{2,1,0:T(8,128)(2,1)}) custom-call(bf16[2048,768]{1,0:T(8,128)(2,1)} %get-tuple-element.16.x_ref, bf16[2048,768]{1,0:T(8,128)(2,1)} %get-tuple-element.17.normed_ref, bf16[3072,768]{1,0:T(8,128)(2,1)} %bitcast.176, f32[1,3072]{1,0:T(1,128)S(1)} %reshape_reshape.12.b_in_ref, ...), custom_call_target="tpu_custom_call" | custom-call | flops 20000000000 | bytes 30000000 | tf_op jit(solution)/shard_map/dense_layer/pallas_call | solution.py:157
  263.4 89.3 %attention_layer.3 = (bf16[2048,768]{1,0:T(8,128)(2,1)}, bf16[2048,768]{1,0:T(8,128)(2,1)}, bf16[3,768,768]{2,1,0:T(8,128)(2,1)}) custom-call(s32[2]{0:T(128)S(1)} %dynamic_slice.27.lens_ref, bf16[2048,768]{1,0:T(8,128)(2,1)} %get-tuple-element.19.x_ref, f32[1,768]{1,0:T(1,128)S(1)} %get-tuple-element.68.gain_ref, f32[1,768]{1,0:T(1,128)S(1)} %get-tuple-element.57.shift_ref, ...), custom_call_target="tpu_custom_call" | custom-call | flops 30000001024 | bytes 40000000 | tf_op jit(solution)/shard_map/attention_layer/pallas_call | solution.py:115
  353.6 2.2 fusion.2
  355.9 2.0 copy-done.3
  358.0 2.7 add_add_fusion
  360.7 4.4 copy.93
  365.3 2.2 fusion.4
  367.6 2.0 copy-done.2
  369.6 2.7 add_add_fusion.1
  372.3 2.4 copy.91
  374.8 4.5 convert_reduce_fusion
  379.4 4.1 fusion.1
  383.7 30.5 %scatter_custom_fusion = s32[16385]{0:T(1024)S(1)} fusion(s32[8192]{0:T(1024)S(1)} %bitcast.169, s32[8192]{0:T(1024)S(1)} %iota.27, s32[]{:T(128)} %constant.27.clone.1), kind=kCustom, calls=%fused_computation.54 | custom fusion | bytes 65544 | tf_op jit(solution)/shard_map/scatter | solution.py:357
  414.2 30.5 %scatter_fusion = s32[16385]{0:T(1024)S(1)} fusion(s32[16385]{0:T(1024)S(1)} %scatter_custom_fusion, s32[8192]{0:T(1024)S(1)} %bitcast.156, s32[8192]{0:T(1024)S(1)} %iota_add_fusion), kind=kCustom, calls=%fused_computation.3 | custom fusion | bytes 131072 | tf_op jit(solution)/shard_map/scatter | solution.py:357
  444.7 0.6 copy.123
  445.6 0.6 gather_fusion.1
  446.2 0.6 copy.121
  446.9 0.6 copy.124
  447.5 0.6 bitcast_select_fusion.2.token_ref
  448.2 25.6 %all-gather.15.cloned.1.call-done = bf16[8192,768]{1,0:T(8,128)(2,1)} async-done(((bf16[2048,768]{1,0:T(8,128)(2,1)}), bf16[8192,768]{1,0:T(8,128)(2,1)}) %all-gather.15.cloned.1.call-update) | async-done | bytes 12582928 | tf_op jit(solution)/shard_map/all_gather | solution.py:366
  473.8 9.3 select_reduce_fusion.1
  483.1 0.6 pad_maximum_fusion.2.gates_ref
  483.8 25.5 %gather_fusion = bf16[4096,768]{1,0:T(8,128)(2,1)} fusion(bf16[8192,768]{1,0:T(8,128)(2,1)} %all-gather.15.cloned.1.call-done, s32[4096]{0:T(1024)S(1)} %broadcast_clamp_fusion), kind=kCustom, calls=%fused_computation | custom fusion | bytes 12599296 | tf_op jit(solution)/shard_map/gather | solution.py:449
  509.3 292.9 %experts.1 = bf16[4,8,128,768]{3,2,1,0:T(8,128)(2,1)} custom-call(bf16[4,8,128,768]{3,2,1,0:T(8,128)(2,1)} %bitcast.130, bf16[3,768,768]{2,1,0:T(8,128)(2,1)} %get-tuple-element.22.refs_0_, bf16[3,768,768]{2,1,0:T(8,128)(2,1)} %get-tuple-element.23.refs_1_, bf16[3,768,768]{2,1,0:T(8,128)(2,1)} %get-tuple-element.24.refs_2_, bf16[16,768,768]{2,1,0:T(8,128)(2,1)} %refs_3_.1, ...), custom_call_target="tpu_custom_call" | custom-call | flops 38654705664 | bytes 60000000 | tf_op jit(solution)/shard_map/experts/pallas_call | solution.py:274
  802.2 39.4 %combine.1 = bf16[8192,768]{1,0:T(8,128)(2,1)} custom-call(s32[4096]{0:T(1024)} %bitcast_select_fusion.2.token_ref, s32[4096]{0:T(1024)} %bitcast.174, f32[16512]{0:T(1024)} %pad_maximum_fusion.2.gates_ref, bf16[32,128,768]{2,1,0:T(8,128)(2,1)} %bitcast.178), custom_call_target="tpu_custom_call" | custom-call | flops 30000001024 | bytes 18874368 | tf_op jit(solution)/shard_map/combine/pallas_call | solution.py:332
  841.7 110.4 %reduce-scatter.2.cloned.1.call-done = bf16[2048,768]{1,0:T(8,128)(2,1)} async-done(((bf16[8192,768]{1,0:T(8,128)(2,1)}), bf16[2048,768]{1,0:T(8,128)(2,1)}) %reduce-scatter.2.cloned.1.call-update) | async-done | bytes 3145744 | tf_op jit(solution)/shard_map/reduce_scatter | solution.py:455
  952.1 5.3 add_convert_fusion
  957.4 116.4 %all-gather.17.cloned.1.call-done = bf16[8192,768]{1,0:T(8,128)(2,1)} async-done(((bf16[2048,768]{1,0:T(8,128)(2,1)}), bf16[8192,768]{1,0:T(8,128)(2,1)}) %all-gather.17.cloned.1.call-update) | async-done | bytes 12582928 | tf_op jit(solution)/shard_map/all_gather | solution.py:366
  1073.8 10.5 copy.127
  (120 shorter events, 4.3 us)
Async XLA Ops:
  6.5 5.7 copy-start
  6.6 59.4 %all-gather.19.cloned.1.call-start = ((), (), s32[]{:S(2)}) async-start(), calls=%async_computation.4 | async-start | bytes 5898240 | tf_op jit(solution)/shard_map/all_gather | solution.py:366
  12.2 81.2 %all-gather.21.cloned.1.call-start = ((), (), s32[]{:S(2)}) async-start(), calls=%async_computation.5 | async-start | bytes 2211840 | tf_op jit(solution)/shard_map/all_gather | solution.py:366
  12.5 85.0 %copy-start.7 = (f32[16,768]{1,0:T(8,128)S(1)}, f32[16,768]{1,0:T(8,128)}, u32[]{:S(2)}) copy-start(f32[16,768]{1,0:T(8,128)} %param.39) | copy-start | bytes 147460
  12.6 85.0 %copy-start.14 = (f32[2,3,64]{2,0,1:T(2,128)S(1)}, f32[2,3,64]{2,0,1:T(2,128)}, u32[]{:S(2)}) copy-start(f32[2,3,64]{2,0,1:T(2,128)} %param.30) | copy-start | bytes 4612
  12.6 85.1 %copy-start.15 = (f32[2,3,64]{2,0,1:T(2,128)S(1)}, f32[2,3,64]{2,0,1:T(2,128)}, u32[]{:S(2)}) copy-start(f32[2,3,64]{2,0,1:T(2,128)} %param.27) | copy-start | bytes 4612
  12.6 85.1 %copy-start.12 = (f32[768]{0:T(1024)S(1)}, f32[768]{0:T(1024)}, u32[]{:S(2)}) copy-start(f32[768]{0:T(1024)} %param.34) | copy-start | bytes 9220
  13.8 94.0 %copy-start.13 = (f32[768]{0:T(1024)S(1)}, f32[768]{0:T(1024)}, u32[]{:S(2)}) copy-start(f32[768]{0:T(1024)} %param.36) | copy-start | bytes 9220
  13.8 94.0 %copy-start.16 = (s32[8]{0:T(128)S(1)}, s32[8]{0:T(128)}, u32[]{:S(2)}) copy-start(s32[8]{0:T(128)} %param.22) | copy-start | bytes 100
  66.0 137.2 %all-gather.27.cloned.1.call-start = ((), (), s32[]{:S(2)}) async-start(), calls=%async_computation.8 | async-start | bytes 5308416 | tf_op jit(solution)/shard_map/all_gather | solution.py:416
  96.1 112.2 %all-gather.23.cloned.1.call-start = ((), (), s32[]{:S(2)}) async-start(), calls=%async_computation.6 | async-start | bytes 5308416 | tf_op jit(solution)/shard_map/all_gather | solution.py:414
  96.8 15.1 %copy-start.11 = (f32[2,768]{1,0:T(2,128)S(1)}, f32[2,768]{1,0:T(2,128)}, u32[]{:S(2)}) copy-start(f32[2,768]{1,0:T(2,128)} %param.32) | copy-start | bytes 18436
  96.8 15.1 %copy-start.9 = (f32[4,768]{1,0:T(4,128)S(1)}, f32[4,768]{1,0:T(4,128)}, u32[]{:S(2)}) copy-start(f32[4,768]{1,0:T(4,128)} %param.25) | copy-start | bytes 36868
  96.8 15.1 %copy-start.10 = (f32[4,768]{1,0:T(4,128)S(1)}, f32[4,768]{1,0:T(4,128)}, u32[]{:S(2)}) copy-start(f32[4,768]{1,0:T(4,128)} %param.24) | copy-start | bytes 36868
  96.8 111.5 %all-gather.25.cloned.1.call-start = ((), (), s32[]{:S(2)}) async-start(), calls=%async_computation.7 | async-start | bytes 5308416 | tf_op jit(solution)/shard_map/all_gather | solution.py:415
  97.4 376.4 %all-gather.15.cloned.1.call-start = ((), (), s32[]{:S(2)}) async-start(), calls=%async_computation.1 | async-start | bytes 15728640 | tf_op jit(solution)/shard_map/all_gather | solution.py:366
  107.8 4.1 copy-start.5
  263.4 89.7 %copy-start.6 = (s32[8,1024,2]{1,2,0:T(2,128)S(1)}, s32[8,1024,2]{1,2,0:T(2,128)}, u32[]{:S(2)}) copy-start(s32[8,1024,2]{1,2,0:T(2,128)} %param.23) | copy-start | bytes 196612
  352.8 599.3 %reduce-scatter.2.cloned.1.call-start = ((), (), s32[]{:S(2)}) async-start(), calls=%async_computation.2 | async-start | bytes 15728640 | tf_op jit(solution)/shard_map/reduce_scatter | solution.py:455
  355.9 2.0 copy-start.3
  367.5 2.0 copy-start.2
  374.8 4.6 copy-start.4
  414.2 32.7 %copy-start.8 = (f32[16,768]{1,0:T(8,128)S(1)}, f32[16,768]{1,0:T(8,128)}, u32[]{:S(2)}) copy-start(f32[16,768]{1,0:T(8,128)} %param.41) | copy-start | bytes 147460
  414.2 59.6 %copy-start.17 = (f32[768,128]{1,0:T(8,128)S(1)}, f32[768,128]{1,0:T(8,128)}, u32[]{:S(2)}) copy-start(f32[768,128]{1,0:T(8,128)} %param.37) | copy-start | bytes 1179652
  841.6 232.2 %all-gather.17.cloned.1.call-start = ((), (), s32[]{:S(2)}) async-start(), calls=%async_computation.3 | async-start | bytes 15728640 | tf_op jit(solution)/shard_map/all_gather | solution.py:366
  1073.8 10.6 copy-start.1
Sparse Core Ops, SparseCore 0:
  12.3 53.6 all-gather.18
  67.5 25.7 all-gather.20
  96.2 31.8 all-gather.26
  129.6 31.4 all-gather.22
  162.5 31.5 all-gather.24
  352.9 120.8 all-gather.14
  841.8 110.2 reduce-scatter.1
  957.6 116.2 all-gather.16

commit v2 on v1

--- a/solution.py
+++ b/solution.py
@@ -40,20 +40,54 @@
     pl.semaphore_wait(barrier, count)
 
 
-def exchange(tp_size, weight_ref, chunk, landing_ref, send_sem, recv_sem):
+def exchange(tp_size, weights, piece, landing_ref, send_sem, recv_sem):
+    chunk, which, start, rows = piece
     return [pltpu.make_async_remote_copy(
-        src_ref=weight_ref.at[chunk * tp_size + away('tp', tp_size, distance)], dst_ref=landing_ref.at[distance - 1],
+        src_ref=weights[which].at[chunk * tp_size + away('tp', tp_size, distance), pl.ds(start, rows)], dst_ref=landing_ref.at[distance - 1],
         send_sem=send_sem.at[distance - 1], recv_sem=recv_sem.at[distance - 1],
         device_id={'tp': away('tp', tp_size, distance)}, device_id_type=pl.DeviceIdType.MESH)
         for distance in sorted(range(1, tp_size), key=lambda d: (min(d, tp_size - d), d))]
 
 
-def attention_body(tp_size, chunk, head_dim, block_q, lens_ref, x_ref, gain_ref, shift_ref, w_qkv_ref, b_qkv_ref, w_out_ref, b_out_ref, gain2_ref, shift2_ref, w_move_ref,
-                   hidden_ref, normed_ref, moved_ref, qkv_ref, context_ref, send_sem, recv_sem):
+def exchange_all(tp_size, weights, pieces, landing_refs, send_sem, recv_sem):
+    copies = []
+    for index, piece in enumerate(pieces):
+        copies += exchange(tp_size, weights, piece, landing_refs[index], send_sem.at[index], recv_sem.at[index])
+    return copies
+
+
+def landings(tp_size, weight, pieces):
+    return [jax.ShapeDtypeStruct((tp_size - 1, rows, weight.shape[2]), BF16) for _, _, _, rows in pieces]
+
+
+def move_body(tp_size, pieces, w_in_ref, w_out_ref, after_ref, *rest):
+    copies = exchange_all(tp_size, (w_in_ref, w_out_ref), pieces, rest[:len(pieces)], *rest[len(pieces):])
+    enter([('tp', tp_size)])
+    for copy in copies:
+        copy.start()
+    for copy in copies:
+        copy.wait()
+
+
+def move(w_in, w_out, after, tp_size, pieces, call_id):
+    hbm = pl.BlockSpec(memory_space=HBM)
+    dma = pltpu.SemaphoreType.DMA((len(pieces), tp_size - 1))
+    return pl.pallas_call(
+        functools.partial(move_body, tp_size, pieces), out_shape=landings(tp_size, w_in, pieces),
+        in_specs=[hbm, hbm, hbm], out_specs=[hbm for _ in pieces], scratch_shapes=[dma, dma],
+        compiler_params=pltpu.CompilerParams(collective_id=call_id, has_side_effects=True, vmem_limit_bytes=56 * 1024 * 1024),
+        cost_estimate=pl.CostEstimate(flops=20_000_000_000, transcendentals=0, bytes_accessed=10_000_000),
+        name='move')(w_in, w_out, after)
+
+
+def attention_body(tp_size, pieces, head_dim, block_q, lens_ref, x_ref, gain_ref, shift_ref, w_qkv_ref, b_qkv_ref, w_out_ref, b_out_ref, gain2_ref, shift2_ref, w_in_ref, w_exp_out_ref, after_ref,
+                   hidden_ref, normed_ref, *rest):
     row = pl.program_id(0)
     block = pl.program_id(1)
     seq, width = x_ref.shape
-    copies = exchange(tp_size, w_move_ref, chunk, moved_ref, send_sem, recv_sem)
+    moved_refs = rest[:len(pieces)]
+    qkv_ref, context_ref, send_sem, recv_sem = rest[len(pieces):]
+    copies = exchange_all(tp_size, (w_in_ref, w_exp_out_ref), pieces, moved_refs, send_sem, recv_sem)
 
     @pl.when((row == 0) & (block == 0))
     def _():
@@ -106,28 +140,29 @@
             copy.wait()
 
 
-def attention_layer(x, lens, seq, head_dim, norm, w_qkv, b_qkv, w_out, b_out, norm2, w_move, tp_size, chunk, call_id):
+def attention_layer(x, lens, seq, head_dim, norm, w_qkv, b_qkv, w_out, b_out, norm2, w_exp_in, w_exp_out, after, tp_size, pieces, call_id):
     tokens, width = x.shape
     block_q = min(256, seq)
     blocks = seq // block_q
     fixed = lambda shape: pl.BlockSpec(shape, lambda r, q: (0,) * len(shape), pipeline_mode=pl.Buffered(1))
-    moved = (tp_size - 1,) + w_move.shape[1:]
+    moved = landings(tp_size, w_exp_in, pieces)
+    hbm = pl.BlockSpec(memory_space=HBM)
     return pl.pallas_call(
-        functools.partial(attention_body, tp_size, chunk, head_dim, block_q),
-        out_shape=(jax.ShapeDtypeStruct((tokens, width), BF16), jax.ShapeDtypeStruct((tokens, width), BF16), jax.ShapeDtypeStruct(moved, BF16)),
+        functools.partial(attention_body, tp_size, pieces, head_dim, block_q),
+        out_shape=(jax.ShapeDtypeStruct((tokens, width), BF16), jax.ShapeDtypeStruct((tokens, width), BF16), *moved),
         grid=(tokens // seq, blocks),
         in_specs=[pl.BlockSpec(memory_space=pltpu.SMEM), pl.BlockSpec((seq, width), lambda r, q: (r, 0)), fixed((1, width)), fixed((1, width)),
-                  fixed(w_qkv.shape), fixed((1, 3 * width)), fixed(w_out.shape), fixed((1, width)), fixed((1, width)), fixed((1, width)), pl.BlockSpec(memory_space=HBM)],
-        out_specs=(pl.BlockSpec((block_q, width), lambda r, q: (r * blocks + q, 0)), pl.BlockSpec((block_q, width), lambda r, q: (r * blocks + q, 0)), pl.BlockSpec(memory_space=HBM)),
-        scratch_shapes=[pltpu.VMEM((seq, 3 * width), BF16), pltpu.VMEM((block_q, width), BF16), pltpu.SemaphoreType.DMA((tp_size - 1,)), pltpu.SemaphoreType.DMA((tp_size - 1,))],
+                  fixed(w_qkv.shape), fixed((1, 3 * width)), fixed(w_out.shape), fixed((1, width)), fixed((1, width)), fixed((1, width)), hbm, hbm, hbm],
+        out_specs=(pl.BlockSpec((block_q, width), lambda r, q: (r * blocks + q, 0)), pl.BlockSpec((block_q, width), lambda r, q: (r * blocks + q, 0)), *[hbm for _ in pieces]),
+        scratch_shapes=[pltpu.VMEM((seq, 3 * width), BF16), pltpu.VMEM((block_q, width), BF16), pltpu.SemaphoreType.DMA((len(pieces), tp_size - 1)), pltpu.SemaphoreType.DMA((len(pieces), tp_size - 1))],
         compiler_params=pltpu.CompilerParams(dimension_semantics=('arbitrary', 'arbitrary'), collective_id=call_id, has_side_effects=True, vmem_limit_bytes=52 * 1024 * 1024),
         cost_estimate=pl.CostEstimate(flops=30_000_000_000, transcendentals=0, bytes_accessed=40_000_000),
-        name='attention_layer')(lens, x, *norm, w_qkv, b_qkv, w_out, b_out, *norm2, w_move)
-
-
-def dense_body(tp_size, chunk, parts, x_ref, normed_ref, w_in_ref, b_in_ref, w_out_ref, b_out_ref, w_move_ref, o_ref, moved_ref, send_sem, recv_sem):
+        name='attention_layer')(lens, x, *norm, w_qkv, b_qkv, w_out, b_out, *norm2, w_exp_in, w_exp_out, after)
+
+
+def dense_body(tp_size, pieces, parts, x_ref, normed_ref, w_in_ref, b_in_ref, w_out_ref, b_out_ref, w_exp_in_ref, w_exp_out_ref, o_ref, *rest):
     block = pl.program_id(0)
-    copies = exchange(tp_size, w_move_ref, chunk, moved_ref, send_sem, recv_sem)
+    copies = exchange_all(tp_size, (w_exp_in_ref, w_exp_out_ref), pieces, rest[:len(pieces)], *rest[len(pieces):])
 
     @pl.when(block == 0)
     def _():
@@ -149,30 +184,30 @@
             copy.wait()
 
 
-def dense_layer(x, normed, w_in, b_in, w_out, b_out, w_move, tp_size, chunk, call_id):
+def dense_layer(x, normed, w_in, b_in, w_out, b_out, w_exp_in, w_exp_out, tp_size, pieces, call_id):
     tokens, width = x.shape
     block_n = min(256, tokens)
     fixed = lambda shape: pl.BlockSpec(shape, lambda i: (0,) * len(shape), pipeline_mode=pl.Buffered(1))
-    moved = (tp_size - 1,) + w_move.shape[1:]
+    hbm = pl.BlockSpec(memory_space=HBM)
+    dma = pltpu.SemaphoreType.DMA((len(pieces), tp_size - 1))
     return pl.pallas_call(
-        functools.partial(dense_body, tp_size, chunk, 4),
-        out_shape=(jax.ShapeDtypeStruct((tokens, width), BF16), jax.ShapeDtypeStruct(moved, BF16)), grid=(tokens // block_n,),
-        in_specs=[pl.BlockSpec((block_n, width), lambda i: (i, 0)), pl.BlockSpec((block_n, width), lambda i: (i, 0)), fixed(w_in.shape), fixed(b_in.shape), fixed(w_out.shape), fixed((1, width)), pl.BlockSpec(memory_space=HBM)],
-        out_specs=(pl.BlockSpec((block_n, width), lambda i: (i, 0)), pl.BlockSpec(memory_space=HBM)),
-        scratch_shapes=[pltpu.SemaphoreType.DMA((tp_size - 1,)), pltpu.SemaphoreType.DMA((tp_size - 1,))],
+        functools.partial(dense_body, tp_size, pieces, 4),
+        out_shape=(jax.ShapeDtypeStruct((tokens, width), BF16), *landings(tp_size, w_exp_in, pieces)), grid=(tokens // block_n,),
+        in_specs=[pl.BlockSpec((block_n, width), lambda i: (i, 0)), pl.BlockSpec((block_n, width), lambda i: (i, 0)), fixed(w_in.shape), fixed(b_in.shape), fixed(w_out.shape), fixed((1, width)), hbm, hbm],
+        out_specs=(pl.BlockSpec((block_n, width), lambda i: (i, 0)), *[hbm for _ in pieces]),
+        scratch_shapes=[dma, dma],
         compiler_params=pltpu.CompilerParams(dimension_semantics=('arbitrary',), collective_id=call_id, has_side_effects=True, vmem_limit_bytes=52 * 1024 * 1024),
         cost_estimate=pl.CostEstimate(flops=20_000_000_000, transcendentals=0, bytes_accessed=30_000_000),
-        name='dense_layer')(x, normed, w_in, b_in, w_out, b_out, w_move)
-
-
-def experts_body(tp_size, ep_size, early, dispatch_ref, early_refs, w_in_ref, w_out_ref, b_in_ref, b_out_ref, returned_ref,
-                 arrived_ref, late_ref, early_buf, own_buf, out_buf, local_sem, send_sem, recv_sem, back_send, back_recv, move_send, move_recv):
+        name='dense_layer')(x, normed, w_in, b_in, w_out, b_out, w_exp_in, w_exp_out)
+
+
+def experts_body(tp_size, ep_size, early, late, dispatch_ref, early_refs, w_in_ref, w_out_ref, normed_ref, b_in_ref, b_out_ref, w_router_ref, index_ref, returned_ref, gates_ref,
+                 normed_buf, arrived_ref, parts_buf, own_buf, out_buf, local_sem, send_sem, recv_sem, back_send, back_recv, move_send, move_recv):
     chunks, _, slots, width = arrived_ref.shape
     me = lax.axis_index('ep')
     mine = lax.axis_index('tp')
     weights = (w_in_ref, w_out_ref)
     units = [(chunk, which) for chunk in range(chunks) for which in range(2)]
-    late = units[early:]
 
     sends = {}
     for chunk in range(chunks):
@@ -181,14 +216,18 @@
             sends[chunk, distance] = pltpu.make_async_remote_copy(
                 src_ref=dispatch_ref.at[chunk, peer], dst_ref=arrived_ref.at[chunk, me], send_sem=send_sem.at[chunk, distance], recv_sem=recv_sem.at[chunk, distance],
                 device_id={'ep': peer}, device_id_type=pl.DeviceIdType.MESH)
-    moves = {unit: exchange(tp_size, weights[unit[1]], unit[0], late_ref.at[index], move_send.at[index], move_recv.at[index]) for index, unit in enumerate(late)}
+    def landing(piece):
+        chunk, which, start, rows = piece
+        return parts_buf.at[units.index((chunk, which)), :, pl.ds(start, rows)]
+
+    moves = {piece: exchange(tp_size, weights, piece, landing(piece), move_send.at[index], move_recv.at[index]) for index, piece in enumerate(late)}
     kept = [pltpu.make_async_copy(dispatch_ref.at[chunk, me], arrived_ref.at[chunk, me], local_sem.at[0, chunk]) for chunk in range(chunks)]
     owns = {unit: pltpu.make_async_copy(weights[unit[1]].at[unit[0] * tp_size + mine], own_buf.at[unit[0], unit[1]], local_sem.at[1 + unit[1], unit[0]]) for unit in units}
-    earlies = {unit: pltpu.make_async_copy(early_refs[index], early_buf.at[index], local_sem.at[3, index]) for index, unit in enumerate(units[:early])}
+    earlies = {piece: pltpu.make_async_copy(early_refs[index], landing(piece), local_sem.at[3, index]) for index, piece in enumerate(early)}
 
     enter([('tp', tp_size), ('ep', ep_size)])
-    for unit in late:
-        for copy in moves[unit]:
+    for piece in late:
+        for copy in moves[piece]:
             copy.start()
     for chunk in range(chunks):
         for distance in range(1, ep_size):
@@ -196,14 +235,33 @@
         kept[chunk].start()
     for unit in units:
         owns[unit].start()
-        if unit in earlies:
-            earlies[unit].start()
+        for piece in early:
+            if piece[:2] == unit:
+                earlies[piece].start()
+
+    step = normed_buf.shape[1]
+    blocks = normed_ref.shape[0] // step
+    num_experts = w_router_ref.shape[0]
+    expert_ids = lax.broadcasted_iota(jnp.int32, (num_experts, step), 0)
+
+    def load(block):
+        return pltpu.make_async_copy(normed_ref.at[pl.ds(block * step, step)], normed_buf.at[block % 2], local_sem.at[5, block % 2])
+
+    load(0).start()
+    for block in range(blocks):
+        if block + 1 < blocks:
+            load(block + 1).start()
+        load(block).wait()
+        logits = dot_t(w_router_ref[...], normed_buf[block % 2])
+        cols = pl.ds(block * step, step)
+        picked = [jnp.sum(jnp.where(expert_ids == index_ref[pl.ds(k, 1), cols], logits, 0.0), axis=0, keepdims=True) for k in range(2)]
+        gates_ref[pl.ds(0, 1), cols] = jax.nn.sigmoid(picked[0] - picked[1])
+        gates_ref[pl.ds(1, 1), cols] = jax.nn.sigmoid(picked[1] - picked[0])
 
     def part_ref(unit, part):
         if part == 0:
             return own_buf.at[unit[0], unit[1]]
-        index = units.index(unit)
-        return early_buf.at[index, part - 1] if index < early else late_ref.at[index - early, part - 1]
+        return parts_buf.at[units.index(unit), part - 1]
 
     backs = {}
     for chunk in range(chunks):
@@ -214,11 +272,13 @@
         for which in range(2):
             unit = (chunk, which)
             owns[unit].wait()
-            if unit in earlies:
-                earlies[unit].wait()
-            else:
-                for copy in moves[unit]:
-                    copy.wait_recv()
+            for piece in early:
+                if piece[:2] == unit:
+                    earlies[piece].wait()
+            for piece in late:
+                if piece[:2] == unit:
+                    for copy in moves[piece]:
+                        copy.wait_recv()
         before = chunk - out_buf.shape[0]
         if before >= 0:
             for copy in backs[before][:-1]:
@@ -254,87 +314,85 @@
                 copy.wait_send()
         if chunk + out_buf.shape[0] >= chunks:
             backs[chunk][-1].wait()
-    for unit in late:
-        for copy in moves[unit]:
+    for piece in late:
+        for copy in moves[piece]:
             copy.wait_send()
 
 
-def experts(dispatch, early_weights, w_in, w_out, b_in, b_out, tp_size, ep_size, call_id):
+def experts(dispatch, early_weights, w_in, w_out, normed, b_in, b_out, w_router, index, tp_size, ep_size, early, late, call_id):
     chunks, _, slots, width = dispatch.shape
     hidden = w_in.shape[2]
-    early = len(early_weights)
-    late = 2 * chunks - early
     hbm = pl.BlockSpec(memory_space=HBM)
     vmem = pl.BlockSpec(memory_space=pltpu.VMEM)
 
     def body(dispatch_ref, *refs):
-        experts_body(tp_size, ep_size, early, dispatch_ref, refs[:early], *refs[early:])
+        experts_body(tp_size, ep_size, early, late, dispatch_ref, refs[:len(early)], *refs[len(early):])
 
     dma = pltpu.SemaphoreType.DMA
     return pl.pallas_call(
-        body, out_shape=jax.ShapeDtypeStruct(dispatch.shape, BF16),
-        in_specs=[hbm] * (3 + early) + [vmem, vmem], out_specs=hbm,
-        scratch_shapes=[pltpu.VMEM(dispatch.shape, BF16), pltpu.VMEM((late, tp_size - 1, width, hidden), BF16), pltpu.VMEM((early, tp_size - 1, width, hidden), BF16),
+        body, out_shape=(jax.ShapeDtypeStruct(dispatch.shape, BF16), jax.ShapeDtypeStruct(index.shape, F32)),
+        in_specs=[hbm] * (4 + len(early)) + [vmem] * 4, out_specs=(hbm, vmem),
+        scratch_shapes=[pltpu.VMEM((2, min(1024, normed.shape[0]), width), BF16), pltpu.VMEM(dispatch.shape, BF16), pltpu.VMEM((2 * chunks, tp_size - 1, width, hidden), BF16),
                         pltpu.VMEM((chunks, 2, width, hidden), BF16), pltpu.VMEM((2, ep_size, slots, width), BF16),
-                        dma((5, max(chunks, early))), dma((chunks, ep_size)), dma((chunks, ep_size)), dma((chunks, ep_size)), dma((chunks, ep_size)),
-                        dma((late, tp_size - 1)), dma((late, tp_size - 1))],
+                        dma((6, max(chunks, len(early)))), dma((chunks, ep_size)), dma((chunks, ep_size)), dma((chunks, ep_size)), dma((chunks, ep_size)),
+                        dma((len(late), tp_size - 1)), dma((len(late), tp_size - 1))],
         compiler_params=pltpu.CompilerParams(collective_id=call_id, has_side_effects=True, vmem_limit_bytes=62 * 1024 * 1024),
         cost_estimate=pl.CostEstimate(flops=4 * chunks * ep_size * slots * width * hidden * tp_size, transcendentals=0, bytes_accessed=60_000_000),
-        name='experts')(dispatch, *early_weights, w_in, w_out, b_in, b_out)
-
-
-def combine_body(block_t, token_ref, gate_at_ref, gates_ref, slots_ref, o_ref, acc_ref, wide_ref):
+        name='experts')(dispatch, *early_weights, w_in, w_out, normed, b_in, b_out, w_router, index)
+
+
+def combine_body(blocks, token_ref, gate_at_ref, gates_ref, slots_ref, o_ref, acc_ref, wide_ref):
     block = pl.program_id(0)
-    slots, width = wide_ref.shape
-    tokens = o_ref.shape[0]
+    slots, width = slots_ref.shape
+    step = o_ref.shape[0]
+    lanes = 128
 
     @pl.when(block == 0)
     def _():
         def clear(index, carry):
-            rows = pl.ds(pl.multiple_of(index * block_t, block_t), block_t)
-            acc_ref[rows, :] = jnp.zeros((block_t, width), F32)
+            acc_ref[pl.ds(pl.multiple_of(index * 256, 256), 256), :] = jnp.zeros((256, lanes), F32)
             return carry
-        lax.fori_loop(0, tokens // block_t, clear, 0)
-        acc_ref[pl.ds(tokens, 8), :] = jnp.zeros((8, width), F32)
-
-    wide_ref[...] = slots_ref[...].astype(F32)
-    base = block * slots
-
-    def step(index, carry):
-        first = index * 8
-        places = [token_ref[base + first + u] for u in range(8)]
-        gates = [gates_ref[gate_at_ref[base + first + u]] for u in range(8)]
-        old = [acc_ref[pl.ds(places[u], 1), :] for u in range(8)]
-        new = [wide_ref[pl.ds(first + u, 1), :] for u in range(8)]
-        for u in range(8):
-            acc_ref[pl.ds(places[u], 1), :] = old[u] + gates[u] * new[u]
-        return carry
-
-    lax.fori_loop(0, slots // 8, step, 0)
-
-    @pl.when(block == pl.num_programs(0) - 1)
-    def _():
-        def write(index, carry):
-            rows = pl.ds(pl.multiple_of(index * block_t, block_t), block_t)
-            o_ref[rows, :] = acc_ref[rows, :].astype(BF16)
+        lax.fori_loop(0, acc_ref.shape[0] // 256, clear, 0)
+
+    @pl.when(block < blocks)
+    def _():
+        for col in range(width // lanes):
+            wide_ref[pl.ds(col, slots, stride=8), :] = slots_ref[:, col * lanes:(col + 1) * lanes].astype(F32)
+        base = block * slots
+
+        def add(index, carry):
+            first = index * 16
+            places = [pl.ds(pl.multiple_of(token_ref[base + first + u], 8), 8) for u in range(16)]
+            gates = [gates_ref[gate_at_ref[base + first + u]] for u in range(16)]
+            start = pl.multiple_of(index * 128, 128)
+            new = [acc_ref[places[u], :] + gates[u] * wide_ref[pl.ds(start + u * 8, 8), :] for u in range(16)]
+            for u in range(16):
+                acc_ref[places[u], :] = new[u]
             return carry
-        lax.fori_loop(0, tokens // block_t, write, 0)
-
-
-def combine(token_of, gate_at, gates, outputs, tokens):
+
+        lax.fori_loop(0, slots // 16, add, 0)
+
+    @pl.when(block >= blocks)
+    def _():
+        first = pl.multiple_of((block - blocks) * (step * 8), step * 8)
+        for col in range(width // lanes):
+            o_ref[:, col * lanes:(col + 1) * lanes] = acc_ref[pl.ds(first + col, step, stride=8), :].astype(BF16)
+
+
+def combine(place, gate_at, gates, outputs, tokens):
     blocks, slots, width = outputs.shape
-    block_t = min(256, tokens)
+    step = min(512, tokens)
     grid_spec = pltpu.PrefetchScalarGridSpec(
-        num_scalar_prefetch=3, grid=(blocks,),
-        in_specs=[pl.BlockSpec((None, slots, width), lambda b, *_: (b, 0, 0))],
-        out_specs=pl.BlockSpec((tokens, width), lambda b, *_: (0, 0)),
-        scratch_shapes=[pltpu.VMEM((tokens + 8, width), F32), pltpu.VMEM((slots, width), F32)])
+        num_scalar_prefetch=3, grid=(blocks + tokens // step,),
+        in_specs=[pl.BlockSpec((None, slots, width), lambda b, *_: (jnp.minimum(b, blocks - 1), 0, 0))],
+        out_specs=pl.BlockSpec((step, width), lambda b, *_: (jnp.maximum(b - blocks, 0), 0)),
+        scratch_shapes=[pltpu.VMEM(((tokens + 32) * 8, 128), F32), pltpu.VMEM((slots * 8, 128), F32)])
     return pl.pallas_call(
-        functools.partial(combine_body, block_t),
+        functools.partial(combine_body, blocks),
         out_shape=jax.ShapeDtypeStruct((tokens, width), BF16), grid_spec=grid_spec,
         compiler_params=pltpu.CompilerParams(dimension_semantics=('arbitrary',), vmem_limit_bytes=56 * 1024 * 1024),
-        cost_estimate=pl.CostEstimate(flops=30_000_000_000, transcendentals=0, bytes_accessed=2 * tokens * width + 2 * blocks * slots * width),
-        name='combine')(token_of, gate_at, gates, outputs)
+        cost_estimate=pl.CostEstimate(flops=15_000_000_000, transcendentals=0, bytes_accessed=2 * tokens * width + 2 * blocks * slots * width),
+        name='combine')(place, gate_at, gates, outputs)
 
 
 def route(key_ok, expert_idx, num_experts, capacity):
@@ -388,32 +446,30 @@
             return jnp.concatenate(columns + [w_attn_out[j].reshape(head_cols, width)], axis=0)
 
         def unpack_attention(gathered):
-            by_kind = gathered.reshape(tp_size, 4, head_cols, width).transpose(1, 0, 2, 3)
+            by_kind = gathered.reshape(4, ep_size // 4, tp_size, -1, width).transpose(0, 2, 1, 3, 4)
             return by_kind[:3].reshape(3 * heads * head_dim, width), by_kind[3].reshape(heads * head_dim, width)
 
+        def own_slice(value):
+            size = value.shape[0] // ep_size
+            return lax.dynamic_slice_in_dim(value, ep_index * size, size, 0)
+
+        slices = [own_slice(value) for value in (pack_attention(0), w_fc1.T, w_fc2, pack_attention(1))]
+        cuts = [value.shape[0] for value in slices]
+        slices = gather_tp(jnp.concatenate(slices, axis=0))
         small = jnp.concatenate([b_query.reshape(-1), b_value.reshape(-1), b_fc1.reshape(-1), b_exp_in.reshape(-1)])
         small = gather_tp(small)
+        slices, small = lax.optimization_barrier((slices, small))
+        starts = [sum(cuts[:i]) for i in range(5)]
+        first_pack = lax.all_gather(slices[:, :starts[1]], 'ep')
+        fc1_all, fc2_all, second_pack = [lax.all_gather(slices[:, starts[i]:starts[i + 1]], 'ep') for i in range(1, 4)]
+        fc1_all, fc2_all = fc1_all.reshape(-1, width), fc2_all.reshape(-1, width)
+        cut = cuts[1]
         attn_bias_size = 2 * head_cols
         b_query_all = small[:, :attn_bias_size].reshape(tp_size, 2, head_cols).transpose(1, 0, 2).reshape(2, -1)
         b_value_all = small[:, attn_bias_size:2 * attn_bias_size].reshape(tp_size, 2, head_cols).transpose(1, 0, 2).reshape(2, -1)
         b_fc1_all = small[:, 2 * attn_bias_size:2 * attn_bias_size + hidden_cols]
         b_exp_in_all = small[:, 2 * attn_bias_size + hidden_cols:].reshape(tp_size, local_experts, -1)
         b_qkv = jnp.concatenate([b_query_all, jnp.zeros_like(b_query_all), b_value_all], axis=1)
-
-        first_pack = gather_tp(pack_attention(0))
-
-        cut = hidden_cols // ep_size
-
-        def own_slice(value):
-            size = value.shape[0] // ep_size
-            return lax.dynamic_slice_in_dim(value, ep_index * size, size, 0)
-
-        later = jnp.concatenate([own_slice(w_fc1.T), own_slice(w_fc2), own_slice(pack_attention(1))], axis=0)
-        later, first_pack = lax.optimization_barrier((later, first_pack))
-        later = gather_tp(later)
-        fc1_all = lax.all_gather(later[:, :cut], 'ep').reshape(-1, width)
-        fc2_all = lax.all_gather(later[:, cut:2 * cut], 'ep').reshape(-1, width)
-        second_pack = lax.all_gather(later[:, 2 * cut:], 'ep').transpose(1, 0, 2, 3).reshape(tp_size, -1, width)
         b_fc1_all = b_fc1_all.reshape(tp_size, ep_size, cut).transpose(1, 0, 2).reshape(-1)
 
         key_ok = jnp.arange(seq)[None, :] < src_len[:, None]
@@ -429,29 +485,34 @@
         def row(value):
             return value.reshape(1, -1)
 
+        half = width // 2
+        pieces = [(2, 1, 0, half)], [(0, 0, 0, width), (0, 1, 0, width)], [(1, 0, 0, width)], [(1, 1, 0, width), (2, 0, 0, width)], [(2, 1, half, half), (3, 0, 0, width), (3, 1, 0, width)]
+        moved = []
+        moved += move(w_exp_in, w_exp_out, slices[0, :8], tp_size, pieces[0], 4)
         w_qkv, w_out = unpack_attention(first_pack)
-        hidden, normed, moved_0 = attention_layer(x_own, len_own, seq, head_dim, norm(0), w_qkv, row(b_qkv[0]), w_out, row(b_attn_out[0]), norm(1), w_exp_in, tp_size, 0, 0)
-        hidden, moved_1 = dense_layer(hidden, normed, fc1_all, row(b_fc1_all), fc2_all, row(b_fc2), w_exp_out, tp_size, 0, 1)
+        hidden, normed, *landed = attention_layer(x_own, len_own, seq, head_dim, norm(0), w_qkv, row(b_qkv[0]), w_out, row(b_attn_out[0]), norm(1), w_exp_in, w_exp_out, moved[0], tp_size, pieces[1], 0)
+        moved += landed
+        second_pack, hidden = lax.optimization_barrier((second_pack, hidden))
+        hidden, *landed = dense_layer(hidden, normed, fc1_all, row(b_fc1_all), fc2_all, row(b_fc2), w_exp_in, w_exp_out, tp_size, pieces[2], 1)
+        moved += landed
         w_qkv, w_out = unpack_attention(second_pack)
-        hidden, normed, moved_2 = attention_layer(hidden, len_own, seq, head_dim, norm(2), w_qkv, row(b_qkv[1]), w_out, row(b_attn_out[1]), norm(3), w_exp_in, tp_size, 1, 2)
+        hidden, normed, *landed = attention_layer(hidden, len_own, seq, head_dim, norm(2), w_qkv, row(b_qkv[1]), w_out, row(b_attn_out[1]), norm(3), w_exp_in, w_exp_out, moved[0], tp_size, pieces[3], 2)
+        moved += landed
         normed_all = gather_tp(normed, tiled=True)
-
-        logits = jnp.dot(normed_all, w_router.astype(BF16), preferred_element_type=F32)
-        expert_ids = jnp.arange(num_experts, dtype=jnp.int32)
-        flat_idx = expert_idx.reshape(tokens, 2)
-        picked = [jnp.sum(jnp.where(flat_idx[:, k:k + 1] == expert_ids, logits, 0.0), axis=1) for k in range(2)]
-        gates = jnp.concatenate([jax.nn.sigmoid(picked[0] - picked[1]), jax.nn.sigmoid(picked[1] - picked[0]), jnp.zeros((128,), F32)])
 
         b_in_own = lax.dynamic_index_in_dim(b_exp_in_all.reshape(tp_size, own_experts, tp_size, -1), tp_index, 2, keepdims=False)
         part_order = lax.rem(tp_index - jnp.arange(tp_size) + tp_size, tp_size)
         b_in_own = b_in_own[part_order].transpose(1, 0, 2)
         b_out_own = lax.dynamic_index_in_dim(b_exp_out.reshape(own_experts, tp_size, width), tp_index, 1, keepdims=False)
         dispatch = normed_all[dispatch_at.transpose(1, 0, 2).reshape(-1)].reshape(own_experts, ep_size, capacity, width)
-        outputs = experts(dispatch, [moved_0, moved_1, moved_2], w_exp_in, w_exp_out, b_in_own, b_out_own, tp_size, ep_size, 3)
+        outputs, gates = experts(dispatch, moved, w_exp_in, w_exp_out, normed_all, b_in_own, b_out_own,
+                                 w_router.T.astype(BF16), expert_idx.reshape(tokens, 2).T, tp_size, ep_size, sum(pieces[:4], []), pieces[4], 3)
         outputs = outputs.reshape(own_experts * ep_size, capacity, width)
         choice = choice.transpose(1, 0, 2).reshape(-1)
         token_of = jnp.where(choice == 2 * tokens, tokens, source.transpose(1, 0, 2).reshape(-1))
-        partial = combine(token_of, choice, gates, outputs, tokens)
+        gate_at = jnp.where(choice == 2 * tokens, 0, choice)
+        gates = gates.reshape(-1)
+        partial = combine(8 * token_of, gate_at, gates, outputs, tokens)
         summed = lax.psum_scatter(partial, 'tp', scatter_dimension=0, tiled=True)
         result = (hidden.astype(F32) + summed.astype(F32)).astype(BF16)
         return gather_tp(result, tiled=True).reshape(rows, seq, width)

time: 1100 us -> 977 us (0.89)
  Pallas kernels: 566 us -> 504 us
  waiting for transfers between devices: 332 us -> 276 us
    pallas_call x5 -> x6, Pallas kernels: 566 us -> 504 us  [the longest x2 211 us: attention_layer(): pl.pallas_call(functools.partial(attention_body, tp_size, pieces, head_di...]
    all_gather x4 -> x3, waiting for transfers between devices: 221 us -> 164 us  [gather_tp(): return lax.all_gather(value, 'tp', axis=axis, tiled=tiled)]
  transfers between devices with their start and end apart: 8 -> 8, of which waited for: 5 -> 4; matrix products, arithmetic and copies ran while one was open for 10% -> 11% of each run, Pallas kernels for 8% -> 14%
where the time goes in v2:
time: 977 us; the launch traced here: 974 us
  Pallas kernels  504 us (52%)
  waiting for transfers between devices  276 us (28%)
  local copies, waits for them, and re-layouts  140 us (14%)
  other arithmetic  26.1 us (3%)
  between operations  14.6 us (1%)
  blocking collectives  12.4 us (1%)
    pallas_call x2, Pallas kernels, attention_layer(): pl.pallas_call(functools.partial(attention_body, tp_size, pieces, head_di...  211 us
    pallas_call x1, Pallas kernels, experts(): pl.pallas_call(body, out_shape=(jax.ShapeDtypeStruct(dispatch.shape, BF16...  167 us
    all_gather x3, waiting for transfers between devices, gather_tp(): return lax.all_gather(value, 'tp', axis=axis, tiled=tiled)  164 us
    reduce_scatter x1, waiting for transfers between devices, local_fn(): summed = lax.psum_scatter(partial, 'tp', scatter_dimension=0, tiled=True)  110 us
    scatter x2, local copies, waits for them, and re-layouts, route(): choice = choice.at[dest_first].set(ids).at[dest_second].set(ids + tokens)  60.9 us
    pallas_call x1, Pallas kernels, dense_layer(): pl.pallas_call(functools.partial(dense_body, tp_size, pieces, 4), out_sha...  56.3 us
    pallas_call x1, Pallas kernels, combine(): pl.pallas_call(functools.partial(combine_body, blocks), out_shape=jax.Sha...  40.2 us
    pallas_call x1, Pallas kernels, move(): pl.pallas_call(functools.partial(move_body, tp_size, pieces), out_shape=l...  28.3 us
  transfers between devices with their start and end apart: 8, of which 4 were waited for; matrix products, arithmetic and copies ran while one was open for 11% of the time, Pallas kernels for 14%

profile of v2, /device:TPU:97, one launch (start us, length us, event | category | flops | bytes accessed | tf_op | source)
XLA Modules:
  0.0 973.9 jit_solution(14932347006214452974)
XLA Ops:
  6.6 1.2 fusion.31
  7.7 1.1 fusion.32
  8.9 1.1 fusion.33
  10.0 1.1 fusion.34
  11.1 0.8 constant_dynamic-slice_fusion.5
  11.9 1.1 copy.108
  13.0 0.9 constant_dynamic-slice_fusion.4
  14.3 0.9 pad_maximum_fusion
  15.6 12.4 %all-gather.6 = f32[4,1,13824]{2,1,0:T(1,128)S(1)} all-gather(f32[1,1,13824]{2,1,0:T(1,128)S(1)} %reshape.375), channel_id=3, replica_groups=mesh['dp'=1,'tp'=4,'ep'=8] {'tp'}, dimensions={0}, use_global_device_ids=true | all-gather | bytes 276480 | tf_op jit(solution)/shard_map/all_gather | solution.py:424
  28.1 21.1 %all-gather.19.cloned.1.call-done = bf16[1536,768]{1,0:T(8,128)(2,1)} async-done(((bf16[384,768]{1,0:T(8,128)(2,1)}), bf16[1536,768]{1,0:T(8,128)(2,1)}) %all-gather.19.cloned.1.call-update) | async-done | bytes 2359312 | tf_op jit(solution)/shard_map/all_gather | solution.py:424
  49.2 3.1 fusion.30
  52.4 0.7 all-gather.21.cloned.1.call-update
  55.2 3.7 constant_dynamic-slice_fusion.3
  59.5 1.3 slice_bitcast_fusion.2.after_ref
  60.9 28.3 %move.1.after_ref.refs_0_ = bf16[3,384,768]{2,1,0:T(8,128)(2,1)} custom-call(bf16[16,768,768]{2,1,0:T(8,128)(2,1)} %refs_6_.1, bf16[16,768,768]{2,1,0:T(8,128)(2,1)} %refs_7_.1, bf16[8,768]{1,0:T(8,128)(2,1)} %slice_bitcast_fusion.2.after_ref), custom_call_target="tpu_custom_call" | custom-call | flops 20000000000 | bytes 10000000 | tf_op jit(solution)/shard_map/move/pallas_call | solution.py:75
  89.2 2.7 copy.123
  92.0 2.0 slice.164
  94.1 106.7 %attention_layer.2 = (bf16[2048,768]{1,0:T(8,128)(2,1)}, bf16[2048,768]{1,0:T(8,128)(2,1)}, bf16[3,768,768]{2,1,0:T(8,128)(2,1)}, bf16[3,768,768]{2,1,0:T(8,128)(2,1)}) custom-call(s32[2]{0:T(128)S(1)} %dynamic_slice.30.lens_ref, bf16[2048,768]{1,0:T(8,128)(2,1)} %bitcast.138, f32[1,768]{1,0:T(1,128)S(1)} %get-tuple-element.78.gain_ref, ...), custom_call_target="tpu_custom_call" | custom-call | flops 30000001024 | bytes 40000000 | tf_op jit(solution)/shard_map/attention_layer/pallas_call | solution.py:150
  200.9 2.2 slice.167
  203.1 1.3 slice.169
  204.5 2.1 copy.94
  206.7 56.3 %dense_layer.1 = (bf16[2048,768]{1,0:T(8,128)(2,1)}, bf16[3,768,768]{2,1,0:T(8,128)(2,1)}) custom-call(bf16[2048,768]{1,0:T(8,128)(2,1)} %get-tuple-element.24.x_ref, bf16[2048,768]{1,0:T(8,128)(2,1)} %get-tuple-element.25.normed_ref, bf16[3072,768]{1,0:T(8,128)(2,1)} %bitcast.179, f32[1,3072]{1,0:T(1,128)S(1)} %reshape_reshape.9.b_in_ref, ...), custom_call_target="tpu_custom_call" | custom-call | flops 20000000000 | bytes 30000000 | tf_op jit(solution)/shard_map/dense_layer/pallas_call | solution.py:193
  263.0 104.7 %attention_layer.3 = (bf16[2048,768]{1,0:T(8,128)(2,1)}, bf16[2048,768]{1,0:T(8,128)(2,1)}, bf16[3,768,768]{2,1,0:T(8,128)(2,1)}, bf16[3,768,768]{2,1,0:T(8,128)(2,1)}) custom-call(s32[2]{0:T(128)S(1)} %dynamic_slice.30.lens_ref, bf16[2048,768]{1,0:T(8,128)(2,1)} %get-tuple-element.26.x_ref, f32[1,768]{1,0:T(1,128)S(1)} %get-tuple-element.77.gain_ref, ...), custom_call_target="tpu_custom_call" | custom-call | flops 30000001024 | bytes 40000000 | tf_op jit(solution)/shard_map/attention_layer/pallas_call | solution.py:150
  368.6 2.2 fusion.4
  370.8 2.0 copy-done.3
  372.9 2.7 add_add_fusion.1
  375.6 4.4 copy.98
  380.2 2.2 fusion.2
  382.5 2.0 copy-done.2
  384.6 2.7 add_add_fusion
  387.3 2.4 copy.100
  389.7 4.3 convert_reduce_fusion
  394.1 4.1 fusion.1
  398.4 30.5 %scatter_custom_fusion = s32[16385]{0:T(1024)S(1)} fusion(s32[8192]{0:T(1024)S(1)} %bitcast.175, s32[8192]{0:T(1024)S(1)} %iota.26, s32[]{:T(128)} %constant.28.clone.1), kind=kCustom, calls=%fused_computation.55 | custom fusion | bytes 65544 | tf_op jit(solution)/shard_map/scatter | solution.py:415
  428.9 30.5 %scatter_fusion = s32[16385]{0:T(1024)S(1)} fusion(s32[16385]{0:T(1024)S(1)} %scatter_custom_fusion, s32[8192]{0:T(1024)S(1)} %bitcast.159, s32[8192]{0:T(1024)S(1)} %iota_add_fusion), kind=kCustom, calls=%fused_computation.3 | custom fusion | bytes 131072 | tf_op jit(solution)/shard_map/scatter | solution.py:415
  459.5 0.6 copy.128
  460.1 0.8 copy.105
  461.0 0.6 compare_select_fusion.4
  462.5 0.6 copy.126
  463.1 26.2 %all-gather.15.cloned.1.call-done.refs_8_ = bf16[8192,768]{1,0:T(8,128)(2,1)} async-done(((bf16[2048,768]{1,0:T(8,128)(2,1)}), bf16[8192,768]{1,0:T(8,128)(2,1)}) %all-gather.15.cloned.1.call-update) | async-done | bytes 12582928 | tf_op jit(solution)/shard_map/all_gather | solution.py:424
  489.3 25.5 %gather_fusion = bf16[4096,768]{1,0:T(8,128)(2,1)} fusion(bf16[8192,768]{1,0:T(8,128)(2,1)} %all-gather.15.cloned.1.call-done.refs_8_, s32[4096]{0:T(1024)S(1)} %broadcast_clamp_fusion), kind=kCustom, calls=%fused_computation | custom fusion | bytes 12599296 | tf_op jit(solution)/shard_map/gather | solution.py:507
  514.8 167.3 %experts.1 = (bf16[4,8,128,768]{3,2,1,0:T(8,128)(2,1)}, f32[2,8192]{1,0:T(2,128)}) custom-call(bf16[4,8,128,768]{3,2,1,0:T(8,128)(2,1)} %bitcast.132, bf16[3,384,768]{2,1,0:T(8,128)(2,1)} %move.1.after_ref.refs_0_, bf16[3,768,768]{2,1,0:T(8,128)(2,1)} %get-tuple-element.30.refs_1_, bf16[3,768,768]{2,1,0:T(8,128)(2,1)} %get-tuple-element.31.refs_2_, ...), custom_call_target="tpu_custom_call" | custom-call | flops 38654705664 | bytes 60000000 | tf_op jit(solution)/shard_map/experts/pallas_call | solution.py:332
  682.1 1.5 copy.113
  683.6 40.2 %combine.1 = bf16[8192,768]{1,0:T(8,128)(2,1)} custom-call(s32[4096]{0:T(1024)} %get-tuple-element.62.token_ref, s32[4096]{0:T(1024)} %get-tuple-element.61.gate_at_ref, f32[16384]{0:T(1024)} %bitcast.171, bf16[32,128,768]{2,1,0:T(8,128)(2,1)} %bitcast.181), custom_call_target="tpu_custom_call" | custom-call | flops 15000000512 | bytes 18874368 | tf_op jit(solution)/shard_map/combine/pallas_call | solution.py:390
  724.0 110.4 %reduce-scatter.2.cloned.1.call-done = bf16[2048,768]{1,0:T(8,128)(2,1)} async-done(((bf16[8192,768]{1,0:T(8,128)(2,1)}), bf16[2048,768]{1,0:T(8,128)(2,1)}) %reduce-scatter.2.cloned.1.call-update) | async-done | bytes 3145744 | tf_op jit(solution)/shard_map/reduce_scatter | solution.py:516
  834.3 5.3 add_convert_fusion
  839.7 116.4 %all-gather.17.cloned.1.call-done = bf16[8192,768]{1,0:T(8,128)(2,1)} async-done(((bf16[2048,768]{1,0:T(8,128)(2,1)}), bf16[8192,768]{1,0:T(8,128)(2,1)}) %all-gather.17.cloned.1.call-update) | async-done | bytes 12582928 | tf_op jit(solution)/shard_map/all_gather | solution.py:424
  956.1 10.5 %copy.131 = bf16[8,1024,768]{2,1,0:T(8,128)(2,1)} copy(bf16[8,1024,768]{2,1,0:T(8,128)(2,1)} %bitcast.131) | data formatting | bytes 25165824
  (116 shorter events, 6.4 us)
Async XLA Ops:
  6.5 4.5 copy-start
  6.6 42.6 %all-gather.19.cloned.1.call-start = ((), (), s32[]{:S(2)}) async-start(), calls=%async_computation.4 | async-start | bytes 2949120 | tf_op jit(solution)/shard_map/all_gather | solution.py:424
  8.8 6.5 copy-start.14
  8.8 6.6 copy-start.15
  8.9 6.7 copy-start.12
  11.9 3.4 copy-start.7
  15.2 39.8 %copy-start.13 = (f32[768]{0:T(1024)S(1)}, f32[768]{0:T(1024)}, u32[]{:S(2)}) copy-start(f32[768]{0:T(1024)} %param.36) | copy-start | bytes 9220
  15.2 39.8 %copy-start.16 = (s32[8]{0:T(128)S(1)}, s32[8]{0:T(128)}, u32[]{:S(2)}) copy-start(s32[8]{0:T(128)} %param.22) | copy-start | bytes 100
  15.3 74.0 %all-gather.23.cloned.1.call-start = ((), (), s32[]{:S(2)}) async-start(), calls=%async_computation.6 | async-start | bytes 5308416 | tf_op jit(solution)/shard_map/all_gather | solution.py:463
  52.3 6.6 copy-start.11
  52.3 6.6 copy-start.9
  52.3 6.6 copy-start.10
  52.3 148.5 %all-gather.21.cloned.1.call-start = ((), (), s32[]{:S(2)}) async-start(), calls=%async_computation.5 | async-start | bytes 5308416 | tf_op jit(solution)/shard_map/all_gather | solution.py:464
  53.1 153.5 %all-gather.25.cloned.1.call-start = ((), (), s32[]{:S(2)}) async-start(), calls=%async_computation.7 | async-start | bytes 5308416 | tf_op jit(solution)/shard_map/all_gather | solution.py:464
  53.8 152.9 %all-gather.27.cloned.1.call-start = ((), (), s32[]{:S(2)}) async-start(), calls=%async_computation.8 | async-start | bytes 5308416 | tf_op jit(solution)/shard_map/all_gather | solution.py:464
  54.4 434.9 %all-gather.15.cloned.1.call-start = ((), (), s32[]{:S(2)}) async-start(), calls=%async_computation.1 | async-start | bytes 15728640 | tf_op jit(solution)/shard_map/all_gather | solution.py:424
  263.0 105.0 %copy-start.6 = (s32[8,1024,2]{1,2,0:T(2,128)S(1)}, s32[8,1024,2]{1,2,0:T(2,128)}, u32[]{:S(2)}) copy-start(s32[8,1024,2]{1,2,0:T(2,128)} %param.23) | copy-start | bytes 196612
  367.7 466.6 %reduce-scatter.2.cloned.1.call-start = ((), (), s32[]{:S(2)}) async-start(), calls=%async_computation.2 | async-start | bytes 15728640 | tf_op jit(solution)/shard_map/reduce_scatter | solution.py:516
  370.8 2.0 copy-start.3
  382.4 2.0 copy-start.2
  387.2 2.5 copy-start.4
  428.9 30.5 %copy-start.8 = (f32[16,768]{1,0:T(8,128)S(1)}, f32[16,768]{1,0:T(8,128)}, u32[]{:S(2)}) copy-start(f32[16,768]{1,0:T(8,128)} %param.41) | copy-start | bytes 147460
  428.9 31.2 %copy-start.5 = (f32[768,128]{1,0:T(8,128)S(1)}, f32[768,128]{1,0:T(8,128)}, u32[]{:S(2)}) copy-start(f32[768,128]{1,0:T(8,128)} %param.37) | copy-start | bytes 1179652
  723.9 232.2 %all-gather.17.cloned.1.call-start = ((), (), s32[]{:S(2)}) async-start(), calls=%async_computation.3 | async-start | bytes 15728640 | tf_op jit(solution)/shard_map/all_gather | solution.py:424
  956.1 10.6 %copy-start.1 = (bf16[768,768]{1,0:T(8,128)(2,1)S(1)}, bf16[768,768]{1,0:T(8,128)(2,1)}, u32[]{:S(2)}) copy-start(bf16[768,768]{1,0:T(8,128)(2,1)} %param.33) | copy-start | bytes 3538948
Sparse Core Ops, SparseCore 0:
  15.3 33.7 all-gather.18
  52.4 32.1 all-gather.22
  86.2 31.4 all-gather.20
  119.1 31.4 all-gather.24
  152.0 31.4 all-gather.26
  367.9 121.3 all-gather.14
  724.0 110.2 reduce-scatter.1
  839.8 116.1 all-gather.16

commit v3 on v2

--- a/solution.py
+++ b/solution.py
@@ -201,8 +201,8 @@
         name='dense_layer')(x, normed, w_in, b_in, w_out, b_out, w_exp_in, w_exp_out)
 
 
-def experts_body(tp_size, ep_size, early, late, dispatch_ref, early_refs, w_in_ref, w_out_ref, normed_ref, b_in_ref, b_out_ref, w_router_ref, index_ref, returned_ref, gates_ref,
-                 normed_buf, arrived_ref, parts_buf, own_buf, out_buf, local_sem, send_sem, recv_sem, back_send, back_recv, move_send, move_recv):
+def experts_body(tp_size, ep_size, early, late, dispatch_ref, early_refs, w_in_ref, w_out_ref, b_in_ref, b_out_ref, w_router_ref, other_ref, returned_ref, gates_ref,
+                 sent_buf, arrived_ref, parts_buf, own_buf, out_buf, local_sem, send_sem, recv_sem, back_send, back_recv, move_send, move_recv):
     chunks, _, slots, width = arrived_ref.shape
     me = lax.axis_index('ep')
     mine = lax.axis_index('tp')
@@ -239,29 +239,42 @@
             if piece[:2] == unit:
                 earlies[piece].start()
 
-    step = normed_buf.shape[1]
-    blocks = normed_ref.shape[0] // step
-    num_experts = w_router_ref.shape[0]
-    expert_ids = lax.broadcasted_iota(jnp.int32, (num_experts, step), 0)
-
-    def load(block):
-        return pltpu.make_async_copy(normed_ref.at[pl.ds(block * step, step)], normed_buf.at[block % 2], local_sem.at[5, block % 2])
+    lane = lax.broadcasted_iota(jnp.int32, (1, w_router_ref.shape[1]), 1)
+    group = lax.broadcasted_iota(jnp.int32, (ep_size * slots, 1), 0) // slots
+
+    def load(chunk):
+        return pltpu.make_async_copy(dispatch_ref.at[chunk], sent_buf.at[chunk % 2], local_sem.at[5, chunk % 2])
 
     load(0).start()
-    for block in range(blocks):
-        if block + 1 < blocks:
-            load(block + 1).start()
-        load(block).wait()
-        logits = dot_t(w_router_ref[...], normed_buf[block % 2])
-        cols = pl.ds(block * step, step)
-        picked = [jnp.sum(jnp.where(expert_ids == index_ref[pl.ds(k, 1), cols], logits, 0.0), axis=0, keepdims=True) for k in range(2)]
-        gates_ref[pl.ds(0, 1), cols] = jax.nn.sigmoid(picked[0] - picked[1])
-        gates_ref[pl.ds(1, 1), cols] = jax.nn.sigmoid(picked[1] - picked[0])
+    for chunk in range(chunks):
+        if chunk + 1 < chunks:
+            load(chunk + 1).start()
+        load(chunk).wait()
+        logits = jnp.dot(sent_buf[chunk % 2].reshape(ep_size * slots, width), w_router_ref[...], preferred_element_type=F32)
+        rows = pl.ds(chunk * ep_size * slots, ep_size * slots)
+        own = jnp.sum(jnp.where(lane == group * (chunks * tp_size) + (chunk * tp_size + mine), logits, 0.0), axis=1, keepdims=True)
+        other = jnp.sum(jnp.where(lane == other_ref[rows, :], logits, 0.0), axis=1, keepdims=True)
+        gates_ref[rows, :] = jax.nn.sigmoid(own - other)
 
     def part_ref(unit, part):
         if part == 0:
             return own_buf.at[unit[0], unit[1]]
         return parts_buf.at[units.index(unit), part - 1]
+
+    def give_back(chunk, slot, index):
+        for half in range(2):
+            peer = 2 * index + half
+            distance = lax.rem(peer - me + ep_size, ep_size)
+
+            @pl.when(distance == 0)
+            def _():
+                pltpu.make_async_copy(out_buf.at[slot, peer], returned_ref.at[chunk, me], local_sem.at[4, chunk]).start()
+
+            @pl.when(distance != 0)
+            def _():
+                pltpu.make_async_remote_copy(
+                    src_ref=out_buf.at[slot, peer], dst_ref=returned_ref.at[chunk, me], send_sem=back_send.at[chunk, distance], recv_sem=back_recv.at[chunk, distance],
+                    device_id={'ep': peer}, device_id_type=pl.DeviceIdType.MESH).start()
 
     backs = {}
     for chunk in range(chunks):
@@ -292,9 +305,15 @@
                 inner = jnp.dot(tokens, part_ref((chunk, 0), part)[...], preferred_element_type=F32) + b_in_ref[chunk, pl.ds(part, 1), :]
                 total += jnp.dot(jnp.maximum(inner, 0.0).astype(BF16), part_ref((chunk, 1), part)[...], preferred_element_type=F32)
             out_buf[slot, pl.ds(2 * index, 2)] = (total + b_out_ref[pl.ds(chunk, 1), :]).astype(BF16).reshape(2, slots, width)
+
+            @pl.when(index > 0)
+            def _():
+                give_back(chunk, slot, index - 1)
+
             return carry
 
         lax.fori_loop(0, ep_size // 2, rows, 0)
+        give_back(chunk, slot, ep_size // 2 - 1)
         backs[chunk] = []
         for distance in range(1, ep_size):
             peer = away('ep', ep_size, distance)
@@ -302,9 +321,6 @@
                 src_ref=out_buf.at[slot, peer], dst_ref=returned_ref.at[chunk, me], send_sem=back_send.at[chunk, distance], recv_sem=back_recv.at[chunk, distance],
                 device_id={'ep': peer}, device_id_type=pl.DeviceIdType.MESH))
         backs[chunk].append(pltpu.make_async_copy(out_buf.at[slot, me], returned_ref.at[chunk, me], local_sem.at[4, chunk]))
-        for copy in backs[chunk]:
-            copy.start()
-
     for chunk in range(chunks):
         for distance in range(1, ep_size):
             sends[chunk, distance].wait_send()
@@ -319,7 +335,7 @@
             copy.wait_send()
 
 
-def experts(dispatch, early_weights, w_in, w_out, normed, b_in, b_out, w_router, index, tp_size, ep_size, early, late, call_id):
+def experts(dispatch, early_weights, w_in, w_out, b_in, b_out, w_router, other, tp_size, ep_size, early, late, call_id):
     chunks, _, slots, width = dispatch.shape
     hidden = w_in.shape[2]
     hbm = pl.BlockSpec(memory_space=HBM)
@@ -330,18 +346,18 @@
 
     dma = pltpu.SemaphoreType.DMA
     return pl.pallas_call(
-        body, out_shape=(jax.ShapeDtypeStruct(dispatch.shape, BF16), jax.ShapeDtypeStruct(index.shape, F32)),
-        in_specs=[hbm] * (4 + len(early)) + [vmem] * 4, out_specs=(hbm, vmem),
-        scratch_shapes=[pltpu.VMEM((2, min(1024, normed.shape[0]), width), BF16), pltpu.VMEM(dispatch.shape, BF16), pltpu.VMEM((2 * chunks, tp_size - 1, width, hidden), BF16),
+        body, out_shape=(jax.ShapeDtypeStruct(dispatch.shape, BF16), jax.ShapeDtypeStruct(other.shape, F32)),
+        in_specs=[hbm] * (3 + len(early)) + [vmem] * 4, out_specs=(hbm, vmem),
+        scratch_shapes=[pltpu.VMEM((2,) + dispatch.shape[1:], BF16), pltpu.VMEM(dispatch.shape, BF16), pltpu.VMEM((2 * chunks, tp_size - 1, width, hidden), BF16),
                         pltpu.VMEM((chunks, 2, width, hidden), BF16), pltpu.VMEM((2, ep_size, slots, width), BF16),
                         dma((6, max(chunks, len(early)))), dma((chunks, ep_size)), dma((chunks, ep_size)), dma((chunks, ep_size)), dma((chunks, ep_size)),
                         dma((len(late), tp_size - 1)), dma((len(late), tp_size - 1))],
         compiler_params=pltpu.CompilerParams(collective_id=call_id, has_side_effects=True, vmem_limit_bytes=62 * 1024 * 1024),
         cost_estimate=pl.CostEstimate(flops=4 * chunks * ep_size * slots * width * hidden * tp_size, transcendentals=0, bytes_accessed=60_000_000),
-        name='experts')(dispatch, *early_weights, w_in, w_out, normed, b_in, b_out, w_router, index)
-
-
-def combine_body(blocks, token_ref, gate_at_ref, gates_ref, slots_ref, o_ref, acc_ref, wide_ref):
+        name='experts')(dispatch, *early_weights, w_in, w_out, b_in, b_out, w_router, other)
+
+
+def combine_body(blocks, token_ref, slots_ref, gates_ref, o_ref, acc_ref, wide_ref):
     block = pl.program_id(0)
     slots, width = slots_ref.shape
     step = o_ref.shape[0]
@@ -357,15 +373,14 @@
     @pl.when(block < blocks)
     def _():
         for col in range(width // lanes):
-            wide_ref[pl.ds(col, slots, stride=8), :] = slots_ref[:, col * lanes:(col + 1) * lanes].astype(F32)
+            wide_ref[pl.ds(col, slots, stride=8), :] = slots_ref[:, col * lanes:(col + 1) * lanes].astype(F32) * gates_ref[...]
         base = block * slots
 
         def add(index, carry):
             first = index * 16
             places = [pl.ds(pl.multiple_of(token_ref[base + first + u], 8), 8) for u in range(16)]
-            gates = [gates_ref[gate_at_ref[base + first + u]] for u in range(16)]
             start = pl.multiple_of(index * 128, 128)
-            new = [acc_ref[places[u], :] + gates[u] * wide_ref[pl.ds(start + u * 8, 8), :] for u in range(16)]
+            new = [acc_ref[places[u], :] + wide_ref[pl.ds(start + u * 8, 8), :] for u in range(16)]
             for u in range(16):
                 acc_ref[places[u], :] = new[u]
             return carry
@@ -379,12 +394,12 @@
             o_ref[:, col * lanes:(col + 1) * lanes] = acc_ref[pl.ds(first + col, step, stride=8), :].astype(BF16)
 
 
-def combine(place, gate_at, gates, outputs, tokens):
+def combine(place, gates, outputs, tokens):
     blocks, slots, width = outputs.shape
     step = min(512, tokens)
     grid_spec = pltpu.PrefetchScalarGridSpec(
-        num_scalar_prefetch=3, grid=(blocks + tokens // step,),
-        in_specs=[pl.BlockSpec((None, slots, width), lambda b, *_: (jnp.minimum(b, blocks - 1), 0, 0))],
+        num_scalar_prefetch=1, grid=(blocks + tokens // step,),
+        in_specs=[pl.BlockSpec((None, slots, width), lambda b, *_: (jnp.minimum(b, blocks - 1), 0, 0)), pl.BlockSpec((slots, 1), lambda b, *_: (jnp.minimum(b, blocks - 1), 0))],
         out_specs=pl.BlockSpec((step, width), lambda b, *_: (jnp.maximum(b - blocks, 0), 0)),
         scratch_shapes=[pltpu.VMEM(((tokens + 32) * 8, 128), F32), pltpu.VMEM((slots * 8, 128), F32)])
     return pl.pallas_call(
@@ -392,7 +407,111 @@
         out_shape=jax.ShapeDtypeStruct((tokens, width), BF16), grid_spec=grid_spec,
         compiler_params=pltpu.CompilerParams(dimension_semantics=('arbitrary',), vmem_limit_bytes=56 * 1024 * 1024),
         cost_estimate=pl.CostEstimate(flops=15_000_000_000, transcendentals=0, bytes_accessed=2 * tokens * width + 2 * blocks * slots * width),
-        name='combine')(place, gate_at, gates, outputs)
+        name='combine')(place, outputs, gates)
+
+
+def finish_body(tp_size, count, partial_ref, hidden_ref, o_ref, partial_buf, hidden_buf, sum_buf, own_buf, load_sem, sum_send, sum_recv, out_send, out_recv):
+    me = lax.axis_index('tp')
+    own_tokens, _ = hidden_ref.shape
+    size = own_tokens // (2 * count)
+    hops = tp_size - 1
+    step_to = (1, tp_size - 1)
+
+    def rows(way, chunk, index):
+        return pl.ds(pl.multiple_of(chunk * own_tokens + (way * count + index) * size, size), size)
+
+    def behind(way, distance):
+        return away('tp', tp_size, (tp_size - distance) % tp_size if way == 0 else distance % tp_size)
+
+    def send_sum(way, hop, index, src_ref):
+        return pltpu.make_async_remote_copy(
+            src_ref=src_ref, dst_ref=sum_buf.at[way, hop, index], send_sem=sum_send.at[way, hop, index], recv_sem=sum_recv.at[way, hop, index],
+            device_id={'tp': away('tp', tp_size, step_to[way])}, device_id_type=pl.DeviceIdType.MESH)
+
+    def send_out(way, hop, index, src_ref, chunk):
+        return pltpu.make_async_remote_copy(
+            src_ref=src_ref, dst_ref=o_ref.at[rows(way, chunk, index)], send_sem=out_send.at[way, hop, index], recv_sem=out_recv.at[way, hop, index],
+            device_id={'tp': away('tp', tp_size, step_to[way])}, device_id_type=pl.DeviceIdType.MESH)
+
+    loads = [pltpu.make_async_copy(partial_ref, partial_buf, load_sem.at[0]), pltpu.make_async_copy(hidden_ref, hidden_buf, load_sem.at[1])]
+    for load in loads:
+        load.start()
+    barrier = pltpu.get_barrier_semaphore()
+    for distance in step_to:
+        pl.semaphore_signal(barrier, inc=1, device_id={'tp': away('tp', tp_size, distance)}, device_id_type=pl.DeviceIdType.MESH)
+    pl.semaphore_wait(barrier, 2)
+
+    def first(index, carry):
+        for way in range(2):
+            send_sum(way, 0, index, partial_ref.at[rows(way, behind(way, 1), index)]).start()
+        return carry
+
+    lax.fori_loop(0, count, first, 0)
+    for load in loads:
+        load.wait()
+
+    def keep(way, index):
+        own = own_buf.at[way, index]
+        return pltpu.make_async_copy(own, o_ref.at[rows(way, me, index)], load_sem.at[2 + way])
+
+    for hop in range(1, tp_size):
+        def add(index, carry):
+            for way in range(2):
+                send_sum(way, hop - 1, index, sum_buf.at[way, hop - 1, index]).wait_recv()
+                total = sum_buf[way, hop - 1, index].astype(F32) + partial_buf[rows(way, behind(way, hop + 1), index), :].astype(F32)
+                if hop < hops:
+                    sum_buf[way, hop - 1, index] = total.astype(BF16)
+                else:
+                    own_rows = pl.ds(pl.multiple_of((way * count + index) * size, size), size)
+                    own_buf[way, index] = (total.astype(BF16).astype(F32) + hidden_buf[own_rows, :].astype(F32)).astype(BF16)
+            for way in range(2):
+                if hop < hops:
+                    send_sum(way, hop, index, sum_buf.at[way, hop - 1, index]).start()
+                else:
+                    send_out(way, 0, index, own_buf.at[way, index], me).start()
+                    keep(way, index).start()
+                    keep(way, index).wait()
+            return carry
+
+        lax.fori_loop(0, count, add, 0)
+
+    for hop in range(1, tp_size):
+        def forward(index, carry):
+            for way in range(2):
+                chunk = behind(way, hop)
+                arrived = o_ref.at[rows(way, chunk, index)]
+                send_out(way, hop - 1, index, arrived, chunk).wait_recv()
+                if hop < hops:
+                    send_out(way, hop, index, arrived, chunk).start()
+            return carry
+
+        lax.fori_loop(0, count, forward, 0)
+
+    def drain(index, carry):
+        for way in range(2):
+            for hop in range(hops):
+                send_sum(way, hop, index, sum_buf.at[way, hop, index]).wait_send()
+                send_out(way, hop, index, own_buf.at[way, index], me).wait_send()
+        return carry
+
+    lax.fori_loop(0, count, drain, 0)
+
+
+def finish(partial, hidden, tp_size, call_id):
+    tokens, width = partial.shape
+    own_tokens = hidden.shape[0]
+    size = min(256, own_tokens // 2)
+    count = own_tokens // (2 * size)
+    hops = tp_size - 1
+    hbm = pl.BlockSpec(memory_space=HBM)
+    dma = pltpu.SemaphoreType.DMA
+    return pl.pallas_call(
+        functools.partial(finish_body, tp_size, count), out_shape=jax.ShapeDtypeStruct(partial.shape, BF16), in_specs=[hbm, hbm], out_specs=hbm,
+        scratch_shapes=[pltpu.VMEM(partial.shape, BF16), pltpu.VMEM(hidden.shape, BF16), pltpu.VMEM((2, hops, count, size, width), BF16), pltpu.VMEM((2, count, size, width), BF16),
+                        dma((4,)), dma((2, hops, count)), dma((2, hops, count)), dma((2, hops, count)), dma((2, hops, count))],
+        compiler_params=pltpu.CompilerParams(collective_id=call_id, has_side_effects=True, vmem_limit_bytes=56 * 1024 * 1024),
+        cost_estimate=pl.CostEstimate(flops=100_000_000_000, transcendentals=0, bytes_accessed=60_000_000),
+        name='finish')(partial, hidden)
 
 
 def route(key_ok, expert_idx, num_experts, capacity):
@@ -410,9 +529,9 @@
     dump = num_experts * capacity
     dest_first = jnp.where(valid & (slot_first < capacity), first * capacity + slot_first, dump)
     dest_second = jnp.where(valid & (slot_second < capacity), second * capacity + slot_second, dump)
-    choice = jnp.full((dump + 1,), 2 * tokens, jnp.int32)
+    choice = jnp.full((dump + 1,), -1, jnp.int32)
     ids = jnp.arange(tokens, dtype=jnp.int32)
-    choice = choice.at[dest_first].set(ids).at[dest_second].set(ids + tokens)
+    choice = choice.at[dest_first].set(ids + tokens * second).at[dest_second].set(ids + tokens * first)
     return choice[:dump].reshape(num_experts, capacity)
 
 
@@ -458,7 +577,7 @@
         slices = gather_tp(jnp.concatenate(slices, axis=0))
         small = jnp.concatenate([b_query.reshape(-1), b_value.reshape(-1), b_fc1.reshape(-1), b_exp_in.reshape(-1)])
         small = gather_tp(small)
-        slices, small = lax.optimization_barrier((slices, small))
+        slices, small, x_own = lax.optimization_barrier((slices, small, x_own))
         starts = [sum(cuts[:i]) for i in range(5)]
         first_pack = lax.all_gather(slices[:, :starts[1]], 'ep')
         fc1_all, fc2_all, second_pack = [lax.all_gather(slices[:, starts[i]:starts[i + 1]], 'ep') for i in range(1, 4)]
@@ -476,8 +595,12 @@
         choice_all = route(key_ok, expert_idx, num_experts, capacity)
         choice = choice_all.reshape(ep_size, own_experts, tp_size, capacity)
         choice = lax.dynamic_index_in_dim(choice, tp_index, 2, keepdims=False)
-        source = jnp.where(choice < tokens, choice, choice - tokens)
-        dispatch_at = jnp.where(choice == 2 * tokens, 0, source)
+        choice = choice.transpose(1, 0, 2).reshape(-1)
+        filled = choice >= 0
+        choice = jnp.where(filled, choice, 0)
+        source = lax.rem(choice, tokens)
+        other = lax.div(choice, tokens).reshape(-1, 1)
+        place = 8 * jnp.where(filled, source, tokens)
 
         def norm(i):
             return ln_gain[i].reshape(1, width), ln_bias[i].reshape(1, width)
@@ -504,18 +627,12 @@
         part_order = lax.rem(tp_index - jnp.arange(tp_size) + tp_size, tp_size)
         b_in_own = b_in_own[part_order].transpose(1, 0, 2)
         b_out_own = lax.dynamic_index_in_dim(b_exp_out.reshape(own_experts, tp_size, width), tp_index, 1, keepdims=False)
-        dispatch = normed_all[dispatch_at.transpose(1, 0, 2).reshape(-1)].reshape(own_experts, ep_size, capacity, width)
-        outputs, gates = experts(dispatch, moved, w_exp_in, w_exp_out, normed_all, b_in_own, b_out_own,
-                                 w_router.T.astype(BF16), expert_idx.reshape(tokens, 2).T, tp_size, ep_size, sum(pieces[:4], []), pieces[4], 3)
+        dispatch = normed_all[source].reshape(own_experts, ep_size, capacity, width)
+        outputs, gates = experts(dispatch, moved, w_exp_in, w_exp_out, b_in_own, b_out_own,
+                                 w_router.astype(BF16), other, tp_size, ep_size, sum(pieces[:4], []), pieces[4], 3)
         outputs = outputs.reshape(own_experts * ep_size, capacity, width)
-        choice = choice.transpose(1, 0, 2).reshape(-1)
-        token_of = jnp.where(choice == 2 * tokens, tokens, source.transpose(1, 0, 2).reshape(-1))
-        gate_at = jnp.where(choice == 2 * tokens, 0, choice)
-        gates = gates.reshape(-1)
-        partial = combine(8 * token_of, gate_at, gates, outputs, tokens)
-        summed = lax.psum_scatter(partial, 'tp', scatter_dimension=0, tiled=True)
-        result = (hidden.astype(F32) + summed.astype(F32)).astype(BF16)
-        return gather_tp(result, tiled=True).reshape(rows, seq, width)
+        partial = combine(place, gates, outputs, tokens)
+        return finish(partial, hidden, tp_size, 5).reshape(rows, seq, width)
 
     in_specs = (P(('dp', 'ep'), None, None), P(('dp', 'ep')), P(('dp', 'ep'), None, None), P(), P(), P(None, None, 'tp', None), P(None, 'tp', None), P(None, None, 'tp', None), P(None, None, 'tp', None), P(None, 'tp', None), P(None, 'tp', None, None), P(), P(None, 'tp'), P('tp'), P('tp', None), P(), P(), P('ep', None, 'tp'), P('ep', 'tp'), P('ep', 'tp', None), P('ep', None))
     return jax.shard_map(local_fn, mesh=mesh, in_specs=in_specs, out_specs=P(('dp', 'ep'), None, None), check_vma=False)

time: 977 us -> 941 us (0.963)
  waiting for transfers between devices: 276 us -> 39.7 us
  Pallas kernels: 504 us -> 707 us
    pallas_call x0 -> x1, Pallas kernels: none -> 205 us  [finish(): pl.pallas_call(functools.partial(finish_body, tp_size, count), out_shape=...]
    all_gather x3 -> x2, waiting for transfers between devices: 164 us -> 37.6 us  [gather_tp(): return lax.all_gather(value, 'tp', axis=axis, tiled=tiled)]
    reduce_scatter x1 -> x0, waiting for transfers between devices: 110 us -> none  [local_fn(): summed = lax.psum_scatter(partial, 'tp', scatter_dimension=0, tiled=True)]
  transfers between devices with their start and end apart: 8 -> 6, of which waited for: 4 -> 2; matrix products, arithmetic and copies ran while one was open for 11% -> 12% of each run, Pallas kernels for 14% -> 14%
where the time goes in v3:
time: 941 us; the launch traced here: 936 us
  Pallas kernels  707 us (75%)
  local copies, waits for them, and re-layouts  137 us (15%)
  waiting for transfers between devices  39.7 us (4%)
  other arithmetic  25 us (3%)
  between operations  14.4 us (2%)
  blocking collectives  12.4 us (1%)
    pallas_call x2, Pallas kernels, attention_layer(): pl.pallas_call(functools.partial(attention_body, tp_size, pieces, head_di...  213 us
    pallas_call x1, Pallas kernels, finish(): pl.pallas_call(functools.partial(finish_body, tp_size, count), out_shape=...  205 us
    pallas_call x1, Pallas kernels, experts(): pl.pallas_call(body, out_shape=(jax.ShapeDtypeStruct(dispatch.shape, BF16...  166 us
    scatter x2, local copies, waits for them, and re-layouts, route(): choice.at[dest_first].set(ids + tokens * second).at[dest_second]  60.9 us
    pallas_call x1, Pallas kernels, dense_layer(): pl.pallas_call(functools.partial(dense_body, tp_size, pieces, 4), out_sha...  57.8 us
    all_gather x2, waiting for transfers between devices, gather_tp(): return lax.all_gather(value, 'tp', axis=axis, tiled=tiled)  37.6 us
    pallas_call x1, Pallas kernels, combine(): pl.pallas_call(functools.partial(combine_body, blocks), out_shape=jax.Sha...  36.6 us
    pallas_call x1, Pallas kernels, move(): pl.pallas_call(functools.partial(move_body, tp_size, pieces), out_shape=l...  28.3 us
  transfers between devices with their start and end apart: 6, of which 2 were waited for; matrix products, arithmetic and copies ran while one was open for 12% of the time, Pallas kernels for 14%

profile of v3, /device:TPU:97, one launch (start us, length us, event | category | flops | bytes accessed | tf_op | source)
XLA Modules:
  0.0 936.5 jit_solution(18224694824490490231)
XLA Ops:
  6.6 1.2 fusion.36
  7.7 1.1 fusion.35
  8.9 1.1 fusion.34
  10.0 1.1 fusion.33
  11.1 0.7 constant_dynamic-slice_fusion.3
  11.8 1.1 constant_dynamic-slice_fusion.4
  13.5 1.8 pad_maximum_fusion
  15.6 12.4 %all-gather.6 = f32[4,1,13824]{2,1,0:T(1,128)S(1)} all-gather(f32[1,1,13824]{2,1,0:T(1,128)S(1)} %reshape.397), channel_id=3, replica_groups=mesh['dp'=1,'tp'=4,'ep'=8] {'tp'}, dimensions={0}, use_global_device_ids=true | all-gather | bytes 276480 | tf_op jit(solution)/shard_map/all_gather | solution.py:543
  28.1 3.9 constant_dynamic-slice_fusion.2
  32.1 17.2 %all-gather.16.cloned.1.call-done = bf16[1536,768]{1,0:T(8,128)(2,1)} async-done(((bf16[384,768]{1,0:T(8,128)(2,1)}), bf16[1536,768]{1,0:T(8,128)(2,1)}) %all-gather.16.cloned.1.call-update) | async-done | bytes 2359312 | tf_op jit(solution)/shard_map/all_gather | solution.py:543
  49.2 3.0 fusion.32
  52.4 0.7 all-gather.18.cloned.1.call-update
  53.8 0.6 all-gather.24.cloned.1.call-update
  55.4 1.3 slice_bitcast_fusion.2.after_ref
  56.8 28.3 %move.1.after_ref.refs_0_ = bf16[3,384,768]{2,1,0:T(8,128)(2,1)} custom-call(bf16[16,768,768]{2,1,0:T(8,128)(2,1)} %refs_6_.1, bf16[16,768,768]{2,1,0:T(8,128)(2,1)} %refs_7_.1, bf16[8,768]{1,0:T(8,128)(2,1)} %slice_bitcast_fusion.2.after_ref), custom_call_target="tpu_custom_call" | custom-call | flops 20000000000 | bytes 10000000 | tf_op jit(solution)/shard_map/move/pallas_call | solution.py:75
  85.1 2.7 copy.99
  87.9 2.0 slice.169
  90.0 107.1 %attention_layer.2 = (bf16[2048,768]{1,0:T(8,128)(2,1)}, bf16[2048,768]{1,0:T(8,128)(2,1)}, bf16[3,768,768]{2,1,0:T(8,128)(2,1)}, bf16[3,768,768]{2,1,0:T(8,128)(2,1)}) custom-call(s32[2]{0:T(128)S(1)} %dynamic_slice.31.lens_ref, bf16[2048,768]{1,0:T(8,128)(2,1)} %bitcast.115, f32[1,768]{1,0:T(1,128)S(1)} %get-tuple-element.80.gain_ref, ...), custom_call_target="tpu_custom_call" | custom-call | flops 30000001024 | bytes 40000000 | tf_op jit(solution)/shard_map/attention_layer/pallas_call | solution.py:150
  197.2 2.2 slice.172
  199.4 1.3 slice.174
  200.8 2.1 copy.79
  203.0 57.8 %dense_layer.1 = (bf16[2048,768]{1,0:T(8,128)(2,1)}, bf16[3,768,768]{2,1,0:T(8,128)(2,1)}) custom-call(bf16[2048,768]{1,0:T(8,128)(2,1)} %get-tuple-element.26.x_ref, bf16[2048,768]{1,0:T(8,128)(2,1)} %get-tuple-element.27.normed_ref, bf16[3072,768]{1,0:T(8,128)(2,1)} %bitcast.153, f32[1,3072]{1,0:T(1,128)S(1)} %reshape_reshape.10.b_in_ref, ...), custom_call_target="tpu_custom_call" | custom-call | flops 20000000000 | bytes 30000000 | tf_op jit(solution)/shard_map/dense_layer/pallas_call | solution.py:193
  260.8 106.1 %attention_layer.3 = (bf16[2048,768]{1,0:T(8,128)(2,1)}, bf16[2048,768]{1,0:T(8,128)(2,1)}, bf16[3,768,768]{2,1,0:T(8,128)(2,1)}, bf16[3,768,768]{2,1,0:T(8,128)(2,1)}) custom-call(s32[2]{0:T(128)S(1)} %dynamic_slice.31.lens_ref, bf16[2048,768]{1,0:T(8,128)(2,1)} %get-tuple-element.28.x_ref, f32[1,768]{1,0:T(1,128)S(1)} %get-tuple-element.79.gain_ref, ...), custom_call_target="tpu_custom_call" | custom-call | flops 30000001024 | bytes 40000000 | tf_op jit(solution)/shard_map/attention_layer/pallas_call | solution.py:150
  367.5 2.2 fusion.2
  369.7 2.0 copy-done.3
  371.8 2.7 add_add_fusion
  374.5 4.4 copy.70
  379.2 2.2 fusion.4
  381.4 1.9 copy-done.2
  383.4 2.7 add_add_fusion.1
  386.1 2.4 copy.68
  388.6 4.3 convert_reduce_fusion
  393.0 4.3 fusion.1
  397.5 30.5 %scatter_custom_fusion = s32[16385]{0:T(1024)S(1)} fusion(s32[8192]{0:T(1024)S(1)} %bitcast.149, s32[8192]{0:T(1024)S(1)} %multiply_add_fusion.1, s32[]{:T(128)} %constant.22.clone.1), kind=kCustom, calls=%fused_computation.58 | custom fusion | bytes 65544 | tf_op jit(solution)/shard_map/scatter | solution.py:534
  428.0 30.5 %scatter_fusion = s32[16385]{0:T(1024)S(1)} fusion(s32[16385]{0:T(1024)S(1)} %scatter_custom_fusion, s32[8192]{0:T(1024)S(1)} %bitcast.137, s32[8192]{0:T(1024)S(1)} %multiply_add_fusion), kind=kCustom, calls=%fused_computation.3 | custom fusion | bytes 131072 | tf_op jit(solution)/shard_map/scatter | solution.py:534
  458.5 0.6 copy.81
  459.2 0.6 copy.104
  459.8 0.7 convert_element_type.18.refs_10_
  460.6 0.6 fusion.28.token_ref
  461.2 2.4 negate_select_fusion
  463.9 0.6 gather_fusion.1
  464.4 0.6 copy.102
  465.1 20.5 %all-gather.14.cloned.1.call-done = bf16[8192,768]{1,0:T(8,128)(2,1)} async-done(((bf16[2048,768]{1,0:T(8,128)(2,1)}), bf16[8192,768]{1,0:T(8,128)(2,1)}) %all-gather.14.cloned.1.call-update) | async-done | bytes 12582928 | tf_op jit(solution)/shard_map/all_gather | solution.py:543
  485.5 25.2 %gather_fusion = bf16[4096,768]{1,0:T(8,128)(2,1)} fusion(bf16[8192,768]{1,0:T(8,128)(2,1)} %all-gather.14.cloned.1.call-done, s32[4096]{0:T(1024)S(1)} %broadcast_clamp_fusion), kind=kCustom, calls=%fused_computation | custom fusion | bytes 12599296 | tf_op jit(solution)/shard_map/gather | solution.py:630
  510.8 166.2 %experts.1 = (bf16[4,8,128,768]{3,2,1,0:T(8,128)(2,1)}, f32[4096,1]{1,0:T(8,128)}) custom-call(bf16[4,8,128,768]{3,2,1,0:T(8,128)(2,1)} %bitcast.109, bf16[3,384,768]{2,1,0:T(8,128)(2,1)} %move.1.after_ref.refs_0_, bf16[3,768,768]{2,1,0:T(8,128)(2,1)} %get-tuple-element.31.refs_1_, bf16[3,768,768]{2,1,0:T(8,128)(2,1)} %get-tuple-element.32.refs_2_, ...), custom_call_target="tpu_custom_call" | custom-call | flops 38654705664 | bytes 60000000 | tf_op jit(solution)/shard_map/experts/pallas_call | solution.py:348
  677.0 36.6 %combine.1.partial_ref = bf16[8192,768]{1,0:T(8,128)(2,1)} custom-call(s32[4096]{0:T(1024)} %fusion.28.token_ref, bf16[32,128,768]{2,1,0:T(8,128)(2,1)} %bitcast.155, f32[4096,1]{1,0:T(8,128)} %get-tuple-element.37.gates_ref), custom_call_target="tpu_custom_call" | custom-call | flops 15000000512 | bytes 18874368 | tf_op jit(solution)/shard_map/combine/pallas_call | solution.py:405
  713.6 205.2 %finish.1 = bf16[8192,768]{1,0:T(8,128)(2,1)} custom-call(bf16[8192,768]{1,0:T(8,128)(2,1)} %combine.1.partial_ref, bf16[2048,768]{1,0:T(8,128)(2,1)} %get-tuple-element.38.hidden_ref), custom_call_target="tpu_custom_call" | custom-call | flops 99999997952 | bytes 60000000 | tf_op jit(solution)/shard_map/finish/pallas_call | solution.py:508
  918.8 10.6 %copy.107 = bf16[8,1024,768]{2,1,0:T(8,128)(2,1)} copy(bf16[8,1024,768]{2,1,0:T(8,128)(2,1)} %bitcast.108) | data formatting | bytes 25165824
  (114 shorter events, 4.6 us)
Async XLA Ops:
  6.5 4.5 copy-start
  6.6 42.7 %all-gather.16.cloned.1.call-start = ((), (), s32[]{:S(2)}) async-start(), calls=%async_computation.1 | async-start | bytes 2949120 | tf_op jit(solution)/shard_map/all_gather | solution.py:543
  8.8 6.6 copy-start.16
  8.8 6.6 copy-start.17
  8.9 6.7 copy-start.14
  11.8 3.6 copy-start.9
  15.3 69.8 %all-gather.20.cloned.1.call-start = ((), (), s32[]{:S(2)}) async-start(), calls=%async_computation.3 | async-start | bytes 5308416 | tf_op jit(solution)/shard_map/all_gather | solution.py:582
  28.1 26.7 %copy-start.5 = (f32[4,1,13824]{2,0,1:T(4,128)}, f32[4,1,13824]{2,0,1:T(4,128)S(1)}, u32[]{:S(2)}) copy-start(f32[4,1,13824]{2,0,1:T(4,128)S(1)} %copy.100) | copy-start | bytes 663556
  32.0 22.6 %copy-start.18 = (s32[8]{0:T(128)S(1)}, s32[8]{0:T(128)}, u32[]{:S(2)}) copy-start(s32[8]{0:T(128)} %param.22) | copy-start | bytes 100
  32.0 22.7 %copy-start.15 = (f32[768]{0:T(1024)S(1)}, f32[768]{0:T(1024)}, u32[]{:S(2)}) copy-start(f32[768]{0:T(1024)} %param.36) | copy-start | bytes 9220
  32.0 22.7 %copy-start.13 = (f32[2,768]{1,0:T(2,128)S(1)}, f32[2,768]{1,0:T(2,128)}, u32[]{:S(2)}) copy-start(f32[2,768]{1,0:T(2,128)} %param.32) | copy-start | bytes 18436
  32.0 22.7 %copy-start.11 = (f32[4,768]{1,0:T(4,128)S(1)}, f32[4,768]{1,0:T(4,128)}, u32[]{:S(2)}) copy-start(f32[4,768]{1,0:T(4,128)} %param.25) | copy-start | bytes 36868
  32.1 22.7 %copy-start.12 = (f32[4,768]{1,0:T(4,128)S(1)}, f32[4,768]{1,0:T(4,128)}, u32[]{:S(2)}) copy-start(f32[4,768]{1,0:T(4,128)} %param.24) | copy-start | bytes 36868
  52.3 144.8 %all-gather.18.cloned.1.call-start = ((), (), s32[]{:S(2)}) async-start(), calls=%async_computation.2 | async-start | bytes 5308416 | tf_op jit(solution)/shard_map/all_gather | solution.py:583
  53.1 149.8 %all-gather.22.cloned.1.call-start = ((), (), s32[]{:S(2)}) async-start(), calls=%async_computation.4 | async-start | bytes 5308416 | tf_op jit(solution)/shard_map/all_gather | solution.py:583
  53.8 149.2 %all-gather.24.cloned.1.call-start = ((), (), s32[]{:S(2)}) async-start(), calls=%async_computation.5 | async-start | bytes 5308416 | tf_op jit(solution)/shard_map/all_gather | solution.py:583
  54.4 431.1 %all-gather.14.cloned.1.call-start = ((), (), s32[]{:S(2)}) async-start(), calls=%async_computation | async-start | bytes 15728640 | tf_op jit(solution)/shard_map/all_gather | solution.py:543
  260.8 106.1 %copy-start.8 = (s32[8,1024,2]{1,2,0:T(2,128)S(1)}, s32[8,1024,2]{1,2,0:T(2,128)}, u32[]{:S(2)}) copy-start(s32[8,1024,2]{1,2,0:T(2,128)} %param.23) | copy-start | bytes 196612
  369.7 2.0 copy-start.3
  381.4 1.9 copy-start.2
  388.6 4.4 copy-start.4
  428.0 31.2 %copy-start.10 = (f32[16,768]{1,0:T(8,128)S(1)}, f32[16,768]{1,0:T(8,128)}, u32[]{:S(2)}) copy-start(f32[16,768]{1,0:T(8,128)} %param.41) | copy-start | bytes 147460
  428.0 31.9 %copy-start.7 = (f32[768,128]{1,0:T(8,128)S(1)}, f32[768,128]{1,0:T(8,128)}, u32[]{:S(2)}) copy-start(f32[768,128]{1,0:T(8,128)} %param.37) | copy-start | bytes 1179652
  458.5 5.1 copy-start.6
  918.8 10.6 %copy-start.1 = (bf16[768,768]{1,0:T(8,128)(2,1)S(1)}, bf16[768,768]{1,0:T(8,128)(2,1)}, u32[]{:S(2)}) copy-start(bf16[768,768]{1,0:T(8,128)(2,1)} %param.35) | copy-start | bytes 3538948
Sparse Core Ops, SparseCore 0:
  15.4 33.7 all-gather.15
  52.4 32.1 all-gather.19
  86.2 31.4 all-gather.17
  119.1 31.4 all-gather.21
  152.1 31.4 all-gather.23
  367.0 118.4 all-gather.13

commit v4 on v3

--- a/solution.py
+++ b/solution.py
@@ -13,11 +13,27 @@
 LOG2E = 1.4426950408889634
 
 
+MESH = pl.DeviceIdType.MESH
+VMEM_SPEC = pl.BlockSpec(memory_space=pltpu.VMEM)
+HBM_SPEC = pl.BlockSpec(memory_space=pltpu.HBM)
+SMEM_SPEC = pl.BlockSpec(memory_space=pltpu.SMEM)
+DMA = pltpu.SemaphoreType.DMA
+
+
+def span(index, size):
+    return pl.ds(pl.multiple_of(index * size, size), size)
+
+
+def settings(call_id=None, mib=56, grid=None):
+    return pltpu.CompilerParams(dimension_semantics=grid, collective_id=call_id, has_side_effects=call_id is not None, vmem_limit_bytes=mib << 20)
+
+
+def cost(gflops):
+    return pl.CostEstimate(flops=gflops * 10**9, transcendentals=0, bytes_accessed=10**7)
+
+
 def dot_t(lhs, rhs_t):
     return lax.dot_general(lhs, rhs_t, (((1,), (1,)), ((), ())), preferred_element_type=F32)
-
-
-HBM = pltpu.HBM
 
 
 def norm_rows(value, gain, shift):
@@ -35,7 +51,7 @@
     count = 0
     for axis, size in groups:
         for distance in range(1, size):
-            pl.semaphore_signal(barrier, inc=1, device_id={axis: away(axis, size, distance)}, device_id_type=pl.DeviceIdType.MESH)
+            pl.semaphore_signal(barrier, device_id={axis: away(axis, size, distance)}, device_id_type=MESH)
             count += 1
     pl.semaphore_wait(barrier, count)
 
@@ -45,7 +61,7 @@
     return [pltpu.make_async_remote_copy(
         src_ref=weights[which].at[chunk * tp_size + away('tp', tp_size, distance), pl.ds(start, rows)], dst_ref=landing_ref.at[distance - 1],
         send_sem=send_sem.at[distance - 1], recv_sem=recv_sem.at[distance - 1],
-        device_id={'tp': away('tp', tp_size, distance)}, device_id_type=pl.DeviceIdType.MESH)
+        device_id={'tp': away('tp', tp_size, distance)}, device_id_type=MESH)
         for distance in sorted(range(1, tp_size), key=lambda d: (min(d, tp_size - d), d))]
 
 
@@ -60,24 +76,178 @@
     return [jax.ShapeDtypeStruct((tp_size - 1, rows, weight.shape[2]), BF16) for _, _, _, rows in pieces]
 
 
-def move_body(tp_size, pieces, w_in_ref, w_out_ref, after_ref, *rest):
-    copies = exchange_all(tp_size, (w_in_ref, w_out_ref), pieces, rest[:len(pieces)], *rest[len(pieces):])
+def route_tables(lens_ref, index_ref, total_ref, total_t_ref):
+    rows, _, seq = index_ref.shape
+    step = min(512, seq)
+    per_row = seq // step
+    experts_count, wide = total_ref.shape
+    slots = wide // 3
+    ids = lax.broadcasted_iota(jnp.int32, (experts_count, 1), 0)
+    slot_ids = lax.broadcasted_iota(jnp.int32, (slots, 1), 0)
+    before = (lax.broadcasted_iota(jnp.int32, (step, step), 0) < lax.broadcasted_iota(jnp.int32, (step, step), 1)).astype(BF16)
+    total_ref[...] = jnp.zeros_like(total_ref)
+    total_t_ref[...] = jnp.zeros_like(total_t_ref)
+    count = jnp.zeros((experts_count, 1), F32)
+    for choice in range(2):
+        def block(index, count):
+            row = index // per_row
+            start = pl.multiple_of((index % per_row) * step, step)
+            cols = pl.ds(start, step)
+            position = lax.broadcasted_iota(jnp.int32, (1, step), 1) + start
+            chosen = jnp.where(position < lens_ref[row], index_ref[row, pl.ds(choice, 1), cols], -1)
+            other = index_ref[row, pl.ds(1 - choice, 1), cols]
+            token = position + row * seq
+            hot = jnp.where(ids == chosen, 1.0, 0.0)
+            rank = jnp.dot(hot.astype(BF16), before, preferred_element_type=F32) + count
+            slot = jnp.sum(rank * hot, axis=0, keepdims=True).astype(jnp.int32)
+            at_slot = slot_ids == slot
+            parts = [jnp.where(at_slot, value.astype(F32), 0.0).astype(BF16) for value in (token & 255, (token >> 8) + 1, other)]
+            values = jnp.concatenate(parts, axis=0)
+            hot16 = hot.astype(BF16)
+            total_ref[...] += dot_t(hot16, values)
+            total_t_ref[...] += dot_t(values, hot16)
+            return count + jnp.sum(hot, axis=1, keepdims=True)
+
+        count = lax.fori_loop(0, rows * per_row, block, count)
+
+
+def move_body(tp_size, ep_size, pieces, own_experts, lens_ref, index_ref, w_in_ref, w_out_ref, after_ref, place_ref, source_ref, other_ref, *rest):
+    moved_refs = rest[:len(pieces)]
+    total_ref, total_t_ref, send_sem, recv_sem = rest[len(pieces):]
+    copies = exchange_all(tp_size, (w_in_ref, w_out_ref), pieces, moved_refs, send_sem, recv_sem)
     enter([('tp', tp_size)])
     for copy in copies:
         copy.start()
+    route_tables(lens_ref, index_ref, total_ref, total_t_ref)
+    rows, _, seq = index_ref.shape
+    experts_count, wide = total_ref.shape
+    slots = wide // 3
+    lane = lax.broadcasted_iota(jnp.int32, (1, experts_count), 1)
+
+    def take(index, carry):
+        chunk = index // ep_size
+        expert = (index % ep_size) * (own_experts * tp_size) + chunk * tp_size + lax.axis_index('tp')
+        line = total_ref[pl.ds(expert, 1), :].astype(jnp.int32)
+        low, high = line[:, :slots], line[:, slots:2 * slots]
+        place_ref[pl.ds(index, 1), :] = 8 * jnp.where(high > 0, 256 * (high - 1) + low, rows * seq)
+        column = jnp.sum(jnp.where(lane == expert, total_t_ref[...], 0.0), axis=1, keepdims=True).astype(jnp.int32)
+        low, high, other = column[:slots], column[slots:2 * slots], column[2 * slots:]
+        at = span(index, slots)
+        source_ref[at, :] = jnp.where(high > 0, 256 * (high - 1) + low, -1)
+        other_ref[at, :] = other
+        return carry
+
+    lax.fori_loop(0, own_experts * ep_size, take, 0)
     for copy in copies:
         copy.wait()
 
 
-def move(w_in, w_out, after, tp_size, pieces, call_id):
-    hbm = pl.BlockSpec(memory_space=HBM)
-    dma = pltpu.SemaphoreType.DMA((len(pieces), tp_size - 1))
+def move(lens, index, w_in, w_out, after, num_experts, capacity, tp_size, ep_size, pieces, call_id):
+    own_experts = w_in.shape[0] // tp_size
+    blocks = own_experts * ep_size
+    dma = DMA((len(pieces), tp_size - 1))
+    column = jax.ShapeDtypeStruct((blocks * capacity, 1), jnp.int32)
     return pl.pallas_call(
-        functools.partial(move_body, tp_size, pieces), out_shape=landings(tp_size, w_in, pieces),
-        in_specs=[hbm, hbm, hbm], out_specs=[hbm for _ in pieces], scratch_shapes=[dma, dma],
-        compiler_params=pltpu.CompilerParams(collective_id=call_id, has_side_effects=True, vmem_limit_bytes=56 * 1024 * 1024),
-        cost_estimate=pl.CostEstimate(flops=20_000_000_000, transcendentals=0, bytes_accessed=10_000_000),
-        name='move')(w_in, w_out, after)
+        functools.partial(move_body, tp_size, ep_size, pieces, own_experts),
+        out_shape=(jax.ShapeDtypeStruct((blocks, capacity), jnp.int32), column, column, *landings(tp_size, w_in, pieces)),
+        in_specs=[SMEM_SPEC, VMEM_SPEC, HBM_SPEC, HBM_SPEC, HBM_SPEC], out_specs=(VMEM_SPEC, VMEM_SPEC, VMEM_SPEC, *[HBM_SPEC for _ in pieces]),
+        scratch_shapes=[pltpu.VMEM((num_experts, 3 * capacity), F32), pltpu.VMEM((3 * capacity, num_experts), F32), dma, dma],
+        compiler_params=settings(call_id),
+        cost_estimate=cost(30),
+        name='move')(lens, index, w_in, w_out, after)
+
+
+def dispatch_body(tp_size, source_ref, normed_ref, o_ref, all_buf, acc_ref, load_sem, send_sem, recv_sem):
+    me = lax.axis_index('tp')
+    _, count, size, width = normed_ref.shape
+    own_tokens = 2 * count * size
+    slots = source_ref.shape[0]
+    block = min(512, slots)
+    hops = tp_size - 1
+    step_to = (1, tp_size - 1)
+    lane = lax.broadcasted_iota(jnp.int32, (1, size), 1)
+
+    def behind(way, distance):
+        return away('tp', tp_size, (tp_size - distance) % tp_size if way == 0 else distance % tp_size)
+
+    def send(way, hop, index, src_ref, chunk):
+        return pltpu.make_async_remote_copy(
+            src_ref=src_ref, dst_ref=all_buf.at[chunk, way, index], send_sem=send_sem.at[way, hop, index], recv_sem=recv_sem.at[way, hop, index],
+            device_id={'tp': away('tp', tp_size, step_to[way])}, device_id_type=MESH)
+
+    load = pltpu.make_async_copy(normed_ref, all_buf.at[me], load_sem)
+    load.start()
+    enter([('tp', tp_size)])
+
+    def first(index, carry):
+        for way in range(2):
+            send(way, 0, index, normed_ref.at[way, index], me).start()
+        return carry
+
+    lax.fori_loop(0, count, first, 0)
+    load.wait()
+
+    def place(index, chunks, fresh):
+        def some(part, carry):
+            at = span(part, block)
+            total = None if fresh else acc_ref[at, :]
+            for way in range(2):
+                base = chunks[way] * own_tokens + (way * count + index) * size
+                hot = jnp.where(source_ref[at, :] == lane + base, 1.0, 0.0).astype(BF16)
+                part_sum = jnp.dot(hot, all_buf[chunks[way], way, index], preferred_element_type=F32)
+                total = part_sum if total is None else total + part_sum
+            acc_ref[at, :] = total
+            return carry
+
+        lax.fori_loop(0, slots // block, some, 0)
+
+    place(0, (me, me), True)
+
+    def own(index, carry):
+        place(index, (me, me), False)
+        return carry
+
+    lax.fori_loop(1, count, own, 0)
+    for hop in range(1, tp_size):
+        def arrive(index, carry):
+            chunks = [behind(way, hop) for way in range(2)]
+            for way in range(2):
+                arrived = all_buf.at[chunks[way], way, index]
+                send(way, hop - 1, index, arrived, chunks[way]).wait_recv()
+                if hop < hops:
+                    send(way, hop, index, arrived, chunks[way]).start()
+            place(index, chunks, False)
+            return carry
+
+        lax.fori_loop(0, count, arrive, 0)
+
+    def finish_rows(part, carry):
+        at = span(part, block)
+        o_ref[at, :] = acc_ref[at, :].astype(BF16)
+        return carry
+
+    lax.fori_loop(0, slots // block, finish_rows, 0)
+
+    def drain(index, carry):
+        for way in range(2):
+            for hop in range(hops):
+                send(way, hop, index, normed_ref.at[way, index], me).wait_send()
+        return carry
+
+    lax.fori_loop(0, count, drain, 0)
+
+
+def dispatch_rows(source, normed, tp_size, call_id):
+    tokens, width = normed.shape
+    size = min(256, tokens // 2)
+    count = tokens // (2 * size)
+    slots = source.shape[0]
+    return pl.pallas_call(
+        functools.partial(dispatch_body, tp_size), out_shape=jax.ShapeDtypeStruct((slots, width), BF16), in_specs=[VMEM_SPEC, HBM_SPEC], out_specs=VMEM_SPEC,
+        scratch_shapes=[pltpu.VMEM((tp_size, 2, count, size, width), BF16), pltpu.VMEM((slots, width), F32), DMA, DMA((2, tp_size - 1, count)), DMA((2, tp_size - 1, count))],
+        compiler_params=settings(call_id),
+        cost_estimate=cost(30),
+        name='dispatch_rows')(source, normed.reshape(2, count, size, width))
 
 
 def attention_body(tp_size, pieces, head_dim, block_q, lens_ref, x_ref, gain_ref, shift_ref, w_qkv_ref, b_qkv_ref, w_out_ref, b_out_ref, gain2_ref, shift2_ref, w_in_ref, w_exp_out_ref, after_ref,
@@ -98,7 +268,7 @@
     @pl.when(block == 0)
     def _():
         def project(index, carry):
-            rows = pl.ds(pl.multiple_of(index * block_q, block_q), block_q)
+            rows = span(index, block_q)
             normed = norm_rows(x_ref[rows, :].astype(F32), gain_ref[...], shift_ref[...]).astype(BF16)
             qkv_ref[rows, :] = (dot_t(normed, w_qkv_ref[...]) + b_qkv_ref[...]).astype(BF16)
             return carry
@@ -109,7 +279,7 @@
     key_ok = lax.broadcasted_iota(jnp.int32, (1, seq), 1) < length
     lane_head = lax.broadcasted_iota(jnp.int32, (1, pair), 1) // head_dim
     factor = (head_dim ** -0.5) * LOG2E
-    rows = pl.ds(pl.multiple_of(block * block_q, block_q), block_q)
+    rows = span(block, block_q)
 
     def heads(index, carry):
         lanes = pl.multiple_of(index * pair, pair)
@@ -146,17 +316,16 @@
     blocks = seq // block_q
     fixed = lambda shape: pl.BlockSpec(shape, lambda r, q: (0,) * len(shape), pipeline_mode=pl.Buffered(1))
     moved = landings(tp_size, w_exp_in, pieces)
-    hbm = pl.BlockSpec(memory_space=HBM)
     return pl.pallas_call(
         functools.partial(attention_body, tp_size, pieces, head_dim, block_q),
         out_shape=(jax.ShapeDtypeStruct((tokens, width), BF16), jax.ShapeDtypeStruct((tokens, width), BF16), *moved),
         grid=(tokens // seq, blocks),
-        in_specs=[pl.BlockSpec(memory_space=pltpu.SMEM), pl.BlockSpec((seq, width), lambda r, q: (r, 0)), fixed((1, width)), fixed((1, width)),
-                  fixed(w_qkv.shape), fixed((1, 3 * width)), fixed(w_out.shape), fixed((1, width)), fixed((1, width)), fixed((1, width)), hbm, hbm, hbm],
-        out_specs=(pl.BlockSpec((block_q, width), lambda r, q: (r * blocks + q, 0)), pl.BlockSpec((block_q, width), lambda r, q: (r * blocks + q, 0)), *[hbm for _ in pieces]),
-        scratch_shapes=[pltpu.VMEM((seq, 3 * width), BF16), pltpu.VMEM((block_q, width), BF16), pltpu.SemaphoreType.DMA((len(pieces), tp_size - 1)), pltpu.SemaphoreType.DMA((len(pieces), tp_size - 1))],
-        compiler_params=pltpu.CompilerParams(dimension_semantics=('arbitrary', 'arbitrary'), collective_id=call_id, has_side_effects=True, vmem_limit_bytes=52 * 1024 * 1024),
-        cost_estimate=pl.CostEstimate(flops=30_000_000_000, transcendentals=0, bytes_accessed=40_000_000),
+        in_specs=[SMEM_SPEC, pl.BlockSpec((seq, width), lambda r, q: (r, 0)), fixed((1, width)), fixed((1, width)),
+                  fixed(w_qkv.shape), fixed((1, 3 * width)), fixed(w_out.shape), fixed((1, width)), fixed((1, width)), fixed((1, width)), HBM_SPEC, HBM_SPEC, HBM_SPEC],
+        out_specs=(pl.BlockSpec((block_q, width), lambda r, q: (r * blocks + q, 0)), pl.BlockSpec((block_q, width), lambda r, q: (r * blocks + q, 0)), *[HBM_SPEC for _ in pieces]),
+        scratch_shapes=[pltpu.VMEM((seq, 3 * width), BF16), pltpu.VMEM((block_q, width), BF16), DMA((len(pieces), tp_size - 1)), DMA((len(pieces), tp_size - 1))],
+        compiler_params=settings(call_id, grid=('arbitrary', 'arbitrary')),
+        cost_estimate=cost(30),
         name='attention_layer')(lens, x, *norm, w_qkv, b_qkv, w_out, b_out, *norm2, w_exp_in, w_exp_out, after)
 
 
@@ -188,16 +357,15 @@
     tokens, width = x.shape
     block_n = min(256, tokens)
     fixed = lambda shape: pl.BlockSpec(shape, lambda i: (0,) * len(shape), pipeline_mode=pl.Buffered(1))
-    hbm = pl.BlockSpec(memory_space=HBM)
-    dma = pltpu.SemaphoreType.DMA((len(pieces), tp_size - 1))
+    dma = DMA((len(pieces), tp_size - 1))
     return pl.pallas_call(
         functools.partial(dense_body, tp_size, pieces, 4),
         out_shape=(jax.ShapeDtypeStruct((tokens, width), BF16), *landings(tp_size, w_exp_in, pieces)), grid=(tokens // block_n,),
-        in_specs=[pl.BlockSpec((block_n, width), lambda i: (i, 0)), pl.BlockSpec((block_n, width), lambda i: (i, 0)), fixed(w_in.shape), fixed(b_in.shape), fixed(w_out.shape), fixed((1, width)), hbm, hbm],
-        out_specs=(pl.BlockSpec((block_n, width), lambda i: (i, 0)), *[hbm for _ in pieces]),
+        in_specs=[pl.BlockSpec((block_n, width), lambda i: (i, 0)), pl.BlockSpec((block_n, width), lambda i: (i, 0)), fixed(w_in.shape), fixed(b_in.shape), fixed(w_out.shape), fixed((1, width)), HBM_SPEC, HBM_SPEC],
+        out_specs=(pl.BlockSpec((block_n, width), lambda i: (i, 0)), *[HBM_SPEC for _ in pieces]),
         scratch_shapes=[dma, dma],
-        compiler_params=pltpu.CompilerParams(dimension_semantics=('arbitrary',), collective_id=call_id, has_side_effects=True, vmem_limit_bytes=52 * 1024 * 1024),
-        cost_estimate=pl.CostEstimate(flops=20_000_000_000, transcendentals=0, bytes_accessed=30_000_000),
+        compiler_params=settings(call_id, grid=('arbitrary',)),
+        cost_estimate=cost(30),
         name='dense_layer')(x, normed, w_in, b_in, w_out, b_out, w_exp_in, w_exp_out)
 
 
@@ -215,7 +383,8 @@
             peer = away('ep', ep_size, distance)
             sends[chunk, distance] = pltpu.make_async_remote_copy(
                 src_ref=dispatch_ref.at[chunk, peer], dst_ref=arrived_ref.at[chunk, me], send_sem=send_sem.at[chunk, distance], recv_sem=recv_sem.at[chunk, distance],
-                device_id={'ep': peer}, device_id_type=pl.DeviceIdType.MESH)
+                device_id={'ep': peer}, device_id_type=MESH)
+
     def landing(piece):
         chunk, which, start, rows = piece
         return parts_buf.at[units.index((chunk, which)), :, pl.ds(start, rows)]
@@ -274,36 +443,52 @@
             def _():
                 pltpu.make_async_remote_copy(
                     src_ref=out_buf.at[slot, peer], dst_ref=returned_ref.at[chunk, me], send_sem=back_send.at[chunk, distance], recv_sem=back_recv.at[chunk, distance],
-                    device_id={'ep': peer}, device_id_type=pl.DeviceIdType.MESH).start()
+                    device_id={'ep': peer}, device_id_type=MESH).start()
+
+    def weights_here(unit):
+        owns[unit].wait()
+        for piece in early:
+            if piece[:2] == unit:
+                earlies[piece].wait()
+        for piece in late:
+            if piece[:2] == unit:
+                for copy in moves[piece]:
+                    copy.wait_recv()
+
+    def inner_part(chunk, index, part):
+        tokens = arrived_ref[chunk, pl.ds(2 * index, 2)].reshape(2 * slots, width)
+        inner = jnp.dot(tokens, part_ref((chunk, 0), part)[...], preferred_element_type=F32) + b_in_ref[chunk, pl.ds(part, 1), :]
+        return jnp.maximum(inner, 0.0).astype(BF16)
 
     backs = {}
     for chunk in range(chunks):
+        last = chunk == chunks - 1
         slot = chunk % out_buf.shape[0]
         for distance in range(1, ep_size):
             sends[chunk, distance].wait_recv()
         kept[chunk].wait()
-        for which in range(2):
-            unit = (chunk, which)
-            owns[unit].wait()
-            for piece in early:
-                if piece[:2] == unit:
-                    earlies[piece].wait()
-            for piece in late:
-                if piece[:2] == unit:
-                    for copy in moves[piece]:
-                        copy.wait_recv()
+        weights_here((chunk, 0))
         before = chunk - out_buf.shape[0]
         if before >= 0:
             for copy in backs[before][:-1]:
                 copy.wait_send()
             backs[before][-1].wait()
 
+        held = [sent_buf.at[0], sent_buf.at[1], arrived_ref.at[0], arrived_ref.at[1]]
+        if last:
+            def first_product(index, carry):
+                for part in range(tp_size):
+                    held[part][pl.ds(2 * index, 2)] = inner_part(chunk, index, part).reshape(2, slots, width)
+                return carry
+
+            lax.fori_loop(0, ep_size // 2, first_product, 0)
+        weights_here((chunk, 1))
+
         def rows(index, carry):
-            tokens = arrived_ref[chunk, pl.ds(2 * index, 2)].reshape(2 * slots, width)
             total = jnp.zeros((2 * slots, width), F32)
             for part in range(tp_size):
-                inner = jnp.dot(tokens, part_ref((chunk, 0), part)[...], preferred_element_type=F32) + b_in_ref[chunk, pl.ds(part, 1), :]
-                total += jnp.dot(jnp.maximum(inner, 0.0).astype(BF16), part_ref((chunk, 1), part)[...], preferred_element_type=F32)
+                inner = held[part][pl.ds(2 * index, 2)].reshape(2 * slots, width) if last else inner_part(chunk, index, part)
+                total += jnp.dot(inner, part_ref((chunk, 1), part)[...], preferred_element_type=F32)
             out_buf[slot, pl.ds(2 * index, 2)] = (total + b_out_ref[pl.ds(chunk, 1), :]).astype(BF16).reshape(2, slots, width)
 
             @pl.when(index > 0)
@@ -319,8 +504,9 @@
             peer = away('ep', ep_size, distance)
             backs[chunk].append(pltpu.make_async_remote_copy(
                 src_ref=out_buf.at[slot, peer], dst_ref=returned_ref.at[chunk, me], send_sem=back_send.at[chunk, distance], recv_sem=back_recv.at[chunk, distance],
-                device_id={'ep': peer}, device_id_type=pl.DeviceIdType.MESH))
+                device_id={'ep': peer}, device_id_type=MESH))
         backs[chunk].append(pltpu.make_async_copy(out_buf.at[slot, me], returned_ref.at[chunk, me], local_sem.at[4, chunk]))
+
     for chunk in range(chunks):
         for distance in range(1, ep_size):
             sends[chunk, distance].wait_send()
@@ -338,22 +524,19 @@
 def experts(dispatch, early_weights, w_in, w_out, b_in, b_out, w_router, other, tp_size, ep_size, early, late, call_id):
     chunks, _, slots, width = dispatch.shape
     hidden = w_in.shape[2]
-    hbm = pl.BlockSpec(memory_space=HBM)
-    vmem = pl.BlockSpec(memory_space=pltpu.VMEM)
 
     def body(dispatch_ref, *refs):
         experts_body(tp_size, ep_size, early, late, dispatch_ref, refs[:len(early)], *refs[len(early):])
 
-    dma = pltpu.SemaphoreType.DMA
     return pl.pallas_call(
         body, out_shape=(jax.ShapeDtypeStruct(dispatch.shape, BF16), jax.ShapeDtypeStruct(other.shape, F32)),
-        in_specs=[hbm] * (3 + len(early)) + [vmem] * 4, out_specs=(hbm, vmem),
+        in_specs=[HBM_SPEC] * (3 + len(early)) + [VMEM_SPEC] * 4, out_specs=(HBM_SPEC, VMEM_SPEC),
         scratch_shapes=[pltpu.VMEM((2,) + dispatch.shape[1:], BF16), pltpu.VMEM(dispatch.shape, BF16), pltpu.VMEM((2 * chunks, tp_size - 1, width, hidden), BF16),
                         pltpu.VMEM((chunks, 2, width, hidden), BF16), pltpu.VMEM((2, ep_size, slots, width), BF16),
-                        dma((6, max(chunks, len(early)))), dma((chunks, ep_size)), dma((chunks, ep_size)), dma((chunks, ep_size)), dma((chunks, ep_size)),
-                        dma((len(late), tp_size - 1)), dma((len(late), tp_size - 1))],
-        compiler_params=pltpu.CompilerParams(collective_id=call_id, has_side_effects=True, vmem_limit_bytes=62 * 1024 * 1024),
-        cost_estimate=pl.CostEstimate(flops=4 * chunks * ep_size * slots * width * hidden * tp_size, transcendentals=0, bytes_accessed=60_000_000),
+                        DMA((6, max(chunks, len(early)))), DMA((chunks, ep_size)), DMA((chunks, ep_size)), DMA((chunks, ep_size)), DMA((chunks, ep_size)),
+                        DMA((len(late), tp_size - 1)), DMA((len(late), tp_size - 1))],
+        compiler_params=settings(call_id, 62),
+        cost_estimate=cost(30),
         name='experts')(dispatch, *early_weights, w_in, w_out, b_in, b_out, w_router, other)
 
 
@@ -362,18 +545,23 @@
     slots, width = slots_ref.shape
     step = o_ref.shape[0]
     lanes = 128
+    piece = min(128, slots)
 
     @pl.when(block == 0)
     def _():
         def clear(index, carry):
-            acc_ref[pl.ds(pl.multiple_of(index * 256, 256), 256), :] = jnp.zeros((256, lanes), F32)
-            return carry
-        lax.fori_loop(0, acc_ref.shape[0] // 256, clear, 0)
+            acc_ref[span(index, lanes), :] = jnp.zeros((lanes, lanes), F32)
+            return carry
+        lax.fori_loop(0, acc_ref.shape[0] // lanes, clear, 0)
 
     @pl.when(block < blocks)
     def _():
-        for col in range(width // lanes):
-            wide_ref[pl.ds(col, slots, stride=8), :] = slots_ref[:, col * lanes:(col + 1) * lanes].astype(F32) * gates_ref[...]
+        def widen(index, carry):
+            rows = span(index, piece)
+            for col in range(width // lanes):
+                wide_ref[pl.ds(index * (piece * 8) + col, piece, stride=8), :] = slots_ref[rows, col * lanes:(col + 1) * lanes].astype(F32) * gates_ref[rows, :]
+            return carry
+        lax.fori_loop(0, slots // piece, widen, 0)
         base = block * slots
 
         def add(index, carry):
@@ -389,14 +577,23 @@
 
     @pl.when(block >= blocks)
     def _():
-        first = pl.multiple_of((block - blocks) * (step * 8), step * 8)
-        for col in range(width // lanes):
-            o_ref[:, col * lanes:(col + 1) * lanes] = acc_ref[pl.ds(first + col, step, stride=8), :].astype(BF16)
+        first = (block - blocks) * (step * 8)
+        some = min(256, step)
+
+        def write(index, carry):
+            rows = span(index, some)
+            for col in range(width // lanes):
+                o_ref[rows, col * lanes:(col + 1) * lanes] = acc_ref[pl.ds(first + index * (some * 8) + col, some, stride=8), :].astype(BF16)
+            return carry
+        lax.fori_loop(0, step // some, write, 0)
 
 
 def combine(place, gates, outputs, tokens):
-    blocks, slots, width = outputs.shape
-    step = min(512, tokens)
+    count, slots, width = outputs.shape
+    blocks = 4
+    slots = count * slots // blocks
+    outputs = outputs.reshape(blocks, slots, width)
+    step = tokens // 4
     grid_spec = pltpu.PrefetchScalarGridSpec(
         num_scalar_prefetch=1, grid=(blocks + tokens // step,),
         in_specs=[pl.BlockSpec((None, slots, width), lambda b, *_: (jnp.minimum(b, blocks - 1), 0, 0)), pl.BlockSpec((slots, 1), lambda b, *_: (jnp.minimum(b, blocks - 1), 0))],
@@ -405,8 +602,8 @@
     return pl.pallas_call(
         functools.partial(combine_body, blocks),
         out_shape=jax.ShapeDtypeStruct((tokens, width), BF16), grid_spec=grid_spec,
-        compiler_params=pltpu.CompilerParams(dimension_semantics=('arbitrary',), vmem_limit_bytes=56 * 1024 * 1024),
-        cost_estimate=pl.CostEstimate(flops=15_000_000_000, transcendentals=0, bytes_accessed=2 * tokens * width + 2 * blocks * slots * width),
+        compiler_params=settings(grid=('arbitrary',)),
+        cost_estimate=cost(30),
         name='combine')(place, outputs, gates)
 
 
@@ -426,20 +623,17 @@
     def send_sum(way, hop, index, src_ref):
         return pltpu.make_async_remote_copy(
             src_ref=src_ref, dst_ref=sum_buf.at[way, hop, index], send_sem=sum_send.at[way, hop, index], recv_sem=sum_recv.at[way, hop, index],
-            device_id={'tp': away('tp', tp_size, step_to[way])}, device_id_type=pl.DeviceIdType.MESH)
+            device_id={'tp': away('tp', tp_size, step_to[way])}, device_id_type=MESH)
 
     def send_out(way, hop, index, src_ref, chunk):
         return pltpu.make_async_remote_copy(
             src_ref=src_ref, dst_ref=o_ref.at[rows(way, chunk, index)], send_sem=out_send.at[way, hop, index], recv_sem=out_recv.at[way, hop, index],
-            device_id={'tp': away('tp', tp_size, step_to[way])}, device_id_type=pl.DeviceIdType.MESH)
+            device_id={'tp': away('tp', tp_size, step_to[way])}, device_id_type=MESH)
 
     loads = [pltpu.make_async_copy(partial_ref, partial_buf, load_sem.at[0]), pltpu.make_async_copy(hidden_ref, hidden_buf, load_sem.at[1])]
     for load in loads:
         load.start()
-    barrier = pltpu.get_barrier_semaphore()
-    for distance in step_to:
-        pl.semaphore_signal(barrier, inc=1, device_id={'tp': away('tp', tp_size, distance)}, device_id_type=pl.DeviceIdType.MESH)
-    pl.semaphore_wait(barrier, 2)
+    enter([('tp', tp_size)])
 
     def first(index, carry):
         for way in range(2):
@@ -503,44 +697,21 @@
     size = min(256, own_tokens // 2)
     count = own_tokens // (2 * size)
     hops = tp_size - 1
-    hbm = pl.BlockSpec(memory_space=HBM)
-    dma = pltpu.SemaphoreType.DMA
     return pl.pallas_call(
-        functools.partial(finish_body, tp_size, count), out_shape=jax.ShapeDtypeStruct(partial.shape, BF16), in_specs=[hbm, hbm], out_specs=hbm,
+        functools.partial(finish_body, tp_size, count), out_shape=jax.ShapeDtypeStruct(partial.shape, BF16), in_specs=[HBM_SPEC, HBM_SPEC], out_specs=HBM_SPEC,
         scratch_shapes=[pltpu.VMEM(partial.shape, BF16), pltpu.VMEM(hidden.shape, BF16), pltpu.VMEM((2, hops, count, size, width), BF16), pltpu.VMEM((2, count, size, width), BF16),
-                        dma((4,)), dma((2, hops, count)), dma((2, hops, count)), dma((2, hops, count)), dma((2, hops, count))],
-        compiler_params=pltpu.CompilerParams(collective_id=call_id, has_side_effects=True, vmem_limit_bytes=56 * 1024 * 1024),
-        cost_estimate=pl.CostEstimate(flops=100_000_000_000, transcendentals=0, bytes_accessed=60_000_000),
+                        DMA((4,)), DMA((2, hops, count)), DMA((2, hops, count)), DMA((2, hops, count)), DMA((2, hops, count))],
+        compiler_params=settings(call_id),
+        cost_estimate=cost(30),
         name='finish')(partial, hidden)
-
-
-def route(key_ok, expert_idx, num_experts, capacity):
-    tokens = key_ok.size
-    valid = key_ok.reshape(tokens)
-    first = expert_idx[..., 0].reshape(tokens)
-    second = expert_idx[..., 1].reshape(tokens)
-    expert_ids = jnp.arange(num_experts, dtype=jnp.int32)
-    hot_first = ((first[:, None] == expert_ids) & valid[:, None]).astype(jnp.int32)
-    hot_second = ((second[:, None] == expert_ids) & valid[:, None]).astype(jnp.int32)
-    rank_first = jnp.cumsum(hot_first, axis=0) - 1
-    rank_second = jnp.cumsum(hot_second, axis=0) - 1 + jnp.sum(hot_first, axis=0)
-    slot_first = jnp.sum(rank_first * hot_first, axis=1)
-    slot_second = jnp.sum(rank_second * hot_second, axis=1)
-    dump = num_experts * capacity
-    dest_first = jnp.where(valid & (slot_first < capacity), first * capacity + slot_first, dump)
-    dest_second = jnp.where(valid & (slot_second < capacity), second * capacity + slot_second, dump)
-    choice = jnp.full((dump + 1,), -1, jnp.int32)
-    ids = jnp.arange(tokens, dtype=jnp.int32)
-    choice = choice.at[dest_first].set(ids + tokens * second).at[dest_second].set(ids + tokens * first)
-    return choice[:dump].reshape(num_experts, capacity)
 
 
 def solution(mesh):
     tp_size = mesh.shape['tp']
     ep_size = mesh.shape['ep']
 
-    def gather_tp(value, axis=0, tiled=False):
-        return lax.all_gather(value, 'tp', axis=axis, tiled=tiled)
+    def gather_tp(value):
+        return lax.all_gather(value, 'tp')
 
     def local_fn(x, src_len, expert_idx, ln_gain, ln_bias, w_query, b_query, w_key, w_value, b_value, w_attn_out, b_attn_out, w_fc1, b_fc1, w_fc2, b_fc2, w_router, w_exp_in, b_exp_in, w_exp_out, b_exp_out):
         rows, seq, width = x.shape
@@ -577,62 +748,59 @@
         slices = gather_tp(jnp.concatenate(slices, axis=0))
         small = jnp.concatenate([b_query.reshape(-1), b_value.reshape(-1), b_fc1.reshape(-1), b_exp_in.reshape(-1)])
         small = gather_tp(small)
-        slices, small, x_own = lax.optimization_barrier((slices, small, x_own))
+        cut = cuts[1]
+        pair = 2 * head_cols
+        b_query_all, b_value_all, b_fc1_all, b_exp_in_all = jnp.split(small, [pair, 2 * pair, 2 * pair + hidden_cols], axis=1)
+        b_query_all, b_value_all = [value.reshape(tp_size, 2, head_cols).transpose(1, 0, 2).reshape(2, -1) for value in (b_query_all, b_value_all)]
+        b_qkv = jnp.concatenate([b_query_all, jnp.zeros_like(b_query_all), b_value_all], axis=1)
+        b_fc1_all = b_fc1_all.reshape(tp_size, ep_size, cut).transpose(1, 0, 2).reshape(-1)
+        b_in_own = lax.dynamic_index_in_dim(b_exp_in_all.reshape(tp_size, own_experts, tp_size, -1), tp_index, 2, keepdims=False)
+        part_order = lax.rem(tp_index - jnp.arange(tp_size) + tp_size, tp_size)
+        b_in_own = b_in_own[part_order].transpose(1, 0, 2)
+        b_out_own = lax.dynamic_index_in_dim(b_exp_out.reshape(own_experts, tp_size, width), tp_index, 1, keepdims=False)
+        router = w_router.astype(BF16)
+        slices, x_own, b_qkv, b_fc1_all, b_in_own, b_out_own, router, len_own = lax.optimization_barrier((slices, x_own, b_qkv, b_fc1_all, b_in_own, b_out_own, router, len_own))
         starts = [sum(cuts[:i]) for i in range(5)]
         first_pack = lax.all_gather(slices[:, :starts[1]], 'ep')
         fc1_all, fc2_all, second_pack = [lax.all_gather(slices[:, starts[i]:starts[i + 1]], 'ep') for i in range(1, 4)]
         fc1_all, fc2_all = fc1_all.reshape(-1, width), fc2_all.reshape(-1, width)
-        cut = cuts[1]
-        attn_bias_size = 2 * head_cols
-        b_query_all = small[:, :attn_bias_size].reshape(tp_size, 2, head_cols).transpose(1, 0, 2).reshape(2, -1)
-        b_value_all = small[:, attn_bias_size:2 * attn_bias_size].reshape(tp_size, 2, head_cols).transpose(1, 0, 2).reshape(2, -1)
-        b_fc1_all = small[:, 2 * attn_bias_size:2 * attn_bias_size + hidden_cols]
-        b_exp_in_all = small[:, 2 * attn_bias_size + hidden_cols:].reshape(tp_size, local_experts, -1)
-        b_qkv = jnp.concatenate([b_query_all, jnp.zeros_like(b_query_all), b_value_all], axis=1)
-        b_fc1_all = b_fc1_all.reshape(tp_size, ep_size, cut).transpose(1, 0, 2).reshape(-1)
-
-        key_ok = jnp.arange(seq)[None, :] < src_len[:, None]
-        choice_all = route(key_ok, expert_idx, num_experts, capacity)
-        choice = choice_all.reshape(ep_size, own_experts, tp_size, capacity)
-        choice = lax.dynamic_index_in_dim(choice, tp_index, 2, keepdims=False)
-        choice = choice.transpose(1, 0, 2).reshape(-1)
-        filled = choice >= 0
-        choice = jnp.where(filled, choice, 0)
-        source = lax.rem(choice, tokens)
-        other = lax.div(choice, tokens).reshape(-1, 1)
-        place = 8 * jnp.where(filled, source, tokens)
-
-        def norm(i):
-            return ln_gain[i].reshape(1, width), ln_bias[i].reshape(1, width)
 
         def row(value):
             return value.reshape(1, -1)
 
-        half = width // 2
-        pieces = [(2, 1, 0, half)], [(0, 0, 0, width), (0, 1, 0, width)], [(1, 0, 0, width)], [(1, 1, 0, width), (2, 0, 0, width)], [(2, 1, half, half), (3, 0, 0, width), (3, 1, 0, width)]
-        moved = []
-        moved += move(w_exp_in, w_exp_out, slices[0, :8], tp_size, pieces[0], 4)
+        def norm(i):
+            return row(ln_gain[i]), row(ln_bias[i])
+
+        def piece(code):
+            chunk, which, *part = map(int, code)
+            size = width // (1 + len(part))
+            return chunk, which, sum(part) * size, size
+
+        plan = ['210'], ['00', '01'], ['10'], ['11', '20'], ['211', '30', '31']
+        at_start, in_first, in_dense, in_second, in_experts = [[piece(code) for code in codes] for codes in plan]
+        place, source, other, *moved = move(src_len, expert_idx.transpose(0, 2, 1), w_exp_in, w_exp_out, slices[0, :8], num_experts, capacity, tp_size, ep_size, at_start, 4)
         w_qkv, w_out = unpack_attention(first_pack)
-        hidden, normed, *landed = attention_layer(x_own, len_own, seq, head_dim, norm(0), w_qkv, row(b_qkv[0]), w_out, row(b_attn_out[0]), norm(1), w_exp_in, w_exp_out, moved[0], tp_size, pieces[1], 0)
+        hidden, normed, *landed = attention_layer(x_own, len_own, seq, head_dim, norm(0), w_qkv, row(b_qkv[0]), w_out, row(b_attn_out[0]), norm(1), w_exp_in, w_exp_out, moved[0], tp_size, in_first, 0)
         moved += landed
         second_pack, hidden = lax.optimization_barrier((second_pack, hidden))
-        hidden, *landed = dense_layer(hidden, normed, fc1_all, row(b_fc1_all), fc2_all, row(b_fc2), w_exp_in, w_exp_out, tp_size, pieces[2], 1)
+        hidden, *landed = dense_layer(hidden, normed, fc1_all, row(b_fc1_all), fc2_all, row(b_fc2), w_exp_in, w_exp_out, tp_size, in_dense, 1)
         moved += landed
         w_qkv, w_out = unpack_attention(second_pack)
-        hidden, normed, *landed = attention_layer(hidden, len_own, seq, head_dim, norm(2), w_qkv, row(b_qkv[1]), w_out, row(b_attn_out[1]), norm(3), w_exp_in, w_exp_out, moved[0], tp_size, pieces[3], 2)
+        hidden, normed, *landed = attention_layer(hidden, len_own, seq, head_dim, norm(2), w_qkv, row(b_qkv[1]), w_out, row(b_attn_out[1]), norm(3), w_exp_in, w_exp_out, moved[0], tp_size, in_second, 2)
         moved += landed
-        normed_all = gather_tp(normed, tiled=True)
-
-        b_in_own = lax.dynamic_index_in_dim(b_exp_in_all.reshape(tp_size, own_experts, tp_size, -1), tp_index, 2, keepdims=False)
-        part_order = lax.rem(tp_index - jnp.arange(tp_size) + tp_size, tp_size)
-        b_in_own = b_in_own[part_order].transpose(1, 0, 2)
-        b_out_own = lax.dynamic_index_in_dim(b_exp_out.reshape(own_experts, tp_size, width), tp_index, 1, keepdims=False)
-        dispatch = normed_all[source].reshape(own_experts, ep_size, capacity, width)
+        dispatch = dispatch_rows(source, normed, tp_size, 6).reshape(own_experts, ep_size, capacity, width)
+
         outputs, gates = experts(dispatch, moved, w_exp_in, w_exp_out, b_in_own, b_out_own,
-                                 w_router.astype(BF16), other, tp_size, ep_size, sum(pieces[:4], []), pieces[4], 3)
+                                 router, other, tp_size, ep_size, at_start + in_first + in_dense + in_second, in_experts, 3)
         outputs = outputs.reshape(own_experts * ep_size, capacity, width)
-        partial = combine(place, gates, outputs, tokens)
+        partial = combine(place.reshape(-1), gates, outputs, tokens)
         return finish(partial, hidden, tp_size, 5).reshape(rows, seq, width)
 
-    in_specs = (P(('dp', 'ep'), None, None), P(('dp', 'ep')), P(('dp', 'ep'), None, None), P(), P(), P(None, None, 'tp', None), P(None, 'tp', None), P(None, None, 'tp', None), P(None, None, 'tp', None), P(None, 'tp', None), P(None, 'tp', None, None), P(), P(None, 'tp'), P('tp'), P('tp', None), P(), P(), P('ep', None, 'tp'), P('ep', 'tp'), P('ep', 'tp', None), P('ep', None))
-    return jax.shard_map(local_fn, mesh=mesh, in_specs=in_specs, out_specs=P(('dp', 'ep'), None, None), check_vma=False)
+    axes = {'g': ('dp', 'ep'), 'e': 'ep', 't': 'tp', '.': None}
+
+    def spec(code):
+        return P(*[axes[letter] for letter in code])
+
+    codes = ['g..', 'g', 'g..', '..', '..', '..t.', '.t.', '..t.', '..t.', '.t.', '.t..', '..', '.t', 't', 't.', '.', '..', 'e.t', 'et', 'et.', 'e.']
+    in_specs = tuple(map(spec, codes))
+    return jax.shard_map(local_fn, mesh=mesh, in_specs=in_specs, out_specs=spec('g..'), check_vma=False)

time: 941 us -> 894 us (0.950)
  Pallas kernels: 707 us -> 806 us
  local copies, waits for them, and re-layouts: 137 us -> 43.4 us
  waiting for transfers between devices: 39.7 us -> 14.7 us
  other arithmetic: 25 us -> 2.01 us
    pallas_call x1 -> x2, Pallas kernels: 28.3 us -> 143 us  [the longest x1 112 us: dispatch_rows(): pl.pallas_call(functools.partial(dispatch_body, tp_size), out_shape=jax.S...]
    scatter x2 -> x0, local copies, waits for them, and re-layouts: 60.9 us -> none  [route(): choice.at[dest_first].set(ids + tokens * second).at[dest_second]]
    gather x1 -> x0, local copies, waits for them, and re-layouts: 25.2 us -> none  [local_fn(): dispatch = normed_all[source].reshape(own_experts, ep_size, capacity, width)]
    all_gather x2 -> x1, waiting for transfers between devices: 37.6 us -> 12.7 us  [gather_tp(): return lax.all_gather(value, 'tp')]
    pallas_call x1, Pallas kernels: 36.6 us -> 25.8 us  [combine(): pl.pallas_call(functools.partial(combine_body, blocks), out_shape=jax.Sha...]
  transfers between devices with their start and end apart: 6 -> 5, of which waited for: 2 -> 1; matrix products, arithmetic and copies ran while one was open for 12% -> 3% of each run, Pallas kernels for 14% -> 15%
where the time goes in v4:
time: 894 us; the launch traced here: 893 us
  Pallas kernels  806 us (90%)
  local copies, waits for them, and re-layouts  43.4 us (5%)
  waiting for transfers between devices  14.7 us (2%)
  between operations  13.5 us (2%)
  blocking collectives  12.4 us (1%)
    pallas_call x2, Pallas kernels, attention_layer(): pl.pallas_call(functools.partial(attention_body, tp_size, pieces, head_di...  212 us
    pallas_call x1, Pallas kernels, finish(): pl.pallas_call(functools.partial(finish_body, tp_size, count), out_shape=...  205 us
    pallas_call x1, Pallas kernels, experts(): pl.pallas_call(body, out_shape=(jax.ShapeDtypeStruct(dispatch.shape, BF16...  164 us
    pallas_call x1, Pallas kernels, dispatch_rows(): pl.pallas_call(functools.partial(dispatch_body, tp_size), out_shape=jax.S...  112 us
    pallas_call x1, Pallas kernels, dense_layer(): pl.pallas_call(functools.partial(dense_body, tp_size, pieces, 4), out_sha...  56.6 us
    pallas_call x1, Pallas kernels, move(): pl.pallas_call(functools.partial(move_body, tp_size, ep_size, pieces, own...  31.3 us
    pallas_call x1, Pallas kernels, combine(): pl.pallas_call(functools.partial(combine_body, blocks), out_shape=jax.Sha...  25.8 us
  transfers between devices with their start and end apart: 5, of which 1 were waited for; matrix products, arithmetic and copies ran while one was open for 3% of the time, Pallas kernels for 15%

profile of v4, /device:TPU:97, one launch (start us, length us, event | category | flops | bytes accessed | tf_op | source)
XLA Modules:
  0.0 892.8 jit_solution(8362129896293951939)
XLA Ops:
  6.6 1.2 fusion.12
  7.8 1.1 fusion.11
  8.9 1.1 fusion.10
  10.1 0.7 constant_dynamic-slice_fusion.3
  10.8 1.2 constant_dynamic-slice_fusion.4
  11.9 0.1 copy.61
  12.1 0.4 fusion.2
  12.5 0.9 pad_maximum_fusion
  13.6 0.1 reshape.110
  13.8 12.4 %all-gather.6 = f32[4,1,13824]{2,1,0:T(1,128)S(1)} all-gather(f32[1,1,13824]{2,1,0:T(1,128)S(1)} %reshape.150), channel_id=3, replica_groups=mesh['dp'=1,'tp'=4,'ep'=8] {'tp'}, dimensions={0}, use_global_device_ids=true | all-gather | bytes 276480 | tf_op jit(solution)/shard_map/all_gather | solution.py:714
  26.3 0.1 reshape.115
  26.4 0.1 reshape.116
  26.5 0.1 reshape.113
  26.6 0.1 reshape.114
  26.8 0.7 reshape.118
  27.5 0.2 reshape.119
  27.8 0.6 gather_fusion
  28.3 0.6 copy.72
  29.0 0.6 copy.73
  29.6 0.7 convert_element_type.3.refs_10_
  30.3 0.6 dynamic_slice.33.lens_ref
  30.9 3.7 constant_dynamic-slice_fusion.2
  34.6 12.7 %all-gather.13.cloned.1.call-done = bf16[1536,768]{1,0:T(8,128)(2,1)} async-done(((bf16[384,768]{1,0:T(8,128)(2,1)}), bf16[1536,768]{1,0:T(8,128)(2,1)}) %all-gather.13.cloned.1.call-update) | async-done | bytes 2359312 | tf_op jit(solution)/shard_map/all_gather | solution.py:714
  47.4 3.1 fusion.8
  50.7 0.7 all-gather.15.cloned.1.call-update
  51.5 0.6 all-gather.19.cloned.1.call-update
  52.1 0.6 all-gather.21.cloned.1.call-update
  52.7 0.6 reshape.127.b_out_ref
  53.3 0.6 fusion.17
  53.9 0.6 fusion.15
  54.5 1.3 slice_bitcast_fusion.after_ref
  55.8 0.6 fusion.14
  56.4 31.3 %move.1 = (s32[32,128]{1,0:T(8,128)}, s32[4096,1]{1,0:T(8,128)}, s32[4096,1]{1,0:T(8,128)}, bf16[3,384,768]{2,1,0:T(8,128)(2,1)}) custom-call(s32[8]{0:T(128)} %lens_ref.1, s32[8,2,1024]{2,1,0:T(2,128)} %bitcast.97, bf16[16,768,768]{2,1,0:T(8,128)(2,1)} %refs_6_.1, bf16[16,768,768]{2,1,0:T(8,128)(2,1)} %refs_7_.1, bf16[8,768]{1,0:T(8,128)(2,1)} %slice_bitcast_fusion.after_ref), custom_call_target="tpu_custom_call" | custom-call | flops 30000001024 | bytes 10000000 | tf_op jit(solution)/shard_map/move/pallas_call | solution.py:150
  87.7 2.7 copy.69
  90.5 2.0 slice.118
  92.5 1.1 slice.119
  93.6 107.0 %attention_layer.2 = (bf16[2048,768]{1,0:T(8,128)(2,1)}, bf16[2048,768]{1,0:T(8,128)(2,1)}, bf16[3,768,768]{2,1,0:T(8,128)(2,1)}, bf16[3,768,768]{2,1,0:T(8,128)(2,1)}) custom-call(s32[2]{0:T(128)} %dynamic_slice.33.lens_ref, bf16[2048,768]{1,0:T(8,128)(2,1)} %bitcast.71, f32[1,768]{1,0:T(1,128)} %get-tuple-element.86.gain_ref, ...), custom_call_target="tpu_custom_call" | custom-call | flops 30000001024 | bytes 10000000 | tf_op jit(solution)/shard_map/attention_layer/pallas_call | solution.py:319
  200.6 2.2 slice.120
  202.9 1.3 slice.121
  204.2 2.1 copy.58
  206.3 1.1 copy.59
  207.4 56.6 %dense_layer.1 = (bf16[2048,768]{1,0:T(8,128)(2,1)}, bf16[3,768,768]{2,1,0:T(8,128)(2,1)}) custom-call(bf16[2048,768]{1,0:T(8,128)(2,1)} %get-tuple-element.39.x_ref, bf16[2048,768]{1,0:T(8,128)(2,1)} %get-tuple-element.40.normed_ref, bf16[3072,768]{1,0:T(8,128)(2,1)} %bitcast.95, f32[1,3072]{1,0:T(1,128)} %bitcast.93, bf16[3072,768]{1,0:T(8,128)(2,1)} %bitcast.96, ...), custom_call_target="tpu_custom_call" | custom-call | flops 30000001024 | bytes 10000000 | tf_op jit(solution)/shard_map/dense_layer/pallas_call | solution.py:361
  264.0 105.2 %attention_layer.3 = (bf16[2048,768]{1,0:T(8,128)(2,1)}, bf16[2048,768]{1,0:T(8,128)(2,1)}, bf16[3,768,768]{2,1,0:T(8,128)(2,1)}, bf16[3,768,768]{2,1,0:T(8,128)(2,1)}) custom-call(s32[2]{0:T(128)} %dynamic_slice.33.lens_ref, bf16[2048,768]{1,0:T(8,128)(2,1)} %get-tuple-element.42.x_ref, f32[1,768]{1,0:T(1,128)} %get-tuple-element.85.gain_ref, ...), custom_call_target="tpu_custom_call" | custom-call | flops 30000001024 | bytes 10000000 | tf_op jit(solution)/shard_map/attention_layer/pallas_call | solution.py:319
  369.2 111.6 %dispatch_rows.1 = bf16[4096,768]{1,0:T(8,128)(2,1)} custom-call(s32[4096,1]{1,0:T(8,128)} %get-tuple-element.33.source_ref, bf16[2,4,256,768]{3,2,1,0:T(8,128)(2,1)} %bitcast.100), custom_call_target="tpu_custom_call" | custom-call | flops 30000001024 | bytes 10000000 | tf_op jit(solution)/shard_map/dispatch_rows/pallas_call | solution.py:245
  480.8 164.0 %experts.1 = (bf16[4,8,128,768]{3,2,1,0:T(8,128)(2,1)}, f32[4096,1]{1,0:T(8,128)}) custom-call(bf16[4,8,128,768]{3,2,1,0:T(8,128)(2,1)} %bitcast.98, bf16[3,384,768]{2,1,0:T(8,128)(2,1)} %get-tuple-element.37.after_ref.refs_0_, bf16[3,768,768]{2,1,0:T(8,128)(2,1)} %get-tuple-element.45.refs_1_, bf16[3,768,768]{2,1,0:T(8,128)(2,1)} %get-tuple-element.46.refs_2_, ...), custom_call_target="tpu_custom_call" | custom-call | flops 30000001024 | bytes 10000000 | tf_op jit(solution)/shard_map/experts/pallas_call | solution.py:531
  644.8 25.8 %combine.1.partial_ref = bf16[8192,768]{1,0:T(8,128)(2,1)} custom-call(s32[4096]{0:T(1024)} %bitcast.101, bf16[4,1024,768]{2,1,0:T(8,128)(2,1)} %bitcast.99, f32[4096,1]{1,0:T(8,128)} %get-tuple-element.55.gates_ref), custom_call_target="tpu_custom_call" | custom-call | flops 30000001024 | bytes 10000000 | tf_op jit(solution)/shard_map/combine/pallas_call | solution.py:602
  670.7 205.0 %finish.1 = bf16[8192,768]{1,0:T(8,128)(2,1)} custom-call(bf16[8192,768]{1,0:T(8,128)(2,1)} %combine.1.partial_ref, bf16[2048,768]{1,0:T(8,128)(2,1)} %get-tuple-element.56.hidden_ref), custom_call_target="tpu_custom_call" | custom-call | flops 30000001024 | bytes 10000000 | tf_op jit(solution)/shard_map/finish/pallas_call | solution.py:700
  875.7 10.6 %copy.75 = bf16[8,1024,768]{2,1,0:T(8,128)(2,1)} copy(bf16[8,1024,768]{2,1,0:T(8,128)(2,1)} %bitcast.65) | data formatting | bytes 25165824
  (65 shorter events, 1.0 us)
Async XLA Ops:
  6.5 3.5 copy-start
  6.6 40.8 %all-gather.13.cloned.1.call-start = ((), (), s32[]{:S(2)}) async-start(), calls=%async_computation | async-start | bytes 2949120 | tf_op jit(solution)/shard_map/all_gather | solution.py:714
  6.6 3.4 copy-start.3
  10.0 3.6 copy-start.12
  10.0 3.7 copy-start.13
  10.0 3.7 copy-start.10
  10.8 1.8 copy-start.2
  10.8 2.8 copy-start.5
  12.1 17.6 %copy-start.4 = (f32[768,128]{1,0:T(8,128)S(1)}, f32[768,128]{1,0:T(8,128)}, u32[]{:S(2)}) copy-start(f32[768,128]{1,0:T(8,128)} %param.37) | copy-start | bytes 1179652
  12.5 16.5 %copy-start.6 = (f32[16,768]{1,0:T(8,128)S(1)}, f32[16,768]{1,0:T(8,128)}, u32[]{:S(2)}) copy-start(f32[16,768]{1,0:T(8,128)} %param.41) | copy-start | bytes 147460
  12.5 17.8 %copy-start.14 = (s32[8]{0:T(128)S(1)}, s32[8]{0:T(128)}, u32[]{:S(2)}) copy-start(s32[8]{0:T(128)} %lens_ref.1) | copy-start | bytes 100
  13.4 74.3 %all-gather.17.cloned.1.call-start = ((), (), s32[]{:S(2)}) async-start(), calls=%async_computation.2 | async-start | bytes 5308416 | tf_op jit(solution)/shard_map/all_gather | solution.py:764
  47.4 5.3 copy-start.11
  47.4 5.9 copy-start.9
  47.4 6.5 copy-start.7
  47.4 6.5 copy-start.8
  50.6 150.0 %all-gather.15.cloned.1.call-start = ((), (), s32[]{:S(2)}) async-start(), calls=%async_computation.1 | async-start | bytes 5308416 | tf_op jit(solution)/shard_map/all_gather | solution.py:765
  51.4 156.0 %all-gather.19.cloned.1.call-start = ((), (), s32[]{:S(2)}) async-start(), calls=%async_computation.3 | async-start | bytes 5308416 | tf_op jit(solution)/shard_map/all_gather | solution.py:765
  52.0 155.4 %all-gather.21.cloned.1.call-start = ((), (), s32[]{:S(2)}) async-start(), calls=%async_computation.4 | async-start | bytes 5308416 | tf_op jit(solution)/shard_map/all_gather | solution.py:765
  875.7 10.6 %copy-start.1 = (bf16[768,768]{1,0:T(8,128)(2,1)S(1)}, bf16[768,768]{1,0:T(8,128)(2,1)}, u32[]{:S(2)}) copy-start(bf16[768,768]{1,0:T(8,128)(2,1)} %param.35) | copy-start | bytes 3538948
Sparse Core Ops, SparseCore 0:
  13.6 33.7 all-gather.12
  50.7 32.1 all-gather.16
  84.5 31.4 all-gather.14
  117.5 31.4 all-gather.18
  150.4 31.4 all-gather.20

commit v5 on v4

--- a/solution.py
+++ b/solution.py
@@ -111,13 +111,66 @@
         count = lax.fori_loop(0, rows * per_row, block, count)
 
 
-def move_body(tp_size, ep_size, pieces, own_experts, lens_ref, index_ref, w_in_ref, w_out_ref, after_ref, place_ref, source_ref, other_ref, *rest):
-    moved_refs = rest[:len(pieces)]
-    total_ref, total_t_ref, send_sem, recv_sem = rest[len(pieces):]
-    copies = exchange_all(tp_size, (w_in_ref, w_out_ref), pieces, moved_refs, send_sem, recv_sem)
-    enter([('tp', tp_size)])
-    for copy in copies:
+def spread(ep_size, src_ref, view, sems):
+    me = lax.axis_index('ep')
+    send_sem, recv_sem = sems
+    copies = [pltpu.make_async_remote_copy(
+        src_ref=src_ref, dst_ref=view(me), send_sem=send_sem.at[distance], recv_sem=recv_sem.at[distance],
+        device_id={'ep': away('ep', ep_size, distance)}, device_id_type=MESH) for distance in range(1, ep_size)]
+    return copies + [pltpu.make_async_copy(src_ref, view(me), send_sem.at[0])]
+
+
+def by_kind(ref, ep_size):
+    per = ep_size // ref.shape[0]
+    return lambda index: ref.at[index // per, :, lax.rem(index, per)]
+
+
+def start_body(tp_size, ep_size, pieces, own_experts, lens_ref, index_ref, w_in_ref, w_out_ref, own_ref, *refs):
+    biases, refs = refs[:4], refs[4:]
+    place_ref, source_ref, other_ref, first_ref, later_ref, *refs = refs
+    biases_all, refs = refs[:4], refs[4:]
+    moved_refs, refs = refs[:len(pieces)], refs[len(pieces):]
+    total_ref, total_t_ref, move_send, move_recv, tp_send, tp_recv, row_send, row_recv, pair_send, pair_recv = refs
+    mine = lax.axis_index('tp')
+    me = lax.axis_index('ep')
+    view = by_kind(first_ref, ep_size)
+    moves = exchange_all(tp_size, (w_in_ref, w_out_ref), pieces, moved_refs, move_send, move_recv)
+    pairs = [(own_ref.at[0], view(me).at[mine])]
+    pairs += [(bias, whole.at[mine]) for bias, whole in zip(biases, biases_all)]
+    pairs += [(own_ref.at[1 + index], later_ref.at[index, mine]) for index in range(later_ref.shape[0])]
+    gathers = []
+    for index, (src, dst) in enumerate(pairs):
+        gathers.append([pltpu.make_async_copy(src, dst, tp_send.at[index, 0])] + [pltpu.make_async_remote_copy(
+            src_ref=src, dst_ref=dst, send_sem=tp_send.at[index, distance], recv_sem=tp_recv.at[index, distance],
+            device_id={'tp': away('tp', tp_size, distance)}, device_id_type=MESH) for distance in (1, tp_size - 1, *range(2, tp_size - 1))])
+    enter([('tp', tp_size), ('ep', ep_size)])
+    for copies in gathers:
+        for copy in copies:
+            copy.start()
+    for copy in moves:
         copy.start()
+
+    cores = 2
+    steps = range(1, ep_size // cores)
+    other_core = me + 1 - cores * lax.rem(me, cores)
+
+    def along(step):
+        return pltpu.make_async_remote_copy(
+            src_ref=view(me), dst_ref=view(me), send_sem=row_send.at[step], recv_sem=row_recv.at[step],
+            device_id={'ep': away('ep', ep_size, cores * step)}, device_id_type=MESH)
+
+    def across(step):
+        part = view(away('ep', ep_size, ep_size - cores * step))
+        return pltpu.make_async_remote_copy(
+            src_ref=part, dst_ref=part, send_sem=pair_send.at[step], recv_sem=pair_recv.at[step],
+            device_id={'ep': other_core}, device_id_type=MESH)
+
+    for copy in gathers[0]:
+        copy.wait()
+    for step in steps:
+        along(step).start()
+    across(0).start()
+
     route_tables(lens_ref, index_ref, total_ref, total_t_ref)
     rows, _, seq = index_ref.shape
     experts_count, wide = total_ref.shape
@@ -126,7 +179,7 @@
 
     def take(index, carry):
         chunk = index // ep_size
-        expert = (index % ep_size) * (own_experts * tp_size) + chunk * tp_size + lax.axis_index('tp')
+        expert = (index % ep_size) * (own_experts * tp_size) + chunk * tp_size + mine
         line = total_ref[pl.ds(expert, 1), :].astype(jnp.int32)
         low, high = line[:, :slots], line[:, slots:2 * slots]
         place_ref[pl.ds(index, 1), :] = 8 * jnp.where(high > 0, 256 * (high - 1) + low, rows * seq)
@@ -137,24 +190,35 @@
         other_ref[at, :] = other
         return carry
 
+    for step in steps:
+        along(step).wait()
+        across(step).start()
     lax.fori_loop(0, own_experts * ep_size, take, 0)
-    for copy in copies:
+    for step in range(ep_size // cores):
+        across(step).wait()
+    for copies in gathers[1:]:
+        for copy in copies:
+            copy.wait()
+    for copy in moves:
         copy.wait()
 
 
-def move(lens, index, w_in, w_out, after, num_experts, capacity, tp_size, ep_size, pieces, call_id):
+def start(lens, index, w_in, w_out, own, biases, num_experts, capacity, tp_size, ep_size, pieces, call_id):
     own_experts = w_in.shape[0] // tp_size
     blocks = own_experts * ep_size
-    dma = DMA((len(pieces), tp_size - 1))
+    packs, cut, width = own.shape
     column = jax.ShapeDtypeStruct((blocks * capacity, 1), jnp.int32)
+    first = jax.ShapeDtypeStruct((packs, tp_size, ep_size // packs, cut, width), BF16)
+    later = jax.ShapeDtypeStruct((packs - 1, tp_size, cut, width), BF16)
+    biases_all = [jax.ShapeDtypeStruct((tp_size,) + bias.shape, F32) for bias in biases]
+    moved = landings(tp_size, w_in, pieces)
+    dma = [DMA((len(pieces), tp_size - 1))] * 2 + [DMA((packs + len(biases), tp_size))] * 2 + [DMA((ep_size,))] * 4
     return pl.pallas_call(
-        functools.partial(move_body, tp_size, ep_size, pieces, own_experts),
-        out_shape=(jax.ShapeDtypeStruct((blocks, capacity), jnp.int32), column, column, *landings(tp_size, w_in, pieces)),
-        in_specs=[SMEM_SPEC, VMEM_SPEC, HBM_SPEC, HBM_SPEC, HBM_SPEC], out_specs=(VMEM_SPEC, VMEM_SPEC, VMEM_SPEC, *[HBM_SPEC for _ in pieces]),
-        scratch_shapes=[pltpu.VMEM((num_experts, 3 * capacity), F32), pltpu.VMEM((3 * capacity, num_experts), F32), dma, dma],
-        compiler_params=settings(call_id),
-        cost_estimate=cost(30),
-        name='move')(lens, index, w_in, w_out, after)
+        functools.partial(start_body, tp_size, ep_size, pieces, own_experts),
+        out_shape=(jax.ShapeDtypeStruct((blocks, capacity), jnp.int32), column, column, first, later, *biases_all, *moved),
+        in_specs=[SMEM_SPEC, VMEM_SPEC] + [HBM_SPEC] * (3 + len(biases)), out_specs=[VMEM_SPEC] * 3 + [HBM_SPEC] * (2 + len(biases) + len(pieces)),
+        scratch_shapes=[pltpu.VMEM((num_experts, 3 * capacity), F32), pltpu.VMEM((3 * capacity, num_experts), F32)] + dma,
+        compiler_params=settings(call_id), cost_estimate=cost(30), name='start')(lens, index, w_in, w_out, own, *biases)
 
 
 def dispatch_body(tp_size, source_ref, normed_ref, o_ref, all_buf, acc_ref, load_sem, send_sem, recv_sem):
@@ -250,31 +314,48 @@
         name='dispatch_rows')(source, normed.reshape(2, count, size, width))
 
 
-def attention_body(tp_size, pieces, head_dim, block_q, lens_ref, x_ref, gain_ref, shift_ref, w_qkv_ref, b_qkv_ref, w_out_ref, b_out_ref, gain2_ref, shift2_ref, w_in_ref, w_exp_out_ref, after_ref,
-                   hidden_ref, normed_ref, *rest):
+def attention_body(tp_size, ep_size, layer, pieces, spreads, head_dim, block_q, lens_ref, x_ref, gain_ref, shift_ref, w_ref, b_query_ref, b_value_ref, b_out_ref, w_in_ref, w_exp_out_ref, later_ref,
+                   hidden_ref, normed_ref, *refs):
+    moved_refs, refs = refs[:len(pieces)], refs[len(pieces):]
+    spread_refs, refs = refs[:spreads], refs[spreads:]
+    x_buf, w_buf, bias_buf, qkv_ref, context_ref, load_sem, move_send, move_recv, spread_sem = refs
     row = pl.program_id(0)
     block = pl.program_id(1)
-    seq, width = x_ref.shape
-    moved_refs = rest[:len(pieces)]
-    qkv_ref, context_ref, send_sem, recv_sem = rest[len(pieces):]
-    copies = exchange_all(tp_size, (w_in_ref, w_exp_out_ref), pieces, moved_refs, send_sem, recv_sem)
+    own_rows, seq, width = x_buf.shape
+    mine = lax.axis_index('tp')
+    copies = exchange_all(tp_size, (w_in_ref, w_exp_out_ref), pieces, moved_refs, move_send, move_recv)
+    for index, ref in enumerate(spread_refs):
+        copies += spread(ep_size, later_ref.at[index], lambda part, ref=ref: ref.at[:, part], (spread_sem.at[0, index], spread_sem.at[1, index]))
 
     @pl.when((row == 0) & (block == 0))
     def _():
-        enter([('tp', tp_size)])
+        base = mine * own_rows if layer == 0 else 0
+        loads = [pltpu.make_async_copy(w_ref, w_buf, load_sem.at[0]), pltpu.make_async_copy(x_ref.at[pl.ds(base, own_rows)], x_buf, load_sem.at[1])]
+        for load in loads:
+            load.start()
+        enter([('tp', tp_size), ('ep', ep_size)] if spreads else [('tp', tp_size)])
         for copy in copies:
             copy.start()
+        bias_buf[...] = jnp.zeros_like(bias_buf)
+        for ref, start in ((b_query_ref, 0), (b_value_ref, 2 * width)):
+            parts = [ref[part, layer, pl.ds(head, 1), :] for part in range(tp_size) for head in range(ref.shape[2])]
+            bias_buf[:, pl.ds(start, width)] = jnp.concatenate(parts, axis=1)
+        for load in loads:
+            load.wait()
+
+    def norm(value, index):
+        return norm_rows(value, gain_ref[pl.ds(index, 1), :], shift_ref[pl.ds(index, 1), :]).astype(BF16)
 
     @pl.when(block == 0)
     def _():
         def project(index, carry):
             rows = span(index, block_q)
-            normed = norm_rows(x_ref[rows, :].astype(F32), gain_ref[...], shift_ref[...]).astype(BF16)
-            qkv_ref[rows, :] = (dot_t(normed, w_qkv_ref[...]) + b_qkv_ref[...]).astype(BF16)
+            normed = norm(x_buf[row, rows, :].astype(F32), 2 * layer)
+            qkv_ref[rows, :] = (dot_t(normed, w_buf[pl.ds(0, 3 * width), :]) + bias_buf[...]).astype(BF16)
             return carry
         lax.fori_loop(0, seq // block_q, project, 0)
 
-    length = lens_ref[row]
+    length = lens_ref[mine * own_rows + row]
     pair = 2 * head_dim
     key_ok = lax.broadcasted_iota(jnp.int32, (1, seq), 1) < length
     lane_head = lax.broadcasted_iota(jnp.int32, (1, pair), 1) // head_dim
@@ -299,10 +380,10 @@
         return carry
 
     lax.fori_loop(0, width // pair, heads, 0)
-    projected = jnp.dot(context_ref[...], w_out_ref[...], preferred_element_type=F32)
-    hidden = (x_ref[rows, :].astype(F32) + projected + b_out_ref[...]).astype(BF16)
+    projected = jnp.dot(context_ref[...], w_buf[pl.ds(3 * width, width), :], preferred_element_type=F32)
+    hidden = (x_buf[row, rows, :].astype(F32) + projected + b_out_ref[pl.ds(layer, 1), :]).astype(BF16)
     hidden_ref[...] = hidden
-    normed_ref[...] = norm_rows(hidden.astype(F32), gain2_ref[...], shift2_ref[...]).astype(BF16)
+    normed_ref[...] = norm(hidden.astype(F32), 2 * layer + 1)
 
     @pl.when((row == pl.num_programs(0) - 1) & (block == pl.num_programs(1) - 1))
     def _():
@@ -310,41 +391,53 @@
             copy.wait()
 
 
-def attention_layer(x, lens, seq, head_dim, norm, w_qkv, b_qkv, w_out, b_out, norm2, w_exp_in, w_exp_out, after, tp_size, pieces, call_id):
-    tokens, width = x.shape
+def attention_layer(layer, x, own_rows, lens, head_dim, gain, shift, w_pack, b_query, b_value, b_out, w_exp_in, w_exp_out, later, tp_size, ep_size, pieces, spreads, call_id):
+    _, seq, width = x.shape
     block_q = min(256, seq)
     blocks = seq // block_q
-    fixed = lambda shape: pl.BlockSpec(shape, lambda r, q: (0,) * len(shape), pipeline_mode=pl.Buffered(1))
+    tokens = own_rows * seq
+    _, _, cut, _ = later.shape
     moved = landings(tp_size, w_exp_in, pieces)
+    spread_out = [jax.ShapeDtypeStruct((tp_size, ep_size, cut, width), BF16)] * spreads
+    result = jax.ShapeDtypeStruct((tokens, width), BF16)
+    result_spec = pl.BlockSpec((block_q, width), lambda r, q: (r * blocks + q, 0))
+    dma = DMA((len(pieces), tp_size - 1))
     return pl.pallas_call(
-        functools.partial(attention_body, tp_size, pieces, head_dim, block_q),
-        out_shape=(jax.ShapeDtypeStruct((tokens, width), BF16), jax.ShapeDtypeStruct((tokens, width), BF16), *moved),
-        grid=(tokens // seq, blocks),
-        in_specs=[SMEM_SPEC, pl.BlockSpec((seq, width), lambda r, q: (r, 0)), fixed((1, width)), fixed((1, width)),
-                  fixed(w_qkv.shape), fixed((1, 3 * width)), fixed(w_out.shape), fixed((1, width)), fixed((1, width)), fixed((1, width)), HBM_SPEC, HBM_SPEC, HBM_SPEC],
-        out_specs=(pl.BlockSpec((block_q, width), lambda r, q: (r * blocks + q, 0)), pl.BlockSpec((block_q, width), lambda r, q: (r * blocks + q, 0)), *[HBM_SPEC for _ in pieces]),
-        scratch_shapes=[pltpu.VMEM((seq, 3 * width), BF16), pltpu.VMEM((block_q, width), BF16), DMA((len(pieces), tp_size - 1)), DMA((len(pieces), tp_size - 1))],
+        functools.partial(attention_body, tp_size, ep_size, layer, pieces, spreads, head_dim, block_q),
+        out_shape=(result, result, *moved, *spread_out), grid=(own_rows, blocks),
+        in_specs=[SMEM_SPEC, HBM_SPEC, VMEM_SPEC, VMEM_SPEC, HBM_SPEC, VMEM_SPEC, VMEM_SPEC, VMEM_SPEC, HBM_SPEC, HBM_SPEC, HBM_SPEC],
+        out_specs=(result_spec, result_spec, *[HBM_SPEC for _ in moved + spread_out]),
+        scratch_shapes=[pltpu.VMEM((own_rows, seq, width), BF16), pltpu.VMEM(w_pack.shape, BF16), pltpu.VMEM((1, 3 * width), F32), pltpu.VMEM((seq, 3 * width), BF16),
+                        pltpu.VMEM((block_q, width), BF16), DMA((2,)), dma, dma, DMA((2, max(spreads, 1), ep_size))],
         compiler_params=settings(call_id, grid=('arbitrary', 'arbitrary')),
         cost_estimate=cost(30),
-        name='attention_layer')(lens, x, *norm, w_qkv, b_qkv, w_out, b_out, *norm2, w_exp_in, w_exp_out, after)
-
-
-def dense_body(tp_size, pieces, parts, x_ref, normed_ref, w_in_ref, b_in_ref, w_out_ref, b_out_ref, w_exp_in_ref, w_exp_out_ref, o_ref, *rest):
+        name='attention_layer')(lens, x, gain, shift, w_pack, b_query, b_value, b_out, w_exp_in, w_exp_out, later)
+
+
+def dense_body(tp_size, ep_size, pieces, x_ref, normed_ref, w_in_ref, b_in_ref, w_out_ref, b_out_ref, w_exp_in_ref, w_exp_out_ref, later_ref, o_ref, *refs):
+    moved_refs, refs = refs[:len(pieces)], refs[len(pieces):]
+    second_ref, w_in_buf, w_out_buf, load_sem, move_send, move_recv, spread_sem = refs
     block = pl.program_id(0)
-    copies = exchange_all(tp_size, (w_exp_in_ref, w_exp_out_ref), pieces, rest[:len(pieces)], *rest[len(pieces):])
+    copies = exchange_all(tp_size, (w_exp_in_ref, w_exp_out_ref), pieces, moved_refs, move_send, move_recv)
+    copies += spread(ep_size, later_ref.at[later_ref.shape[0] - 1], by_kind(second_ref, ep_size), (spread_sem.at[0], spread_sem.at[1]))
 
     @pl.when(block == 0)
     def _():
-        enter([('tp', tp_size)])
+        loads = [pltpu.make_async_copy(w_in_ref, w_in_buf, load_sem.at[0]), pltpu.make_async_copy(w_out_ref, w_out_buf, load_sem.at[1])]
+        for load in loads:
+            load.start()
+        enter([('tp', tp_size), ('ep', ep_size)])
         for copy in copies:
             copy.start()
-
-    size = w_in_ref.shape[0] // parts
+        for load in loads:
+            load.wait()
+
+    parts, _, size = b_in_ref.shape
     total = x_ref[...].astype(F32) + b_out_ref[...]
     for part in range(parts):
         cols = pl.ds(part * size, size)
-        inner = jnp.maximum(dot_t(normed_ref[...], w_in_ref[cols, :]) + b_in_ref[:, cols], 0.0).astype(BF16)
-        total += jnp.dot(inner, w_out_ref[cols, :], preferred_element_type=F32)
+        inner = jnp.maximum(dot_t(normed_ref[...], w_in_buf[cols, :]) + b_in_ref[part], 0.0).astype(BF16)
+        total += jnp.dot(inner, w_out_buf[cols, :], preferred_element_type=F32)
     o_ref[...] = total.astype(BF16)
 
     @pl.when(block == pl.num_programs(0) - 1)
@@ -353,20 +446,23 @@
             copy.wait()
 
 
-def dense_layer(x, normed, w_in, b_in, w_out, b_out, w_exp_in, w_exp_out, tp_size, pieces, call_id):
+def dense_layer(x, normed, w_in, b_in, w_out, b_out, w_exp_in, w_exp_out, later, tp_size, ep_size, pieces, call_id):
     tokens, width = x.shape
     block_n = min(256, tokens)
-    fixed = lambda shape: pl.BlockSpec(shape, lambda i: (0,) * len(shape), pipeline_mode=pl.Buffered(1))
+    _, _, cut, _ = later.shape
+    kinds = 4
+    second = jax.ShapeDtypeStruct((kinds, tp_size, ep_size // kinds, cut, width), BF16)
     dma = DMA((len(pieces), tp_size - 1))
+    rows = pl.BlockSpec((block_n, width), lambda i: (i, 0))
     return pl.pallas_call(
-        functools.partial(dense_body, tp_size, pieces, 4),
-        out_shape=(jax.ShapeDtypeStruct((tokens, width), BF16), *landings(tp_size, w_exp_in, pieces)), grid=(tokens // block_n,),
-        in_specs=[pl.BlockSpec((block_n, width), lambda i: (i, 0)), pl.BlockSpec((block_n, width), lambda i: (i, 0)), fixed(w_in.shape), fixed(b_in.shape), fixed(w_out.shape), fixed((1, width)), HBM_SPEC, HBM_SPEC],
-        out_specs=(pl.BlockSpec((block_n, width), lambda i: (i, 0)), *[HBM_SPEC for _ in pieces]),
-        scratch_shapes=[dma, dma],
+        functools.partial(dense_body, tp_size, ep_size, pieces),
+        out_shape=(jax.ShapeDtypeStruct((tokens, width), BF16), *landings(tp_size, w_exp_in, pieces), second), grid=(tokens // block_n,),
+        in_specs=[rows, rows, HBM_SPEC, VMEM_SPEC, HBM_SPEC, VMEM_SPEC, HBM_SPEC, HBM_SPEC, HBM_SPEC],
+        out_specs=(rows, *[HBM_SPEC for _ in pieces], HBM_SPEC),
+        scratch_shapes=[pltpu.VMEM(w_in.shape, BF16), pltpu.VMEM(w_out.shape, BF16), DMA((2,)), dma, dma, DMA((2, ep_size))],
         compiler_params=settings(call_id, grid=('arbitrary',)),
         cost_estimate=cost(30),
-        name='dense_layer')(x, normed, w_in, b_in, w_out, b_out, w_exp_in, w_exp_out)
+        name='dense_layer')(x, normed, w_in, b_in, w_out, b_out, w_exp_in, w_exp_out, later)
 
 
 def experts_body(tp_size, ep_size, early, late, dispatch_ref, early_refs, w_in_ref, w_out_ref, b_in_ref, b_out_ref, w_router_ref, other_ref, returned_ref, gates_ref,
@@ -419,7 +515,7 @@
         if chunk + 1 < chunks:
             load(chunk + 1).start()
         load(chunk).wait()
-        logits = jnp.dot(sent_buf[chunk % 2].reshape(ep_size * slots, width), w_router_ref[...], preferred_element_type=F32)
+        logits = jnp.dot(sent_buf[chunk % 2].reshape(ep_size * slots, width), w_router_ref[...].astype(BF16), preferred_element_type=F32)
         rows = pl.ds(chunk * ep_size * slots, ep_size * slots)
         own = jnp.sum(jnp.where(lane == group * (chunks * tp_size) + (chunk * tp_size + mine), logits, 0.0), axis=1, keepdims=True)
         other = jnp.sum(jnp.where(lane == other_ref[rows, :], logits, 0.0), axis=1, keepdims=True)
@@ -455,9 +551,12 @@
                 for copy in moves[piece]:
                     copy.wait_recv()
 
+    def expert_row(chunk):
+        return pl.ds(chunk * tp_size + mine, 1)
+
     def inner_part(chunk, index, part):
         tokens = arrived_ref[chunk, pl.ds(2 * index, 2)].reshape(2 * slots, width)
-        inner = jnp.dot(tokens, part_ref((chunk, 0), part)[...], preferred_element_type=F32) + b_in_ref[chunk, pl.ds(part, 1), :]
+        inner = jnp.dot(tokens, part_ref((chunk, 0), part)[...], preferred_element_type=F32) + b_in_ref[away('tp', tp_size, tp_size - part), expert_row(chunk), :]
         return jnp.maximum(inner, 0.0).astype(BF16)
 
     backs = {}
@@ -489,7 +588,7 @@
             for part in range(tp_size):
                 inner = held[part][pl.ds(2 * index, 2)].reshape(2 * slots, width) if last else inner_part(chunk, index, part)
                 total += jnp.dot(inner, part_ref((chunk, 1), part)[...], preferred_element_type=F32)
-            out_buf[slot, pl.ds(2 * index, 2)] = (total + b_out_ref[pl.ds(chunk, 1), :]).astype(BF16).reshape(2, slots, width)
+            out_buf[slot, pl.ds(2 * index, 2)] = (total + b_out_ref[expert_row(chunk), :]).astype(BF16).reshape(2, slots, width)
 
             @pl.when(index > 0)
             def _():
@@ -710,9 +809,6 @@
     tp_size = mesh.shape['tp']
     ep_size = mesh.shape['ep']
 
-    def gather_tp(value):
-        return lax.all_gather(value, 'tp')
-
     def local_fn(x, src_len, expert_idx, ln_gain, ln_bias, w_query, b_query, w_key, w_value, b_value, w_attn_out, b_attn_out, w_fc1, b_fc1, w_fc2, b_fc2, w_router, w_exp_in, b_exp_in, w_exp_out, b_exp_out):
         rows, seq, width = x.shape
         tokens = rows * seq
@@ -721,55 +817,18 @@
         local_experts = w_exp_in.shape[0]
         own_experts = local_experts // tp_size
         _, _, local_heads, head_dim = w_query.shape
-        heads = local_heads * tp_size
         head_cols = local_heads * head_dim
-        hidden_cols = w_fc1.shape[1]
-        tp_index = lax.axis_index('tp')
-        ep_index = lax.axis_index('ep')
         own_rows = rows // tp_size
-        own_tokens = own_rows * seq
-        x_own = lax.dynamic_slice_in_dim(x, tp_index * own_rows, own_rows, 0).reshape(own_tokens, width)
-        len_own = lax.dynamic_slice_in_dim(src_len, tp_index * own_rows, own_rows, 0)
 
         def pack_attention(j):
             columns = [w[j].reshape(width, head_cols).T for w in (w_query, w_key, w_value)]
             return jnp.concatenate(columns + [w_attn_out[j].reshape(head_cols, width)], axis=0)
 
-        def unpack_attention(gathered):
-            by_kind = gathered.reshape(4, ep_size // 4, tp_size, -1, width).transpose(0, 2, 1, 3, 4)
-            return by_kind[:3].reshape(3 * heads * head_dim, width), by_kind[3].reshape(heads * head_dim, width)
-
         def own_slice(value):
             size = value.shape[0] // ep_size
-            return lax.dynamic_slice_in_dim(value, ep_index * size, size, 0)
-
-        slices = [own_slice(value) for value in (pack_attention(0), w_fc1.T, w_fc2, pack_attention(1))]
-        cuts = [value.shape[0] for value in slices]
-        slices = gather_tp(jnp.concatenate(slices, axis=0))
-        small = jnp.concatenate([b_query.reshape(-1), b_value.reshape(-1), b_fc1.reshape(-1), b_exp_in.reshape(-1)])
-        small = gather_tp(small)
-        cut = cuts[1]
-        pair = 2 * head_cols
-        b_query_all, b_value_all, b_fc1_all, b_exp_in_all = jnp.split(small, [pair, 2 * pair, 2 * pair + hidden_cols], axis=1)
-        b_query_all, b_value_all = [value.reshape(tp_size, 2, head_cols).transpose(1, 0, 2).reshape(2, -1) for value in (b_query_all, b_value_all)]
-        b_qkv = jnp.concatenate([b_query_all, jnp.zeros_like(b_query_all), b_value_all], axis=1)
-        b_fc1_all = b_fc1_all.reshape(tp_size, ep_size, cut).transpose(1, 0, 2).reshape(-1)
-        b_in_own = lax.dynamic_index_in_dim(b_exp_in_all.reshape(tp_size, own_experts, tp_size, -1), tp_index, 2, keepdims=False)
-        part_order = lax.rem(tp_index - jnp.arange(tp_size) + tp_size, tp_size)
-        b_in_own = b_in_own[part_order].transpose(1, 0, 2)
-        b_out_own = lax.dynamic_index_in_dim(b_exp_out.reshape(own_experts, tp_size, width), tp_index, 1, keepdims=False)
-        router = w_router.astype(BF16)
-        slices, x_own, b_qkv, b_fc1_all, b_in_own, b_out_own, router, len_own = lax.optimization_barrier((slices, x_own, b_qkv, b_fc1_all, b_in_own, b_out_own, router, len_own))
-        starts = [sum(cuts[:i]) for i in range(5)]
-        first_pack = lax.all_gather(slices[:, :starts[1]], 'ep')
-        fc1_all, fc2_all, second_pack = [lax.all_gather(slices[:, starts[i]:starts[i + 1]], 'ep') for i in range(1, 4)]
-        fc1_all, fc2_all = fc1_all.reshape(-1, width), fc2_all.reshape(-1, width)
-
-        def row(value):
-            return value.reshape(1, -1)
-
-        def norm(i):
-            return row(ln_gain[i]), row(ln_bias[i])
+            return lax.dynamic_slice_in_dim(value, lax.axis_index('ep') * size, size, 0)
+
+        own = jnp.stack([own_slice(value) for value in (pack_attention(0), w_fc1.T, w_fc2, pack_attention(1))])
 
         def piece(code):
             chunk, which, *part = map(int, code)
@@ -778,22 +837,23 @@
 
         plan = ['210'], ['00', '01'], ['10'], ['11', '20'], ['211', '30', '31']
         at_start, in_first, in_dense, in_second, in_experts = [[piece(code) for code in codes] for codes in plan]
-        place, source, other, *moved = move(src_len, expert_idx.transpose(0, 2, 1), w_exp_in, w_exp_out, slices[0, :8], num_experts, capacity, tp_size, ep_size, at_start, 4)
-        w_qkv, w_out = unpack_attention(first_pack)
-        hidden, normed, *landed = attention_layer(x_own, len_own, seq, head_dim, norm(0), w_qkv, row(b_qkv[0]), w_out, row(b_attn_out[0]), norm(1), w_exp_in, w_exp_out, moved[0], tp_size, in_first, 0)
+        weights = w_exp_in, w_exp_out
+        place, source, other, pack, later, b_query, b_value, b_fc1, b_exp_in, *moved = start(
+            src_len, expert_idx.transpose(0, 2, 1), *weights, own, (b_query, b_value, b_fc1.reshape(1, -1), b_exp_in), num_experts, capacity, tp_size, ep_size, at_start, 4)
+
+        def attention(layer, hidden, pack, pieces, spreads):
+            return attention_layer(layer, hidden, own_rows, src_len, head_dim, ln_gain, ln_bias, pack.reshape(-1, width), b_query, b_value, b_attn_out, *weights, later,
+                                   tp_size, ep_size, pieces, spreads, layer)
+
+        hidden, normed, *landed, fc1_all, fc2_all = attention(0, x, pack, in_first, 2)
         moved += landed
-        second_pack, hidden = lax.optimization_barrier((second_pack, hidden))
-        hidden, *landed = dense_layer(hidden, normed, fc1_all, row(b_fc1_all), fc2_all, row(b_fc2), w_exp_in, w_exp_out, tp_size, in_dense, 1)
+        hidden, *landed, pack = dense_layer(hidden, normed, fc1_all.reshape(-1, width), b_fc1, fc2_all.reshape(-1, width), b_fc2.reshape(1, width), *weights, later, tp_size, ep_size, in_dense, 2)
         moved += landed
-        w_qkv, w_out = unpack_attention(second_pack)
-        hidden, normed, *landed = attention_layer(hidden, len_own, seq, head_dim, norm(2), w_qkv, row(b_qkv[1]), w_out, row(b_attn_out[1]), norm(3), w_exp_in, w_exp_out, moved[0], tp_size, in_second, 2)
+        hidden, normed, *landed = attention(1, hidden.reshape(own_rows, seq, width), pack, in_second, 0)
         moved += landed
         dispatch = dispatch_rows(source, normed, tp_size, 6).reshape(own_experts, ep_size, capacity, width)
-
-        outputs, gates = experts(dispatch, moved, w_exp_in, w_exp_out, b_in_own, b_out_own,
-                                 router, other, tp_size, ep_size, at_start + in_first + in_dense + in_second, in_experts, 3)
-        outputs = outputs.reshape(own_experts * ep_size, capacity, width)
-        partial = combine(place.reshape(-1), gates, outputs, tokens)
+        outputs, gates = experts(dispatch, moved, *weights, b_exp_in, b_exp_out, w_router, other, tp_size, ep_size, at_start + in_first + in_dense + in_second, in_experts, 3)
+        partial = combine(place.reshape(-1), gates, outputs.reshape(-1, capacity, width), tokens)
         return finish(partial, hidden, tp_size, 5).reshape(rows, seq, width)
 
     axes = {'g': ('dp', 'ep'), 'e': 'ep', 't': 'tp', '.': None}

time: 894 us -> 866 us (0.969)
  Pallas kernels: 806 us -> 843 us
  local copies, waits for them, and re-layouts: 43.4 us -> 18.4 us
  waiting for transfers between devices: 14.7 us -> 0 us
  between operations: 13.5 us -> 0.14 us
  blocking collectives: 12.4 us -> 0 us
    pallas_call x4, Pallas kernels: 300 us -> 339 us  [the longest x2 215 us: attention_layer(): pl.pallas_call(functools.partial(attention_body, tp_size, ep_size, layer,...]
    slice x10 -> x0, local copies, waits for them, and re-layouts: 14.9 us -> none  [the longest x3 6.36 us: unpack_attention(): by_kind[:3].reshape(3 * heads * head_dim, width)]
    all_gather x5 -> x0, waiting for transfers between devices: 12.8 us -> none  [the longest x1 12.7 us: gather_tp(): return lax.all_gather(value, 'tp')]
    all_gather x1 -> x0, blocking collectives: 12.4 us -> none  [gather_tp(): return lax.all_gather(value, 'tp')]
  transfers between devices with their start and end apart: 5 -> 0, of which waited for: 1 -> 0; matrix products, arithmetic and copies ran while one was open for 3% -> 0% of each run, Pallas kernels for 15% -> 0%
where the time goes in v5:
time: 866 us; the launch traced here: 864 us
  Pallas kernels  843 us (97%)
  local copies, waits for them, and re-layouts  18.4 us (2%)
    pallas_call x2, Pallas kernels, attention_layer(): pl.pallas_call(functools.partial(attention_body, tp_size, ep_size, layer,...  215 us
    pallas_call x1, Pallas kernels, finish(): pl.pallas_call(functools.partial(finish_body, tp_size, count), out_shape=...  206 us
    pallas_call x1, Pallas kernels, experts(): pl.pallas_call(body, out_shape=(jax.ShapeDtypeStruct(dispatch.shape, BF16...  160 us
    pallas_call x1, Pallas kernels, dispatch_rows(): pl.pallas_call(functools.partial(dispatch_body, tp_size), out_shape=jax.S...  113 us
    pallas_call x1, Pallas kernels, start(): pl.pallas_call(functools.partial(start_body, tp_size, ep_size, pieces, ow...  66.1 us
    pallas_call x1, Pallas kernels, dense_layer(): pl.pallas_call(functools.partial(dense_body, tp_size, ep_size, pieces), o...  57.4 us
    pallas_call x1, Pallas kernels, combine(): pl.pallas_call(functools.partial(combine_body, blocks), out_shape=jax.Sha...  25.8 us

profile of v5, /device:TPU:97, one launch (start us, length us, event | category | flops | bytes accessed | tf_op | source)
XLA Modules:
  0.0 864.2 jit_solution(13718662318937563186)
XLA Ops:
  0.0 0.0 copy-start
  0.0 0.0 copy-start.3
  0.0 0.0 copy-start.2
  0.0 1.4 reshape.33.refs_2_
  1.4 1.3 reshape.38.b_out_ref
  2.7 1.3 copy.23.refs_0_
  4.0 1.3 copy.24.refs_1_
  5.3 0.0 copy-done
  5.3 0.1 constant_dynamic-slice_fusion
  5.4 0.1 copy.25
  5.5 1.1 fusion.8
  6.6 1.1 fusion.9
  7.7 0.0 copy-done.2
  7.8 0.0 copy-done.3
  7.9 1.2 dynamic-slice_bitcast_fusion
  9.1 0.3 fusion.7
  9.4 0.9 pad_maximum_fusion.own_ref
  10.2 66.1 %start.1 = (s32[32,128]{1,0:T(8,128)}, s32[4096,1]{1,0:T(8,128)}, s32[4096,1]{1,0:T(8,128)}, bf16[4,4,2,96,768]{4,3,2,1,0:T(8,128)(2,1)}, bf16[3,4,96,768]{3,2,1...) custom-call(s32[8]{0:T(128)} %lens_ref.5, ...), custom_call_target="tpu_custom_call" | custom-call | flops 30000001024 | bytes 10000000 | tf_op jit(solution)/shard_map/start/pallas_call | solution.py:216
  76.4 108.8 %attention_layer.2 = (bf16[2048,768]{1,0:T(8,128)(2,1)}, bf16[2048,768]{1,0:T(8,128)(2,1)}, bf16[3,768,768]{2,1,0:T(8,128)(2,1)}, bf16[3,768,768]{2,1,0:T(8,128)...) custom-call(s32[8]{0:T(128)} %lens_ref.5, bf16[8,1024,768]{2,1,0:T(8,128)(2,1)} %x_ref.1, ...), custom_call_target="tpu_custom_call" | custom-call | flops 30000001024 | bytes 10000000 | tf_op jit(solution)/shard_map/attention_layer/pallas_call | solution.py:405
  185.2 57.4 %dense_layer.1 = (bf16[2048,768]{1,0:T(8,128)(2,1)}, bf16[3,768,768]{2,1,0:T(8,128)(2,1)}, bf16[4,4,2,96,768]{4,3,2,1,0:T(8,128)(2,1)}) custom-call(bf16[2048,768]{1,0:T(8,128)(2,1)} %get-tuple-element.36.x_ref, bf16[2048,768]{1,0:T(8,128)(2,1)} %get-tuple-element.37.normed_ref, bf16[3072,768]{1,0:T(8,128)(2,1)} %bitcast.55, ...), custom_call_target="tpu_custom_call" | custom-call | flops 30000001024 | bytes 10000000 | tf_op jit(solution)/shard_map/dense_layer/pallas_call | solution.py:457
  242.6 106.5 %attention_layer.3 = (bf16[2048,768]{1,0:T(8,128)(2,1)}, bf16[2048,768]{1,0:T(8,128)(2,1)}, bf16[3,768,768]{2,1,0:T(8,128)(2,1)}, bf16[3,768,768]{2,1,0:T(8,128)(2,1)}) custom-call(s32[8]{0:T(128)} %lens_ref.5, bf16[2,1024,768]{2,1,0:T(8,128)(2,1)} %bitcast.57, f32[4,768]{1,0:T(4,128)} %gain_ref.3, f32[4,768]{1,0:T(4,128)} %shift_ref.3, ...), custom_call_target="tpu_custom_call" | custom-call | flops 30000001024 | bytes 10000000 | tf_op jit(solution)/shard_map/attention_layer/pallas_call | solution.py:405
  349.1 113.4 %dispatch_rows.1 = bf16[4096,768]{1,0:T(8,128)(2,1)} custom-call(s32[4096,1]{1,0:T(8,128)} %get-tuple-element.31.source_ref, bf16[2,4,256,768]{3,2,1,0:T(8,128)(2,1)} %bitcast.58), custom_call_target="tpu_custom_call" | custom-call | flops 30000001024 | bytes 10000000 | tf_op jit(solution)/shard_map/dispatch_rows/pallas_call | solution.py:309
  462.5 159.7 %experts.1 = (bf16[4,8,128,768]{3,2,1,0:T(8,128)(2,1)}, f32[4096,1]{1,0:T(8,128)}) custom-call(bf16[4,8,128,768]{3,2,1,0:T(8,128)(2,1)} %bitcast.51, bf16[3,384,768]{2,1,0:T(8,128)(2,1)} %get-tuple-element.44.refs_0_, bf16[3,768,768]{2,1,0:T(8,128)(2,1)} %get-tuple-element.45.refs_1_, bf16[3,768,768]{2,1,0:T(8,128)(2,1)} %get-tuple-element.46.refs_2_, ...), custom_call_target="tpu_custom_call" | custom-call | flops 30000001024 | bytes 10000000 | tf_op jit(solution)/shard_map/experts/pallas_call | solution.py:630
  622.2 25.8 %combine.1.partial_ref = bf16[8192,768]{1,0:T(8,128)(2,1)} custom-call(s32[4096]{0:T(1024)} %bitcast.59, bf16[4,1024,768]{2,1,0:T(8,128)(2,1)} %bitcast.52, f32[4096,1]{1,0:T(8,128)} %get-tuple-element.53.gates_ref), custom_call_target="tpu_custom_call" | custom-call | flops 30000001024 | bytes 10000000 | tf_op jit(solution)/shard_map/combine/pallas_call | solution.py:701
  648.0 205.6 %finish.1 = bf16[8192,768]{1,0:T(8,128)(2,1)} custom-call(bf16[8192,768]{1,0:T(8,128)(2,1)} %combine.1.partial_ref, bf16[2048,768]{1,0:T(8,128)(2,1)} %get-tuple-element.54.hidden_ref), custom_call_target="tpu_custom_call" | custom-call | flops 30000001024 | bytes 10000000 | tf_op jit(solution)/shard_map/finish/pallas_call | solution.py:799
  853.6 0.0 copy-start.1
  853.6 10.6 %copy.27 = bf16[8,1024,768]{2,1,0:T(8,128)(2,1)} copy(bf16[8,1024,768]{2,1,0:T(8,128)(2,1)} %bitcast.40) | data formatting | bytes 25165824
  864.2 0.0 copy-done.1
  (2 shorter events, 0.1 us)
Async XLA Ops:
  0.0 5.3 copy-start
  0.0 7.8 copy-start.3
  0.0 7.7 copy-start.2
  853.6 10.6 %copy-start.1 = (bf16[768,768]{1,0:T(8,128)(2,1)S(1)}, bf16[768,768]{1,0:T(8,128)(2,1)}, u32[]{:S(2)}) copy-start(bf16[768,768]{1,0:T(8,128)(2,1)} %param.33) | copy-start | bytes 3538948

commit v6 on v5

--- a/solution.py
+++ b/solution.py
@@ -57,9 +57,9 @@
 
 
 def exchange(tp_size, weights, piece, landing_ref, send_sem, recv_sem):
-    chunk, which, start, rows = piece
+    chunk, which, start, cols = piece
     return [pltpu.make_async_remote_copy(
-        src_ref=weights[which].at[chunk * tp_size + away('tp', tp_size, distance), pl.ds(start, rows)], dst_ref=landing_ref.at[distance - 1],
+        src_ref=weights[which].at[chunk * tp_size + away('tp', tp_size, distance), :, pl.ds(start, cols)], dst_ref=landing_ref.at[distance - 1],
         send_sem=send_sem.at[distance - 1], recv_sem=recv_sem.at[distance - 1],
         device_id={'tp': away('tp', tp_size, distance)}, device_id_type=MESH)
         for distance in sorted(range(1, tp_size), key=lambda d: (min(d, tp_size - d), d))]
@@ -73,7 +73,7 @@
 
 
 def landings(tp_size, weight, pieces):
-    return [jax.ShapeDtypeStruct((tp_size - 1, rows, weight.shape[2]), BF16) for _, _, _, rows in pieces]
+    return [jax.ShapeDtypeStruct((tp_size - 1, weight.shape[1], cols), BF16) for _, _, _, cols in pieces]
 
 
 def route_tables(lens_ref, index_ref, total_ref, total_t_ref):
@@ -125,24 +125,30 @@
     return lambda index: ref.at[index // per, :, lax.rem(index, per)]
 
 
-def start_body(tp_size, ep_size, pieces, own_experts, lens_ref, index_ref, w_in_ref, w_out_ref, own_ref, *refs):
+def front_body(tp_size, ep_size, pieces, own_experts, head_dim, lens_ref, index_ref, gain_ref, shift_ref, b_out_ref, b_fc2_ref, x_ref, w_in_ref, w_out_ref, own_ref, *refs):
     biases, refs = refs[:4], refs[4:]
-    place_ref, source_ref, other_ref, first_ref, later_ref, *refs = refs
-    biases_all, refs = refs[:4], refs[4:]
+    place_ref, other_ref, hidden_ref, o_ref, b_exp_ref, *refs = refs
     moved_refs, refs = refs[:len(pieces)], refs[len(pieces):]
-    total_ref, total_t_ref, move_send, move_recv, tp_send, tp_recv, row_send, row_recv, pair_send, pair_recv = refs
+    (b_query_ref, b_value_ref, b_fc1_ref, first_ref, second_ref, later_ref, fc1_ref, fc2_ref, source_ref, total_ref, total_t_ref, bias_buf, qkv_ref, context_ref, all_buf,
+     load_sem, move_send, move_recv, tp_send, tp_recv, row_send, row_recv, pair_send, pair_recv, spread_sem, ring_send, ring_recv) = refs
     mine = lax.axis_index('tp')
     me = lax.axis_index('ep')
+    own_rows, seq, width = hidden_ref.shape
+    _, ways, count, size, _ = all_buf.shape
+    own_tokens = own_rows * seq
+
     view = by_kind(first_ref, ep_size)
     moves = exchange_all(tp_size, (w_in_ref, w_out_ref), pieces, moved_refs, move_send, move_recv)
     pairs = [(own_ref.at[0], view(me).at[mine])]
-    pairs += [(bias, whole.at[mine]) for bias, whole in zip(biases, biases_all)]
+    pairs += [(bias, whole.at[mine]) for bias, whole in zip(biases, (b_query_ref, b_value_ref, b_fc1_ref, b_exp_ref))]
     pairs += [(own_ref.at[1 + index], later_ref.at[index, mine]) for index in range(later_ref.shape[0])]
     gathers = []
     for index, (src, dst) in enumerate(pairs):
         gathers.append([pltpu.make_async_copy(src, dst, tp_send.at[index, 0])] + [pltpu.make_async_remote_copy(
             src_ref=src, dst_ref=dst, send_sem=tp_send.at[index, distance], recv_sem=tp_recv.at[index, distance],
             device_id={'tp': away('tp', tp_size, distance)}, device_id_type=MESH) for distance in (1, tp_size - 1, *range(2, tp_size - 1))])
+    load_x = pltpu.make_async_copy(x_ref.at[pl.ds(mine * own_rows, own_rows)], hidden_ref, load_sem)
+    load_x.start()
     enter([('tp', tp_size), ('ep', ep_size)])
     for copies in gathers:
         for copy in copies:
@@ -170,9 +176,17 @@
     for step in steps:
         along(step).start()
     across(0).start()
+    for copies in gathers[1:]:
+        for copy in copies:
+            copy.wait()
+    views = [lambda part: fc1_ref.at[:, part], lambda part: fc2_ref.at[:, part], by_kind(second_ref, ep_size)]
+    spreads = [spread(ep_size, later_ref.at[index], where, (spread_sem.at[0, index], spread_sem.at[1, index])) for index, where in enumerate(views)]
+    for copies in spreads:
+        for copy in copies:
+            copy.start()
 
     route_tables(lens_ref, index_ref, total_ref, total_t_ref)
-    rows, _, seq = index_ref.shape
+    rows, _, _ = index_ref.shape
     experts_count, wide = total_ref.shape
     slots = wide // 3
     lane = lax.broadcasted_iota(jnp.int32, (1, experts_count), 1)
@@ -196,273 +210,180 @@
     lax.fori_loop(0, own_experts * ep_size, take, 0)
     for step in range(ep_size // cores):
         across(step).wait()
-    for copies in gathers[1:]:
+    load_x.wait()
+
+    hops = tp_size - 1
+
+    def behind(way, distance):
+        return away('tp', tp_size, (tp_size - distance) % tp_size if way == 0 else distance % tp_size)
+
+    def ring(way, hop, index, chunk):
+        piece = all_buf.at[chunk, way, index]
+        return pltpu.make_async_remote_copy(
+            src_ref=piece, dst_ref=piece, send_sem=ring_send.at[way, hop, index], recv_sem=ring_recv.at[way, hop, index],
+            device_id={'tp': away('tp', tp_size, 1 + way * (tp_size - 2))}, device_id_type=MESH)
+
+    def norm(value, index):
+        return norm_rows(value, gain_ref[pl.ds(index, 1), :], shift_ref[pl.ds(index, 1), :]).astype(BF16)
+
+    pair = 2 * head_dim
+    lane_head = lax.broadcasted_iota(jnp.int32, (1, pair), 1) // head_dim
+    factor = (head_dim ** -0.5) * LOG2E
+    blocks = seq // size
+
+    def attention(layer, pack_ref):
+        def pack_rows(start, number):
+            return pack_ref[pl.ds(start, number)].reshape(number * width, width)
+
+        bias_buf[...] = jnp.zeros_like(bias_buf)
+        for ref, start in ((b_query_ref, 0), (b_value_ref, 2 * width)):
+            parts = [ref[part, head, pl.ds(layer, 1), :] for part in range(tp_size) for head in range(ref.shape[1])]
+            bias_buf[:, pl.ds(start, width)] = jnp.concatenate(parts, axis=1)
+        def one_row(row, carry):
+            key_ok = lax.broadcasted_iota(jnp.int32, (1, seq), 1) < lens_ref[mine * own_rows + row]
+
+            def project(index, carry):
+                rows = span(index, size)
+                normed = norm(hidden_ref[row, rows, :].astype(F32), 2 * layer)
+                qkv_ref[rows, :] = (dot_t(normed, pack_rows(0, 3)) + bias_buf[...]).astype(BF16)
+                return carry
+
+            lax.fori_loop(0, blocks, project, 0)
+
+            def attend(block, carry):
+                rows = span(block, size)
+
+                def heads(index, carry):
+                    lanes = pl.multiple_of(index * pair, pair)
+                    query = qkv_ref[rows, pl.ds(lanes, pair)]
+                    keys = qkv_ref[:, pl.ds(pl.multiple_of(lanes + width, pair), pair)]
+                    values = qkv_ref[:, pl.ds(pl.multiple_of(lanes + 2 * width, pair), pair)]
+                    result = None
+                    for head in range(2):
+                        scores = dot_t(jnp.where(lane_head == head, query, jnp.zeros_like(query)), keys)
+                        scores = jnp.where(key_ok, scores, -1e30)
+                        top = jnp.max(scores, axis=-1, keepdims=True)
+                        weights = jnp.exp2((scores - top) * factor)
+                        scale = 1.0 / jnp.sum(weights, axis=-1, keepdims=True)
+                        part = jnp.dot((weights * scale).astype(BF16), values, preferred_element_type=F32)
+                        result = part if result is None else jnp.where(lane_head == head, part, result)
+                    context_ref[:, pl.ds(lanes, pair)] = result.astype(BF16)
+                    return carry
+
+                lax.fori_loop(0, width // pair, heads, 0)
+                projected = jnp.dot(context_ref[...], pack_rows(3, 1), preferred_element_type=F32)
+                hidden = (hidden_ref[row, rows, :].astype(F32) + projected + b_out_ref[pl.ds(layer, 1), :]).astype(BF16)
+                hidden_ref[row, rows, :] = hidden
+                if layer:
+                    all_buf[mine, row, block] = norm(hidden.astype(F32), 2 * layer + 1)
+                    ring(row, 0, block, mine).start()
+                return carry
+
+            lax.fori_loop(0, blocks, attend, 0)
+            return carry
+
+        lax.fori_loop(0, own_rows, one_row, 0)
+
+    attention(0, first_ref)
+
+    for copies in spreads[:2]:
         for copy in copies:
             copy.wait()
+
+    def dense(index, carry):
+        row, rows = index // blocks, span(index % blocks, size)
+        value = hidden_ref[row, rows, :].astype(F32)
+        normed = norm(value, 1)
+        total = value + b_fc2_ref[...]
+        for part in range(tp_size):
+            cols = fc1_ref[part].reshape(-1, width)
+            inner = jnp.maximum(dot_t(normed, cols) + b_fc1_ref[part], 0.0).astype(BF16)
+            total += jnp.dot(inner, fc2_ref[part].reshape(-1, width), preferred_element_type=F32)
+        hidden_ref[row, rows, :] = total.astype(BF16)
+        return carry
+
+    lax.fori_loop(0, own_rows * blocks, dense, 0)
+    for copy in spreads[2]:
+        copy.wait()
+    attention(1, second_ref)
+
+    token = lax.broadcasted_iota(jnp.int32, (1, size), 1)
+    slot_count, _ = o_ref.shape
+    some = min(512, slot_count)
+
+    def dispatch(index, chunks, fresh):
+        def part(part, carry):
+            at = span(part, some)
+            total = None if fresh else o_ref[at, :].astype(F32)
+            for way in range(ways):
+                base = chunks[way] * own_tokens + (way * count + index) * size
+                hot = jnp.where(source_ref[at, :] == token + base, 1.0, 0.0).astype(BF16)
+                taken = jnp.dot(hot, all_buf[chunks[way], way, index], preferred_element_type=F32)
+                total = taken if total is None else total + taken
+            o_ref[at, :] = total.astype(BF16)
+            return carry
+
+        lax.fori_loop(0, slot_count // some, part, 0)
+
+    dispatch(0, (mine, mine), True)
+
+    def own(index, carry):
+        dispatch(index, (mine, mine), False)
+        return carry
+
+    lax.fori_loop(1, count, own, 0)
+    for hop in range(1, tp_size):
+        def arrive(index, carry):
+            chunks = [behind(way, hop) for way in range(ways)]
+            for way in range(ways):
+                ring(way, hop - 1, index, chunks[way]).wait_recv()
+                if hop < hops:
+                    ring(way, hop, index, chunks[way]).start()
+            dispatch(index, chunks, False)
+            return carry
+
+        lax.fori_loop(0, count, arrive, 0)
+
+    def drain(index, carry):
+        for way in range(ways):
+            for hop in range(hops):
+                ring(way, hop, index, mine).wait_send()
+        return carry
+
+    lax.fori_loop(0, count, drain, 0)
     for copy in moves:
         copy.wait()
 
 
-def start(lens, index, w_in, w_out, own, biases, num_experts, capacity, tp_size, ep_size, pieces, call_id):
+def front(lens, index, gain, shift, b_out, b_fc2, x, w_in, w_out, own, biases, num_experts, capacity, head_dim, tp_size, ep_size, pieces, call_id):
     own_experts = w_in.shape[0] // tp_size
     blocks = own_experts * ep_size
     packs, cut, width = own.shape
-    column = jax.ShapeDtypeStruct((blocks * capacity, 1), jnp.int32)
-    first = jax.ShapeDtypeStruct((packs, tp_size, ep_size // packs, cut, width), BF16)
-    later = jax.ShapeDtypeStruct((packs - 1, tp_size, cut, width), BF16)
-    biases_all = [jax.ShapeDtypeStruct((tp_size,) + bias.shape, F32) for bias in biases]
+    rows, seq, _ = x.shape
+    own_rows = rows // tp_size
+    size = min(256, seq)
+    count = seq // size
+    slots = blocks * capacity
+    per = ep_size // packs
+
+    def vmem(*shape, dtype=BF16):
+        return pltpu.VMEM(shape, dtype)
+
     moved = landings(tp_size, w_in, pieces)
-    dma = [DMA((len(pieces), tp_size - 1))] * 2 + [DMA((packs + len(biases), tp_size))] * 2 + [DMA((ep_size,))] * 4
+    b_exp = jax.ShapeDtypeStruct((tp_size,) + biases[3].shape, F32)
+    pack = vmem(packs, tp_size, per, cut, width)
+    piece_dma, gather_dma, ring_dma = DMA((len(pieces), tp_size - 1)), DMA((packs + len(biases), tp_size)), DMA((own_rows, tp_size - 1, count))
     return pl.pallas_call(
-        functools.partial(start_body, tp_size, ep_size, pieces, own_experts),
-        out_shape=(jax.ShapeDtypeStruct((blocks, capacity), jnp.int32), column, column, first, later, *biases_all, *moved),
-        in_specs=[SMEM_SPEC, VMEM_SPEC] + [HBM_SPEC] * (3 + len(biases)), out_specs=[VMEM_SPEC] * 3 + [HBM_SPEC] * (2 + len(biases) + len(pieces)),
-        scratch_shapes=[pltpu.VMEM((num_experts, 3 * capacity), F32), pltpu.VMEM((3 * capacity, num_experts), F32)] + dma,
-        compiler_params=settings(call_id), cost_estimate=cost(30), name='start')(lens, index, w_in, w_out, own, *biases)
-
-
-def dispatch_body(tp_size, source_ref, normed_ref, o_ref, all_buf, acc_ref, load_sem, send_sem, recv_sem):
-    me = lax.axis_index('tp')
-    _, count, size, width = normed_ref.shape
-    own_tokens = 2 * count * size
-    slots = source_ref.shape[0]
-    block = min(512, slots)
-    hops = tp_size - 1
-    step_to = (1, tp_size - 1)
-    lane = lax.broadcasted_iota(jnp.int32, (1, size), 1)
-
-    def behind(way, distance):
-        return away('tp', tp_size, (tp_size - distance) % tp_size if way == 0 else distance % tp_size)
-
-    def send(way, hop, index, src_ref, chunk):
-        return pltpu.make_async_remote_copy(
-            src_ref=src_ref, dst_ref=all_buf.at[chunk, way, index], send_sem=send_sem.at[way, hop, index], recv_sem=recv_sem.at[way, hop, index],
-            device_id={'tp': away('tp', tp_size, step_to[way])}, device_id_type=MESH)
-
-    load = pltpu.make_async_copy(normed_ref, all_buf.at[me], load_sem)
-    load.start()
-    enter([('tp', tp_size)])
-
-    def first(index, carry):
-        for way in range(2):
-            send(way, 0, index, normed_ref.at[way, index], me).start()
-        return carry
-
-    lax.fori_loop(0, count, first, 0)
-    load.wait()
-
-    def place(index, chunks, fresh):
-        def some(part, carry):
-            at = span(part, block)
-            total = None if fresh else acc_ref[at, :]
-            for way in range(2):
-                base = chunks[way] * own_tokens + (way * count + index) * size
-                hot = jnp.where(source_ref[at, :] == lane + base, 1.0, 0.0).astype(BF16)
-                part_sum = jnp.dot(hot, all_buf[chunks[way], way, index], preferred_element_type=F32)
-                total = part_sum if total is None else total + part_sum
-            acc_ref[at, :] = total
-            return carry
-
-        lax.fori_loop(0, slots // block, some, 0)
-
-    place(0, (me, me), True)
-
-    def own(index, carry):
-        place(index, (me, me), False)
-        return carry
-
-    lax.fori_loop(1, count, own, 0)
-    for hop in range(1, tp_size):
-        def arrive(index, carry):
-            chunks = [behind(way, hop) for way in range(2)]
-            for way in range(2):
-                arrived = all_buf.at[chunks[way], way, index]
-                send(way, hop - 1, index, arrived, chunks[way]).wait_recv()
-                if hop < hops:
-                    send(way, hop, index, arrived, chunks[way]).start()
-            place(index, chunks, False)
-            return carry
-
-        lax.fori_loop(0, count, arrive, 0)
-
-    def finish_rows(part, carry):
-        at = span(part, block)
-        o_ref[at, :] = acc_ref[at, :].astype(BF16)
-        return carry
-
-    lax.fori_loop(0, slots // block, finish_rows, 0)
-
-    def drain(index, carry):
-        for way in range(2):
-            for hop in range(hops):
-                send(way, hop, index, normed_ref.at[way, index], me).wait_send()
-        return carry
-
-    lax.fori_loop(0, count, drain, 0)
-
-
-def dispatch_rows(source, normed, tp_size, call_id):
-    tokens, width = normed.shape
-    size = min(256, tokens // 2)
-    count = tokens // (2 * size)
-    slots = source.shape[0]
-    return pl.pallas_call(
-        functools.partial(dispatch_body, tp_size), out_shape=jax.ShapeDtypeStruct((slots, width), BF16), in_specs=[VMEM_SPEC, HBM_SPEC], out_specs=VMEM_SPEC,
-        scratch_shapes=[pltpu.VMEM((tp_size, 2, count, size, width), BF16), pltpu.VMEM((slots, width), F32), DMA, DMA((2, tp_size - 1, count)), DMA((2, tp_size - 1, count))],
-        compiler_params=settings(call_id),
-        cost_estimate=cost(30),
-        name='dispatch_rows')(source, normed.reshape(2, count, size, width))
-
-
-def attention_body(tp_size, ep_size, layer, pieces, spreads, head_dim, block_q, lens_ref, x_ref, gain_ref, shift_ref, w_ref, b_query_ref, b_value_ref, b_out_ref, w_in_ref, w_exp_out_ref, later_ref,
-                   hidden_ref, normed_ref, *refs):
-    moved_refs, refs = refs[:len(pieces)], refs[len(pieces):]
-    spread_refs, refs = refs[:spreads], refs[spreads:]
-    x_buf, w_buf, bias_buf, qkv_ref, context_ref, load_sem, move_send, move_recv, spread_sem = refs
-    row = pl.program_id(0)
-    block = pl.program_id(1)
-    own_rows, seq, width = x_buf.shape
-    mine = lax.axis_index('tp')
-    copies = exchange_all(tp_size, (w_in_ref, w_exp_out_ref), pieces, moved_refs, move_send, move_recv)
-    for index, ref in enumerate(spread_refs):
-        copies += spread(ep_size, later_ref.at[index], lambda part, ref=ref: ref.at[:, part], (spread_sem.at[0, index], spread_sem.at[1, index]))
-
-    @pl.when((row == 0) & (block == 0))
-    def _():
-        base = mine * own_rows if layer == 0 else 0
-        loads = [pltpu.make_async_copy(w_ref, w_buf, load_sem.at[0]), pltpu.make_async_copy(x_ref.at[pl.ds(base, own_rows)], x_buf, load_sem.at[1])]
-        for load in loads:
-            load.start()
-        enter([('tp', tp_size), ('ep', ep_size)] if spreads else [('tp', tp_size)])
-        for copy in copies:
-            copy.start()
-        bias_buf[...] = jnp.zeros_like(bias_buf)
-        for ref, start in ((b_query_ref, 0), (b_value_ref, 2 * width)):
-            parts = [ref[part, layer, pl.ds(head, 1), :] for part in range(tp_size) for head in range(ref.shape[2])]
-            bias_buf[:, pl.ds(start, width)] = jnp.concatenate(parts, axis=1)
-        for load in loads:
-            load.wait()
-
-    def norm(value, index):
-        return norm_rows(value, gain_ref[pl.ds(index, 1), :], shift_ref[pl.ds(index, 1), :]).astype(BF16)
-
-    @pl.when(block == 0)
-    def _():
-        def project(index, carry):
-            rows = span(index, block_q)
-            normed = norm(x_buf[row, rows, :].astype(F32), 2 * layer)
-            qkv_ref[rows, :] = (dot_t(normed, w_buf[pl.ds(0, 3 * width), :]) + bias_buf[...]).astype(BF16)
-            return carry
-        lax.fori_loop(0, seq // block_q, project, 0)
-
-    length = lens_ref[mine * own_rows + row]
-    pair = 2 * head_dim
-    key_ok = lax.broadcasted_iota(jnp.int32, (1, seq), 1) < length
-    lane_head = lax.broadcasted_iota(jnp.int32, (1, pair), 1) // head_dim
-    factor = (head_dim ** -0.5) * LOG2E
-    rows = span(block, block_q)
-
-    def heads(index, carry):
-        lanes = pl.multiple_of(index * pair, pair)
-        query = qkv_ref[rows, pl.ds(lanes, pair)]
-        keys = qkv_ref[:, pl.ds(pl.multiple_of(lanes + width, pair), pair)]
-        values = qkv_ref[:, pl.ds(pl.multiple_of(lanes + 2 * width, pair), pair)]
-        result = None
-        for head in range(2):
-            scores = dot_t(jnp.where(lane_head == head, query, jnp.zeros_like(query)), keys)
-            scores = jnp.where(key_ok, scores, -1e30)
-            top = jnp.max(scores, axis=-1, keepdims=True)
-            weights = jnp.exp2((scores - top) * factor)
-            scale = 1.0 / jnp.sum(weights, axis=-1, keepdims=True)
-            part = jnp.dot((weights * scale).astype(BF16), values, preferred_element_type=F32)
-            result = part if result is None else jnp.where(lane_head == head, part, result)
-        context_ref[:, pl.ds(lanes, pair)] = result.astype(BF16)
-        return carry
-
-    lax.fori_loop(0, width // pair, heads, 0)
-    projected = jnp.dot(context_ref[...], w_buf[pl.ds(3 * width, width), :], preferred_element_type=F32)
-    hidden = (x_buf[row, rows, :].astype(F32) + projected + b_out_ref[pl.ds(layer, 1), :]).astype(BF16)
-    hidden_ref[...] = hidden
-    normed_ref[...] = norm(hidden.astype(F32), 2 * layer + 1)
-
-    @pl.when((row == pl.num_programs(0) - 1) & (block == pl.num_programs(1) - 1))
-    def _():
-        for copy in copies:
-            copy.wait()
-
-
-def attention_layer(layer, x, own_rows, lens, head_dim, gain, shift, w_pack, b_query, b_value, b_out, w_exp_in, w_exp_out, later, tp_size, ep_size, pieces, spreads, call_id):
-    _, seq, width = x.shape
-    block_q = min(256, seq)
-    blocks = seq // block_q
-    tokens = own_rows * seq
-    _, _, cut, _ = later.shape
-    moved = landings(tp_size, w_exp_in, pieces)
-    spread_out = [jax.ShapeDtypeStruct((tp_size, ep_size, cut, width), BF16)] * spreads
-    result = jax.ShapeDtypeStruct((tokens, width), BF16)
-    result_spec = pl.BlockSpec((block_q, width), lambda r, q: (r * blocks + q, 0))
-    dma = DMA((len(pieces), tp_size - 1))
-    return pl.pallas_call(
-        functools.partial(attention_body, tp_size, ep_size, layer, pieces, spreads, head_dim, block_q),
-        out_shape=(result, result, *moved, *spread_out), grid=(own_rows, blocks),
-        in_specs=[SMEM_SPEC, HBM_SPEC, VMEM_SPEC, VMEM_SPEC, HBM_SPEC, VMEM_SPEC, VMEM_SPEC, VMEM_SPEC, HBM_SPEC, HBM_SPEC, HBM_SPEC],
-        out_specs=(result_spec, result_spec, *[HBM_SPEC for _ in moved + spread_out]),
-        scratch_shapes=[pltpu.VMEM((own_rows, seq, width), BF16), pltpu.VMEM(w_pack.shape, BF16), pltpu.VMEM((1, 3 * width), F32), pltpu.VMEM((seq, 3 * width), BF16),
-                        pltpu.VMEM((block_q, width), BF16), DMA((2,)), dma, dma, DMA((2, max(spreads, 1), ep_size))],
-        compiler_params=settings(call_id, grid=('arbitrary', 'arbitrary')),
-        cost_estimate=cost(30),
-        name='attention_layer')(lens, x, gain, shift, w_pack, b_query, b_value, b_out, w_exp_in, w_exp_out, later)
-
-
-def dense_body(tp_size, ep_size, pieces, x_ref, normed_ref, w_in_ref, b_in_ref, w_out_ref, b_out_ref, w_exp_in_ref, w_exp_out_ref, later_ref, o_ref, *refs):
-    moved_refs, refs = refs[:len(pieces)], refs[len(pieces):]
-    second_ref, w_in_buf, w_out_buf, load_sem, move_send, move_recv, spread_sem = refs
-    block = pl.program_id(0)
-    copies = exchange_all(tp_size, (w_exp_in_ref, w_exp_out_ref), pieces, moved_refs, move_send, move_recv)
-    copies += spread(ep_size, later_ref.at[later_ref.shape[0] - 1], by_kind(second_ref, ep_size), (spread_sem.at[0], spread_sem.at[1]))
-
-    @pl.when(block == 0)
-    def _():
-        loads = [pltpu.make_async_copy(w_in_ref, w_in_buf, load_sem.at[0]), pltpu.make_async_copy(w_out_ref, w_out_buf, load_sem.at[1])]
-        for load in loads:
-            load.start()
-        enter([('tp', tp_size), ('ep', ep_size)])
-        for copy in copies:
-            copy.start()
-        for load in loads:
-            load.wait()
-
-    parts, _, size = b_in_ref.shape
-    total = x_ref[...].astype(F32) + b_out_ref[...]
-    for part in range(parts):
-        cols = pl.ds(part * size, size)
-        inner = jnp.maximum(dot_t(normed_ref[...], w_in_buf[cols, :]) + b_in_ref[part], 0.0).astype(BF16)
-        total += jnp.dot(inner, w_out_buf[cols, :], preferred_element_type=F32)
-    o_ref[...] = total.astype(BF16)
-
-    @pl.when(block == pl.num_programs(0) - 1)
-    def _():
-        for copy in copies:
-            copy.wait()
-
-
-def dense_layer(x, normed, w_in, b_in, w_out, b_out, w_exp_in, w_exp_out, later, tp_size, ep_size, pieces, call_id):
-    tokens, width = x.shape
-    block_n = min(256, tokens)
-    _, _, cut, _ = later.shape
-    kinds = 4
-    second = jax.ShapeDtypeStruct((kinds, tp_size, ep_size // kinds, cut, width), BF16)
-    dma = DMA((len(pieces), tp_size - 1))
-    rows = pl.BlockSpec((block_n, width), lambda i: (i, 0))
-    return pl.pallas_call(
-        functools.partial(dense_body, tp_size, ep_size, pieces),
-        out_shape=(jax.ShapeDtypeStruct((tokens, width), BF16), *landings(tp_size, w_exp_in, pieces), second), grid=(tokens // block_n,),
-        in_specs=[rows, rows, HBM_SPEC, VMEM_SPEC, HBM_SPEC, VMEM_SPEC, HBM_SPEC, HBM_SPEC, HBM_SPEC],
-        out_specs=(rows, *[HBM_SPEC for _ in pieces], HBM_SPEC),
-        scratch_shapes=[pltpu.VMEM(w_in.shape, BF16), pltpu.VMEM(w_out.shape, BF16), DMA((2,)), dma, dma, DMA((2, ep_size))],
-        compiler_params=settings(call_id, grid=('arbitrary',)),
-        cost_estimate=cost(30),
-        name='dense_layer')(x, normed, w_in, b_in, w_out, b_out, w_exp_in, w_exp_out, later)
+        functools.partial(front_body, tp_size, ep_size, pieces, own_experts, head_dim),
+        out_shape=(jax.ShapeDtypeStruct((blocks, capacity), jnp.int32), jax.ShapeDtypeStruct((slots, 1), jnp.int32), jax.ShapeDtypeStruct((own_rows, seq, width), BF16),
+                   jax.ShapeDtypeStruct((slots, width), BF16), b_exp, *moved),
+        in_specs=[SMEM_SPEC] + [VMEM_SPEC] * 5 + [HBM_SPEC] * (4 + len(biases)), out_specs=[VMEM_SPEC] * 4 + [HBM_SPEC] * (1 + len(pieces)),
+        scratch_shapes=[vmem(tp_size, *biases[0].shape, dtype=F32), vmem(tp_size, *biases[1].shape, dtype=F32), vmem(tp_size, *biases[2].shape, dtype=F32), pack, pack,
+                        vmem(packs - 1, tp_size, cut, width), vmem(tp_size, ep_size, cut, width), vmem(tp_size, ep_size, cut, width), vmem(slots, 1, dtype=jnp.int32),
+                        vmem(num_experts, 3 * capacity, dtype=F32), vmem(3 * capacity, num_experts, dtype=F32), vmem(1, 3 * width, dtype=F32), vmem(seq, 3 * width), vmem(size, width),
+                        vmem(tp_size, own_rows, count, size, width), DMA, piece_dma, piece_dma, gather_dma, gather_dma] + [DMA((ep_size,))] * 4
+                       + [DMA((2, packs - 1, ep_size)), ring_dma, ring_dma],
+        compiler_params=settings(call_id, 62), cost_estimate=cost(100), name='front')(lens, index, gain, shift, b_out, b_fc2, x, w_in, w_out, own, *biases)
 
 
 def experts_body(tp_size, ep_size, early, late, dispatch_ref, early_refs, w_in_ref, w_out_ref, b_in_ref, b_out_ref, w_router_ref, other_ref, returned_ref, gates_ref,
@@ -482,8 +403,8 @@
                 device_id={'ep': peer}, device_id_type=MESH)
 
     def landing(piece):
-        chunk, which, start, rows = piece
-        return parts_buf.at[units.index((chunk, which)), :, pl.ds(start, rows)]
+        chunk, which, start, cols = piece
+        return parts_buf.at[units.index((chunk, which)), :, :, pl.ds(start, cols)]
 
     moves = {piece: exchange(tp_size, weights, piece, landing(piece), move_send.at[index], move_recv.at[index]) for index, piece in enumerate(late)}
     kept = [pltpu.make_async_copy(dispatch_ref.at[chunk, me], arrived_ref.at[chunk, me], local_sem.at[0, chunk]) for chunk in range(chunks)]
@@ -526,28 +447,30 @@
             return own_buf.at[unit[0], unit[1]]
         return parts_buf.at[units.index(unit), part - 1]
 
-    def give_back(chunk, slot, index):
+    def give_back(chunk, slot, index, cols):
         for half in range(2):
             peer = 2 * index + half
             distance = lax.rem(peer - me + ep_size, ep_size)
 
             @pl.when(distance == 0)
             def _():
-                pltpu.make_async_copy(out_buf.at[slot, peer], returned_ref.at[chunk, me], local_sem.at[4, chunk]).start()
+                pltpu.make_async_copy(out_buf.at[slot, peer, :, cols], returned_ref.at[chunk, me, :, cols], local_sem.at[4, chunk]).start()
 
             @pl.when(distance != 0)
             def _():
                 pltpu.make_async_remote_copy(
-                    src_ref=out_buf.at[slot, peer], dst_ref=returned_ref.at[chunk, me], send_sem=back_send.at[chunk, distance], recv_sem=back_recv.at[chunk, distance],
+                    src_ref=out_buf.at[slot, peer, :, cols], dst_ref=returned_ref.at[chunk, me, :, cols], send_sem=back_send.at[chunk, distance], recv_sem=back_recv.at[chunk, distance],
                     device_id={'ep': peer}, device_id_type=MESH).start()
 
-    def weights_here(unit):
-        owns[unit].wait()
-        for piece in early:
-            if piece[:2] == unit:
-                earlies[piece].wait()
+    def weights_here(chunk, which, cols=None):
+        unit = (chunk, which)
+        if cols is None or cols.start == 0:
+            owns[unit].wait()
+            for piece in early:
+                if piece[:2] == unit:
+                    earlies[piece].wait()
         for piece in late:
-            if piece[:2] == unit:
+            if piece[:2] == unit and (cols is None or piece[2] == cols.start):
                 for copy in moves[piece]:
                     copy.wait_recv()
 
@@ -566,7 +489,7 @@
         for distance in range(1, ep_size):
             sends[chunk, distance].wait_recv()
         kept[chunk].wait()
-        weights_here((chunk, 0))
+        weights_here(chunk, 0)
         before = chunk - out_buf.shape[0]
         if before >= 0:
             for copy in backs[before][:-1]:
@@ -581,23 +504,24 @@
                 return carry
 
             lax.fori_loop(0, ep_size // 2, first_product, 0)
-        weights_here((chunk, 1))
-
-        def rows(index, carry):
-            total = jnp.zeros((2 * slots, width), F32)
-            for part in range(tp_size):
-                inner = held[part][pl.ds(2 * index, 2)].reshape(2 * slots, width) if last else inner_part(chunk, index, part)
-                total += jnp.dot(inner, part_ref((chunk, 1), part)[...], preferred_element_type=F32)
-            out_buf[slot, pl.ds(2 * index, 2)] = (total + b_out_ref[expert_row(chunk), :]).astype(BF16).reshape(2, slots, width)
-
-            @pl.when(index > 0)
-            def _():
-                give_back(chunk, slot, index - 1)
-
-            return carry
-
-        lax.fori_loop(0, ep_size // 2, rows, 0)
-        give_back(chunk, slot, ep_size // 2 - 1)
+        for cols in ([pl.ds(0, width // 2), pl.ds(width // 2, width // 2)] if last else [pl.ds(0, width)]):
+            weights_here(chunk, 1, cols if last else None)
+
+            def rows(index, carry):
+                total = jnp.zeros((2 * slots, cols.size), F32)
+                for part in range(tp_size):
+                    inner = held[part][pl.ds(2 * index, 2)].reshape(2 * slots, width) if last else inner_part(chunk, index, part)
+                    total += jnp.dot(inner, part_ref((chunk, 1), part)[:, cols], preferred_element_type=F32)
+                out_buf[slot, pl.ds(2 * index, 2), :, cols] = (total + b_out_ref[expert_row(chunk), cols]).astype(BF16).reshape(2, slots, cols.size)
+
+                @pl.when(index > 0)
+                def _():
+                    give_back(chunk, slot, index - 1, cols)
+
+                return carry
+
+            lax.fori_loop(0, ep_size // 2, rows, 0)
+            give_back(chunk, slot, ep_size // 2 - 1, cols)
         backs[chunk] = []
         for distance in range(1, ep_size):
             peer = away('ep', ep_size, distance)
@@ -639,7 +563,7 @@
         name='experts')(dispatch, *early_weights, w_in, w_out, b_in, b_out, w_router, other)
 
 
-def combine_body(blocks, token_ref, slots_ref, gates_ref, o_ref, acc_ref, wide_ref):
+def combine_body(blocks, batch, token_ref, slots_ref, gates_ref, o_ref, acc_ref, wide_ref):
     block = pl.program_id(0)
     slots, width = slots_ref.shape
     step = o_ref.shape[0]
@@ -664,15 +588,15 @@
         base = block * slots
 
         def add(index, carry):
-            first = index * 16
-            places = [pl.ds(pl.multiple_of(token_ref[base + first + u], 8), 8) for u in range(16)]
-            start = pl.multiple_of(index * 128, 128)
-            new = [acc_ref[places[u], :] + wide_ref[pl.ds(start + u * 8, 8), :] for u in range(16)]
-            for u in range(16):
+            first = index * batch
+            places = [pl.ds(pl.multiple_of(token_ref[base + first + u], 8), 8) for u in range(batch)]
+            start = pl.multiple_of(first * 8, batch * 8)
+            new = [acc_ref[places[u], :] + wide_ref[pl.ds(start + u * 8, 8), :] for u in range(batch)]
+            for u in range(batch):
                 acc_ref[places[u], :] = new[u]
             return carry
 
-        lax.fori_loop(0, slots // 16, add, 0)
+        lax.fori_loop(0, slots // batch, add, 0)
 
     @pl.when(block >= blocks)
     def _():
@@ -690,6 +614,7 @@
 def combine(place, gates, outputs, tokens):
     count, slots, width = outputs.shape
     blocks = 4
+    batch = min(32, slots)
     slots = count * slots // blocks
     outputs = outputs.reshape(blocks, slots, width)
     step = tokens // 4
@@ -699,7 +624,7 @@
         out_specs=pl.BlockSpec((step, width), lambda b, *_: (jnp.maximum(b - blocks, 0), 0)),
         scratch_shapes=[pltpu.VMEM(((tokens + 32) * 8, 128), F32), pltpu.VMEM((slots * 8, 128), F32)])
     return pl.pallas_call(
-        functools.partial(combine_body, blocks),
+        functools.partial(combine_body, blocks, batch),
         out_shape=jax.ShapeDtypeStruct((tokens, width), BF16), grid_spec=grid_spec,
         compiler_params=settings(grid=('arbitrary',)),
         cost_estimate=cost(30),
@@ -818,7 +743,6 @@
         own_experts = local_experts // tp_size
         _, _, local_heads, head_dim = w_query.shape
         head_cols = local_heads * head_dim
-        own_rows = rows // tp_size
 
         def pack_attention(j):
             columns = [w[j].reshape(width, head_cols).T for w in (w_query, w_key, w_value)]
@@ -835,26 +759,16 @@
             size = width // (1 + len(part))
             return chunk, which, sum(part) * size, size
 
-        plan = ['210'], ['00', '01'], ['10'], ['11', '20'], ['211', '30', '31']
-        at_start, in_first, in_dense, in_second, in_experts = [[piece(code) for code in codes] for codes in plan]
+        plan = ['00', '01', '10', '11', '20', '210'], ['211', '30', '310', '311']
+        early, late = [[piece(code) for code in codes] for codes in plan]
         weights = w_exp_in, w_exp_out
-        place, source, other, pack, later, b_query, b_value, b_fc1, b_exp_in, *moved = start(
-            src_len, expert_idx.transpose(0, 2, 1), *weights, own, (b_query, b_value, b_fc1.reshape(1, -1), b_exp_in), num_experts, capacity, tp_size, ep_size, at_start, 4)
-
-        def attention(layer, hidden, pack, pieces, spreads):
-            return attention_layer(layer, hidden, own_rows, src_len, head_dim, ln_gain, ln_bias, pack.reshape(-1, width), b_query, b_value, b_attn_out, *weights, later,
-                                   tp_size, ep_size, pieces, spreads, layer)
-
-        hidden, normed, *landed, fc1_all, fc2_all = attention(0, x, pack, in_first, 2)
-        moved += landed
-        hidden, *landed, pack = dense_layer(hidden, normed, fc1_all.reshape(-1, width), b_fc1, fc2_all.reshape(-1, width), b_fc2.reshape(1, width), *weights, later, tp_size, ep_size, in_dense, 2)
-        moved += landed
-        hidden, normed, *landed = attention(1, hidden.reshape(own_rows, seq, width), pack, in_second, 0)
-        moved += landed
-        dispatch = dispatch_rows(source, normed, tp_size, 6).reshape(own_experts, ep_size, capacity, width)
-        outputs, gates = experts(dispatch, moved, *weights, b_exp_in, b_exp_out, w_router, other, tp_size, ep_size, at_start + in_first + in_dense + in_second, in_experts, 3)
+        biases = b_query.transpose(1, 0, 2), b_value.transpose(1, 0, 2), b_fc1.reshape(1, -1), b_exp_in
+        place, other, hidden, dispatch, b_exp_in, *moved = front(
+            src_len, expert_idx.transpose(0, 2, 1), ln_gain, ln_bias, b_attn_out, b_fc2.reshape(1, -1), x, *weights, own, biases, num_experts, capacity, head_dim, tp_size, ep_size, early, 0)
+        dispatch = dispatch.reshape(own_experts, ep_size, capacity, width)
+        outputs, gates = experts(dispatch, moved, *weights, b_exp_in, b_exp_out, w_router, other, tp_size, ep_size, early, late, 1)
         partial = combine(place.reshape(-1), gates, outputs.reshape(-1, capacity, width), tokens)
-        return finish(partial, hidden, tp_size, 5).reshape(rows, seq, width)
+        return finish(partial, hidden.reshape(-1, width), tp_size, 2).reshape(rows, seq, width)
 
     axes = {'g': ('dp', 'ep'), 'e': 'ep', 't': 'tp', '.': None}
 

time: 866 us -> 829 us (0.957)
  Pallas kernels: 843 us -> 811 us
    pallas_call x6 -> x2, Pallas kernels: 478 us -> 456 us  [the longest x1 429 us: front(): pl.pallas_call(functools.partial(front_body, tp_size, ep_size, pieces, ow...]
    pallas_call x1, Pallas kernels: 160 us -> 149 us  [experts(): pl.pallas_call(body, out_shape=(jax.ShapeDtypeStruct(dispatch.shape, BF16...]
where the time goes in v6:
time: 829 us; the launch traced here: 828 us
  Pallas kernels  811 us (98%)
  local copies, waits for them, and re-layouts  14.8 us (2%)
    pallas_call x1, Pallas kernels, front(): pl.pallas_call(functools.partial(front_body, tp_size, ep_size, pieces, ow...  429 us
    pallas_call x1, Pallas kernels, finish(): pl.pallas_call(functools.partial(finish_body, tp_size, count), out_shape=...  206 us
    pallas_call x1, Pallas kernels, experts(): pl.pallas_call(body, out_shape=(jax.ShapeDtypeStruct(dispatch.shape, BF16...  149 us
    pallas_call x1, Pallas kernels, combine(): pl.pallas_call(functools.partial(combine_body, blocks, batch), out_shape=...  26.9 us

profile of v6, /device:TPU:97, one launch (start us, length us, event | category | flops | bytes accessed | tf_op | source)
XLA Modules:
  0.0 828.1 jit_solution(9845176354020138484)
XLA Ops:
  0.0 0.0 copy-start
  0.0 0.0 copy-start.3
  0.0 0.0 copy-start.2
  0.0 1.4 reshape.19.refs_2_
  1.4 1.3 reshape.18.b_fc2_ref
  2.7 0.0 copy-done
  2.7 0.0 copy-start.4
  2.7 0.1 constant_dynamic-slice_fusion
  2.9 0.1 copy.23
  3.0 1.1 fusion.8
  4.1 0.0 copy-done.2
  4.2 0.0 copy-done.3
  4.2 0.0 copy-done.4
  4.3 1.2 dynamic-slice_bitcast_fusion
  5.5 0.3 fusion.7
  5.8 0.9 pad_maximum_fusion.own_ref
  6.7 428.9 %front.1 = (s32[32,128]{1,0:T(8,128)}, s32[4096,1]{1,0:T(8,128)}, bf16[2,1024,768]{2,1,0:T(8,128)(2,1)}, bf16[4096,768]{1,0:T(8,128)(2,1)}, f32[4,16,768]{2,1,0:...) custom-call(s32[8]{0:T(128)} %lens_ref.1, ...), custom_call_target="tpu_custom_call" | custom-call | flops 99999997952 | bytes 10000000 | tf_op jit(solution)/shard_map/front/pallas_call | solution.py:376
  435.6 148.8 %experts.1 = (bf16[4,8,128,768]{3,2,1,0:T(8,128)(2,1)}, f32[4096,1]{1,0:T(8,128)}) custom-call(bf16[4,8,128,768]{3,2,1,0:T(8,128)(2,1)} %bitcast.50, bf16[3,768,768]{2,1,0:T(8,128)(2,1)} %get-tuple-element.20.refs_0_, bf16[3,768,768]{2,1,0:T(8,128)(2,1)} %get-tuple-element.21.refs_1_, bf16[3,768,768]{2,1,0:T(8,128)(2,1)} %get-tuple-element.22.refs_2_, ...), custom_call_target="tpu_custom_call" | custom-call | flops 30000001024 | bytes 10000000 | tf_op jit(solution)/shard_map/experts/pallas_call | solution.py:554
  584.3 26.9 %combine.1.partial_ref = bf16[8192,768]{1,0:T(8,128)(2,1)} custom-call(s32[4096]{0:T(1024)} %bitcast.53, bf16[4,1024,768]{2,1,0:T(8,128)(2,1)} %bitcast.51, f32[4096,1]{1,0:T(8,128)} %get-tuple-element.29.gates_ref), custom_call_target="tpu_custom_call" | custom-call | flops 30000001024 | bytes 10000000 | tf_op jit(solution)/shard_map/combine/pallas_call | solution.py:626
  611.3 206.2 %finish.1 = bf16[8192,768]{1,0:T(8,128)(2,1)} custom-call(bf16[8192,768]{1,0:T(8,128)(2,1)} %combine.1.partial_ref, bf16[2048,768]{1,0:T(8,128)(2,1)} %bitcast.52), custom_call_target="tpu_custom_call" | custom-call | flops 30000001024 | bytes 10000000 | tf_op jit(solution)/shard_map/finish/pallas_call | solution.py:724
  817.5 0.0 copy-start.1
  817.5 10.6 %copy.25 = bf16[8,1024,768]{2,1,0:T(8,128)(2,1)} copy(bf16[8,1024,768]{2,1,0:T(8,128)(2,1)} %bitcast.37) | data formatting | bytes 25165824
  828.1 0.0 copy-done.1
  (3 shorter events, 0.1 us)
Async XLA Ops:
  0.0 2.7 copy-start
  0.0 4.2 copy-start.3
  0.0 4.1 copy-start.2
  2.7 1.5 copy-start.4
  817.5 10.6 %copy-start.1 = (bf16[768,768]{1,0:T(8,128)(2,1)S(1)}, bf16[768,768]{1,0:T(8,128)(2,1)}, u32[]{:S(2)}) copy-start(bf16[768,768]{1,0:T(8,128)(2,1)} %param.33) | copy-start | bytes 3538948

commit v7 on v6

--- a/solution.py
+++ b/solution.py
@@ -76,17 +76,18 @@
     return [jax.ShapeDtypeStruct((tp_size - 1, weight.shape[1], cols), BF16) for _, _, _, cols in pieces]
 
 
-def route_tables(lens_ref, index_ref, total_ref, total_t_ref):
+def route_tables(own_experts, tp_size, ep_size, lens_ref, index_ref, table_ref, total_ref):
     rows, _, seq = index_ref.shape
     step = min(512, seq)
     per_row = seq // step
-    experts_count, wide = total_ref.shape
+    wide, experts_count = total_ref.shape
     slots = wide // 3
+    lanes = table_ref.shape[1]
+    mine = lax.axis_index('tp')
     ids = lax.broadcasted_iota(jnp.int32, (experts_count, 1), 0)
     slot_ids = lax.broadcasted_iota(jnp.int32, (slots, 1), 0)
     before = (lax.broadcasted_iota(jnp.int32, (step, step), 0) < lax.broadcasted_iota(jnp.int32, (step, step), 1)).astype(BF16)
     total_ref[...] = jnp.zeros_like(total_ref)
-    total_t_ref[...] = jnp.zeros_like(total_t_ref)
     count = jnp.zeros((experts_count, 1), F32)
     for choice in range(2):
         def block(index, count):
@@ -104,8 +105,14 @@
             parts = [jnp.where(at_slot, value.astype(F32), 0.0).astype(BF16) for value in (token & 255, (token >> 8) + 1, other)]
             values = jnp.concatenate(parts, axis=0)
             hot16 = hot.astype(BF16)
-            total_ref[...] += dot_t(hot16, values)
-            total_t_ref[...] += dot_t(values, hot16)
+            total_ref[...] += dot_t(values, hot16)
+            local = own_experts * tp_size
+            own = (lax.rem(chosen, tp_size) == mine) & (slot < slots)
+            line = (lax.div(lax.rem(chosen, local), tp_size) * ep_size + lax.div(chosen, local)) * slots + slot
+            line = jnp.where(own, line, own_experts * ep_size * slots)
+            for part in range(step // lanes):
+                at = (choice * rows * per_row + index) * (step // lanes) + part
+                table_ref[pl.ds(at, 1), :] = line[:, part * lanes:(part + 1) * lanes]
             return count + jnp.sum(hot, axis=1, keepdims=True)
 
         count = lax.fori_loop(0, rows * per_row, block, count)
@@ -127,9 +134,9 @@
 
 def front_body(tp_size, ep_size, pieces, own_experts, head_dim, lens_ref, index_ref, gain_ref, shift_ref, b_out_ref, b_fc2_ref, x_ref, w_in_ref, w_out_ref, own_ref, *refs):
     biases, refs = refs[:4], refs[4:]
-    place_ref, other_ref, hidden_ref, o_ref, b_exp_ref, *refs = refs
+    table_ref, other_ref, hidden_ref, o_ref, b_exp_ref, *refs = refs
     moved_refs, refs = refs[:len(pieces)], refs[len(pieces):]
-    (b_query_ref, b_value_ref, b_fc1_ref, first_ref, second_ref, later_ref, fc1_ref, fc2_ref, source_ref, total_ref, total_t_ref, bias_buf, qkv_ref, context_ref, all_buf,
+    (b_query_ref, b_value_ref, b_fc1_ref, first_ref, second_ref, later_ref, fc1_ref, fc2_ref, source_ref, total_ref, bias_buf, qkv_ref, context_ref, all_buf,
      load_sem, move_send, move_recv, tp_send, tp_recv, row_send, row_recv, pair_send, pair_recv, spread_sem, ring_send, ring_recv) = refs
     mine = lax.axis_index('tp')
     me = lax.axis_index('ep')
@@ -185,19 +192,15 @@
         for copy in copies:
             copy.start()
 
-    route_tables(lens_ref, index_ref, total_ref, total_t_ref)
-    rows, _, _ = index_ref.shape
-    experts_count, wide = total_ref.shape
+    route_tables(own_experts, tp_size, ep_size, lens_ref, index_ref, table_ref, total_ref)
+    wide, experts_count = total_ref.shape
     slots = wide // 3
     lane = lax.broadcasted_iota(jnp.int32, (1, experts_count), 1)
 
     def take(index, carry):
         chunk = index // ep_size
         expert = (index % ep_size) * (own_experts * tp_size) + chunk * tp_size + mine
-        line = total_ref[pl.ds(expert, 1), :].astype(jnp.int32)
-        low, high = line[:, :slots], line[:, slots:2 * slots]
-        place_ref[pl.ds(index, 1), :] = 8 * jnp.where(high > 0, 256 * (high - 1) + low, rows * seq)
-        column = jnp.sum(jnp.where(lane == expert, total_t_ref[...], 0.0), axis=1, keepdims=True).astype(jnp.int32)
+        column = jnp.sum(jnp.where(lane == expert, total_ref[...], 0.0), axis=1, keepdims=True).astype(jnp.int32)
         low, high, other = column[:slots], column[slots:2 * slots], column[2 * slots:]
         at = span(index, slots)
         source_ref[at, :] = jnp.where(high > 0, 256 * (high - 1) + low, -1)
@@ -290,14 +293,17 @@
         for copy in copies:
             copy.wait()
 
+    def as_row(ref):
+        return jnp.concatenate([ref[pl.ds(part, 1), :] for part in range(ref.shape[0])], axis=1)
+
     def dense(index, carry):
         row, rows = index // blocks, span(index % blocks, size)
         value = hidden_ref[row, rows, :].astype(F32)
         normed = norm(value, 1)
-        total = value + b_fc2_ref[...]
+        total = value + as_row(b_fc2_ref)
         for part in range(tp_size):
             cols = fc1_ref[part].reshape(-1, width)
-            inner = jnp.maximum(dot_t(normed, cols) + b_fc1_ref[part], 0.0).astype(BF16)
+            inner = jnp.maximum(dot_t(normed, cols) + as_row(b_fc1_ref.at[part]), 0.0).astype(BF16)
             total += jnp.dot(inner, fc2_ref[part].reshape(-1, width), preferred_element_type=F32)
         hidden_ref[row, rows, :] = total.astype(BF16)
         return carry
@@ -375,12 +381,12 @@
     piece_dma, gather_dma, ring_dma = DMA((len(pieces), tp_size - 1)), DMA((packs + len(biases), tp_size)), DMA((own_rows, tp_size - 1, count))
     return pl.pallas_call(
         functools.partial(front_body, tp_size, ep_size, pieces, own_experts, head_dim),
-        out_shape=(jax.ShapeDtypeStruct((blocks, capacity), jnp.int32), jax.ShapeDtypeStruct((slots, 1), jnp.int32), jax.ShapeDtypeStruct((own_rows, seq, width), BF16),
+        out_shape=(jax.ShapeDtypeStruct((2 * rows * seq // 128, 128), jnp.int32), jax.ShapeDtypeStruct((slots, 1), jnp.int32), jax.ShapeDtypeStruct((own_rows, seq, width), BF16),
                    jax.ShapeDtypeStruct((slots, width), BF16), b_exp, *moved),
         in_specs=[SMEM_SPEC] + [VMEM_SPEC] * 5 + [HBM_SPEC] * (4 + len(biases)), out_specs=[VMEM_SPEC] * 4 + [HBM_SPEC] * (1 + len(pieces)),
         scratch_shapes=[vmem(tp_size, *biases[0].shape, dtype=F32), vmem(tp_size, *biases[1].shape, dtype=F32), vmem(tp_size, *biases[2].shape, dtype=F32), pack, pack,
                         vmem(packs - 1, tp_size, cut, width), vmem(tp_size, ep_size, cut, width), vmem(tp_size, ep_size, cut, width), vmem(slots, 1, dtype=jnp.int32),
-                        vmem(num_experts, 3 * capacity, dtype=F32), vmem(3 * capacity, num_experts, dtype=F32), vmem(1, 3 * width, dtype=F32), vmem(seq, 3 * width), vmem(size, width),
+                        vmem(3 * capacity, num_experts, dtype=F32), vmem(1, 3 * width, dtype=F32), vmem(seq, 3 * width), vmem(size, width),
                         vmem(tp_size, own_rows, count, size, width), DMA, piece_dma, piece_dma, gather_dma, gather_dma] + [DMA((ep_size,))] * 4
                        + [DMA((2, packs - 1, ep_size)), ring_dma, ring_dma],
         compiler_params=settings(call_id, 62), cost_estimate=cost(100), name='front')(lens, index, gain, shift, b_out, b_fc2, x, w_in, w_out, own, *biases)
@@ -504,7 +510,7 @@
                 return carry
 
             lax.fori_loop(0, ep_size // 2, first_product, 0)
-        for cols in ([pl.ds(0, width // 2), pl.ds(width // 2, width // 2)] if last else [pl.ds(0, width)]):
+        for cols in ([pl.ds(piece[2], piece[3]) for piece in late if piece[:2] == (chunk, 1)] if last else [pl.ds(0, width)]):
             weights_here(chunk, 1, cols if last else None)
 
             def rows(index, carry):
@@ -563,125 +569,100 @@
         name='experts')(dispatch, *early_weights, w_in, w_out, b_in, b_out, w_router, other)
 
 
-def combine_body(blocks, batch, token_ref, slots_ref, gates_ref, o_ref, acc_ref, wide_ref):
-    block = pl.program_id(0)
-    slots, width = slots_ref.shape
-    step = o_ref.shape[0]
-    lanes = 128
-    piece = min(128, slots)
-
-    @pl.when(block == 0)
-    def _():
-        def clear(index, carry):
-            acc_ref[span(index, lanes), :] = jnp.zeros((lanes, lanes), F32)
-            return carry
-        lax.fori_loop(0, acc_ref.shape[0] // lanes, clear, 0)
-
-    @pl.when(block < blocks)
-    def _():
-        def widen(index, carry):
-            rows = span(index, piece)
-            for col in range(width // lanes):
-                wide_ref[pl.ds(index * (piece * 8) + col, piece, stride=8), :] = slots_ref[rows, col * lanes:(col + 1) * lanes].astype(F32) * gates_ref[rows, :]
-            return carry
-        lax.fori_loop(0, slots // piece, widen, 0)
-        base = block * slots
-
-        def add(index, carry):
-            first = index * batch
-            places = [pl.ds(pl.multiple_of(token_ref[base + first + u], 8), 8) for u in range(batch)]
-            start = pl.multiple_of(first * 8, batch * 8)
-            new = [acc_ref[places[u], :] + wide_ref[pl.ds(start + u * 8, 8), :] for u in range(batch)]
-            for u in range(batch):
-                acc_ref[places[u], :] = new[u]
-            return carry
-
-        lax.fori_loop(0, slots // batch, add, 0)
-
-    @pl.when(block >= blocks)
-    def _():
-        first = (block - blocks) * (step * 8)
-        some = min(256, step)
-
-        def write(index, carry):
-            rows = span(index, some)
-            for col in range(width // lanes):
-                o_ref[rows, col * lanes:(col + 1) * lanes] = acc_ref[pl.ds(first + index * (some * 8) + col, some, stride=8), :].astype(BF16)
-            return carry
-        lax.fori_loop(0, step // some, write, 0)
-
-
-def combine(place, gates, outputs, tokens):
-    count, slots, width = outputs.shape
-    blocks = 4
-    batch = min(32, slots)
-    slots = count * slots // blocks
-    outputs = outputs.reshape(blocks, slots, width)
-    step = tokens // 4
-    grid_spec = pltpu.PrefetchScalarGridSpec(
-        num_scalar_prefetch=1, grid=(blocks + tokens // step,),
-        in_specs=[pl.BlockSpec((None, slots, width), lambda b, *_: (jnp.minimum(b, blocks - 1), 0, 0)), pl.BlockSpec((slots, 1), lambda b, *_: (jnp.minimum(b, blocks - 1), 0))],
-        out_specs=pl.BlockSpec((step, width), lambda b, *_: (jnp.maximum(b - blocks, 0), 0)),
-        scratch_shapes=[pltpu.VMEM(((tokens + 32) * 8, 128), F32), pltpu.VMEM((slots * 8, 128), F32)])
-    return pl.pallas_call(
-        functools.partial(combine_body, blocks, batch),
-        out_shape=jax.ShapeDtypeStruct((tokens, width), BF16), grid_spec=grid_spec,
-        compiler_params=settings(grid=('arbitrary',)),
-        cost_estimate=cost(30),
-        name='combine')(place, outputs, gates)
-
-
-def finish_body(tp_size, count, partial_ref, hidden_ref, o_ref, partial_buf, hidden_buf, sum_buf, own_buf, load_sem, sum_send, sum_recv, out_send, out_recv):
+def finish_body(tp_size, count, table_ref, gates_ref, outputs_ref, hidden_ref, o_ref, slots_buf, wide_ref, stage_ref, first_buf, hidden_buf, sum_buf, own_buf,
+                load_sem, slots_sem, sum_send, sum_recv, out_send, out_recv):
     me = lax.axis_index('tp')
-    own_tokens, _ = hidden_ref.shape
+    own_tokens, width = hidden_ref.shape
+    tokens = tp_size * own_tokens
     size = own_tokens // (2 * count)
     hops = tp_size - 1
-    step_to = (1, tp_size - 1)
+    lanes = 128
+    columns = [slice(start, start + lanes) for start in range(0, width, lanes)]
 
     def rows(way, chunk, index):
         return pl.ds(pl.multiple_of(chunk * own_tokens + (way * count + index) * size, size), size)
 
     def behind(way, distance):
         return away('tp', tp_size, (tp_size - distance) % tp_size if way == 0 else distance % tp_size)
+
+    def ahead(way):
+        return {'tp': away('tp', tp_size, 1 if way == 0 else tp_size - 1)}
 
     def send_sum(way, hop, index, src_ref):
         return pltpu.make_async_remote_copy(
             src_ref=src_ref, dst_ref=sum_buf.at[way, hop, index], send_sem=sum_send.at[way, hop, index], recv_sem=sum_recv.at[way, hop, index],
-            device_id={'tp': away('tp', tp_size, step_to[way])}, device_id_type=MESH)
+            device_id=ahead(way), device_id_type=MESH)
 
     def send_out(way, hop, index, src_ref, chunk):
         return pltpu.make_async_remote_copy(
             src_ref=src_ref, dst_ref=o_ref.at[rows(way, chunk, index)], send_sem=out_send.at[way, hop, index], recv_sem=out_recv.at[way, hop, index],
-            device_id={'tp': away('tp', tp_size, step_to[way])}, device_id_type=MESH)
-
-    loads = [pltpu.make_async_copy(partial_ref, partial_buf, load_sem.at[0]), pltpu.make_async_copy(hidden_ref, hidden_buf, load_sem.at[1])]
-    for load in loads:
+            device_id=ahead(way), device_id_type=MESH)
+
+    slots = outputs_ref.shape[0]
+    parts = slots_sem.shape[0]
+    part_slots = slots // parts
+    piece = min(128, part_slots)
+    loads = [pltpu.make_async_copy(outputs_ref.at[span(part, part_slots)], slots_buf.at[span(part, part_slots)], slots_sem.at[part]) for part in range(parts)]
+    load_hidden = pltpu.make_async_copy(hidden_ref, hidden_buf, load_sem.at[2])
+    for load in loads + [load_hidden]:
         load.start()
     enter([('tp', tp_size)])
+    wide_ref[slots] = jnp.zeros(wide_ref.shape[1:], F32)
+
+    def widen(index, carry):
+        at = span(index, piece)
+        for column, cols in enumerate(columns):
+            wide_ref[at, column, :] = slots_buf[at, cols].astype(F32) * gates_ref[at, :]
+        return carry
+
+    for part, load in enumerate(loads):
+        load.wait()
+        lax.fori_loop(part * (part_slots // piece), (part + 1) * (part_slots // piece), widen, 0)
+
+    def combine(way, chunk, index):
+        base = chunk * own_tokens + (way * count + index) * size
+        batch = 16
+
+        def some(part, carry):
+            first = part * batch
+            for u in range(batch):
+                slot_of = [table_ref[choice * tokens + base + first + u] for choice in range(2)]
+                stage_ref[way, pl.ds(pl.multiple_of((first + u) * 8, 8), 8), :] = wide_ref[slot_of[0]] + wide_ref[slot_of[1]]
+            return carry
+
+        lax.fori_loop(0, size // batch, some, 0)
+
+    def staged(way, column):
+        return stage_ref[way, pl.ds(column, size, stride=8), :]
 
     def first(index, carry):
         for way in range(2):
-            send_sum(way, 0, index, partial_ref.at[rows(way, behind(way, 1), index)]).start()
+            combine(way, behind(way, 1), index)
+            for column, cols in enumerate(columns):
+                first_buf[way, index, :, cols] = staged(way, column).astype(BF16)
+        for way in range(2):
+            send_sum(way, 0, index, first_buf.at[way, index]).start()
         return carry
 
     lax.fori_loop(0, count, first, 0)
-    for load in loads:
-        load.wait()
+    load_hidden.wait()
 
     def keep(way, index):
-        own = own_buf.at[way, index]
-        return pltpu.make_async_copy(own, o_ref.at[rows(way, me, index)], load_sem.at[2 + way])
+        return pltpu.make_async_copy(own_buf.at[way, index], o_ref.at[rows(way, me, index)], load_sem.at[way])
 
     for hop in range(1, tp_size):
         def add(index, carry):
             for way in range(2):
+                combine(way, behind(way, hop + 1), index)
+            for way in range(2):
                 send_sum(way, hop - 1, index, sum_buf.at[way, hop - 1, index]).wait_recv()
-                total = sum_buf[way, hop - 1, index].astype(F32) + partial_buf[rows(way, behind(way, hop + 1), index), :].astype(F32)
-                if hop < hops:
-                    sum_buf[way, hop - 1, index] = total.astype(BF16)
-                else:
-                    own_rows = pl.ds(pl.multiple_of((way * count + index) * size, size), size)
-                    own_buf[way, index] = (total.astype(BF16).astype(F32) + hidden_buf[own_rows, :].astype(F32)).astype(BF16)
+                own_rows = pl.ds(pl.multiple_of((way * count + index) * size, size), size)
+                for column, cols in enumerate(columns):
+                    total = (sum_buf[way, hop - 1, index, :, cols].astype(F32) + staged(way, column)).astype(BF16)
+                    if hop < hops:
+                        sum_buf[way, hop - 1, index, :, cols] = total
+                    else:
+                        own_buf[way, index, :, cols] = (total.astype(F32) + hidden_buf[own_rows, cols].astype(F32)).astype(BF16)
             for way in range(2):
                 if hop < hops:
                     send_sum(way, hop, index, sum_buf.at[way, hop - 1, index]).start()
@@ -715,19 +696,24 @@
     lax.fori_loop(0, count, drain, 0)
 
 
-def finish(partial, hidden, tp_size, call_id):
-    tokens, width = partial.shape
+def finish(table, gates, outputs, hidden, tp_size, call_id):
+    slots, width = outputs.shape
     own_tokens = hidden.shape[0]
     size = min(256, own_tokens // 2)
     count = own_tokens // (2 * size)
     hops = tp_size - 1
+    pieces = (2, count, size, width)
+    ring = DMA((2, hops, count))
+
+    def vmem(*shape, dtype=BF16):
+        return pltpu.VMEM(shape, dtype)
+
     return pl.pallas_call(
-        functools.partial(finish_body, tp_size, count), out_shape=jax.ShapeDtypeStruct(partial.shape, BF16), in_specs=[HBM_SPEC, HBM_SPEC], out_specs=HBM_SPEC,
-        scratch_shapes=[pltpu.VMEM(partial.shape, BF16), pltpu.VMEM(hidden.shape, BF16), pltpu.VMEM((2, hops, count, size, width), BF16), pltpu.VMEM((2, count, size, width), BF16),
-                        DMA((4,)), DMA((2, hops, count)), DMA((2, hops, count)), DMA((2, hops, count)), DMA((2, hops, count))],
-        compiler_params=settings(call_id),
-        cost_estimate=cost(30),
-        name='finish')(partial, hidden)
+        functools.partial(finish_body, tp_size, count), out_shape=jax.ShapeDtypeStruct((tp_size * own_tokens, width), BF16),
+        in_specs=[SMEM_SPEC, VMEM_SPEC, HBM_SPEC, HBM_SPEC], out_specs=HBM_SPEC,
+        scratch_shapes=[vmem(slots, width), vmem(slots + 1, 8, 128, dtype=F32), vmem(2, size * 8, 128, dtype=F32), vmem(*pieces), vmem(own_tokens, width),
+                        vmem(2, hops, *pieces[1:]), vmem(*pieces), DMA((3,)), DMA((4,)), ring, ring, ring, ring],
+        compiler_params=settings(call_id), cost_estimate=cost(100), name='finish')(table, gates, outputs, hidden)
 
 
 def solution(mesh):
@@ -756,19 +742,18 @@
 
         def piece(code):
             chunk, which, *part = map(int, code)
-            size = width // (1 + len(part))
+            size = width // 3 if part else width
             return chunk, which, sum(part) * size, size
 
-        plan = ['00', '01', '10', '11', '20', '210'], ['211', '30', '310', '311']
+        plan = ['00', '01', '10', '11', '20', '210'], ['211', '212', '30', '310', '311', '312']
         early, late = [[piece(code) for code in codes] for codes in plan]
         weights = w_exp_in, w_exp_out
-        biases = b_query.transpose(1, 0, 2), b_value.transpose(1, 0, 2), b_fc1.reshape(1, -1), b_exp_in
-        place, other, hidden, dispatch, b_exp_in, *moved = front(
-            src_len, expert_idx.transpose(0, 2, 1), ln_gain, ln_bias, b_attn_out, b_fc2.reshape(1, -1), x, *weights, own, biases, num_experts, capacity, head_dim, tp_size, ep_size, early, 0)
+        biases = b_query.transpose(1, 0, 2), b_value.transpose(1, 0, 2), b_fc1.reshape(-1, 128), b_exp_in
+        table, other, hidden, dispatch, b_exp_in, *moved = front(
+            src_len, expert_idx.transpose(0, 2, 1), ln_gain, ln_bias, b_attn_out, b_fc2.reshape(-1, 128), x, *weights, own, biases, num_experts, capacity, head_dim, tp_size, ep_size, early, 0)
         dispatch = dispatch.reshape(own_experts, ep_size, capacity, width)
         outputs, gates = experts(dispatch, moved, *weights, b_exp_in, b_exp_out, w_router, other, tp_size, ep_size, early, late, 1)
-        partial = combine(place.reshape(-1), gates, outputs.reshape(-1, capacity, width), tokens)
-        return finish(partial, hidden.reshape(-1, width), tp_size, 2).reshape(rows, seq, width)
+        return finish(table.reshape(-1), gates, outputs.reshape(-1, width), hidden.reshape(-1, width), tp_size, 2).reshape(rows, seq, width)
 
     axes = {'g': ('dp', 'ep'), 'e': 'ep', 't': 'tp', '.': None}
 

time: 829 us -> 811 us (0.978)
  Pallas kernels: 811 us -> 795 us
    pallas_call x1 -> x0, Pallas kernels: 26.9 us -> none  [combine(): pl.pallas_call(functools.partial(combine_body, blocks, batch), out_shape=...]
    pallas_call x1, Pallas kernels: 206 us -> 220 us  [finish(): pl.pallas_call(functools.partial(finish_body, tp_size, count), out_shape=...]
where the time goes in v7:
time: 811 us; the launch traced here: 810 us
  Pallas kernels  795 us (98%)
  local copies, waits for them, and re-layouts  13.5 us (2%)
    pallas_call x1, Pallas kernels, front(): pl.pallas_call(functools.partial(front_body, tp_size, ep_size, pieces, ow...  421 us
    pallas_call x1, Pallas kernels, finish(): pl.pallas_call(functools.partial(finish_body, tp_size, count), out_shape=...  220 us
    pallas_call x1, Pallas kernels, experts(): pl.pallas_call(body, out_shape=(jax.ShapeDtypeStruct(dispatch.shape, BF16...  154 us

profile of v7, /device:TPU:97, one launch (start us, length us, event | category | flops | bytes accessed | tf_op | source)
XLA Modules:
  0.0 810.5 jit_solution(10964778708800480919)
XLA Ops:
  0.0 0.0 copy-start
  0.0 0.0 copy-start.3
  0.0 0.0 copy-start.2
  0.0 1.4 copy-done
  1.4 0.0 copy-start.4
  1.5 0.1 constant_dynamic-slice_fusion
  1.6 0.1 copy.23
  1.7 1.1 fusion.8
  2.8 0.0 copy-done.2
  2.9 0.0 copy-done.3
  2.9 0.0 copy-done.4
  3.0 1.2 dynamic-slice_bitcast_fusion
  4.2 0.3 fusion.7
  4.5 0.9 pad_maximum_fusion.own_ref
  5.4 420.7 %front.1 = (s32[128,128]{1,0:T(8,128)}, s32[4096,1]{1,0:T(8,128)}, bf16[2,1024,768]{2,1,0:T(8,128)(2,1)}, bf16[4096,768]{1,0:T(8,128)(2,1)}, f32[4,16,768]{2,1,0...) custom-call(s32[8]{0:T(128)} %lens_ref.1, ...), custom_call_target="tpu_custom_call" | custom-call | flops 99999997952 | bytes 10000000 | tf_op jit(solution)/shard_map/front/pallas_call | solution.py:382
  426.1 153.8 %experts.1 = (bf16[4,8,128,768]{3,2,1,0:T(8,128)(2,1)}, f32[4096,1]{1,0:T(8,128)}) custom-call(bf16[4,8,128,768]{3,2,1,0:T(8,128)(2,1)} %bitcast.54, bf16[3,768,768]{2,1,0:T(8,128)(2,1)} %get-tuple-element.20.refs_0_, bf16[3,768,768]{2,1,0:T(8,128)(2,1)} %get-tuple-element.21.refs_1_, bf16[3,768,768]{2,1,0:T(8,128)(2,1)} %get-tuple-element.22.refs_2_, ...), custom_call_target="tpu_custom_call" | custom-call | flops 30000001024 | bytes 10000000 | tf_op jit(solution)/shard_map/experts/pallas_call | solution.py:560
  579.9 220.0 %finish.1 = bf16[8192,768]{1,0:T(8,128)(2,1)} custom-call(s32[16384]{0:T(1024)} %bitcast.57, f32[4096,1]{1,0:T(8,128)} %get-tuple-element.28.gates_ref, bf16[4096,768]{1,0:T(8,128)(2,1)} %bitcast.55, bf16[2048,768]{1,0:T(8,128)(2,1)} %bitcast.56), custom_call_target="tpu_custom_call" | custom-call | flops 99999997952 | bytes 10000000 | tf_op jit(solution)/shard_map/finish/pallas_call | solution.py:711
  799.9 0.0 copy-start.1
  799.9 10.6 %copy.25 = bf16[8,1024,768]{2,1,0:T(8,128)(2,1)} copy(bf16[8,1024,768]{2,1,0:T(8,128)(2,1)} %bitcast.39) | data formatting | bytes 25165824
  810.5 0.0 copy-done.1
  (3 shorter events, 0.1 us)
Async XLA Ops:
  0.0 1.4 copy-start
  0.0 2.9 copy-start.3
  0.0 2.8 copy-start.2
  1.4 1.5 copy-start.4
  799.9 10.6 %copy-start.1 = (bf16[768,768]{1,0:T(8,128)(2,1)S(1)}, bf16[768,768]{1,0:T(8,128)(2,1)}, u32[]{:S(2)}) copy-start(bf16[768,768]{1,0:T(8,128)(2,1)} %param.33) | copy-start | bytes 3538948

commit v8 on v7

--- a/solution.py
+++ b/solution.py
@@ -134,9 +134,9 @@
 
 def front_body(tp_size, ep_size, pieces, own_experts, head_dim, lens_ref, index_ref, gain_ref, shift_ref, b_out_ref, b_fc2_ref, x_ref, w_in_ref, w_out_ref, own_ref, *refs):
     biases, refs = refs[:4], refs[4:]
-    table_ref, other_ref, hidden_ref, o_ref, b_exp_ref, *refs = refs
+    table_ref, o_ref, other_out, hidden_out, b_exp_ref, *refs = refs
     moved_refs, refs = refs[:len(pieces)], refs[len(pieces):]
-    (b_query_ref, b_value_ref, b_fc1_ref, first_ref, second_ref, later_ref, fc1_ref, fc2_ref, source_ref, total_ref, bias_buf, qkv_ref, context_ref, all_buf,
+    (other_ref, hidden_ref, b_query_ref, b_value_ref, b_fc1_ref, first_ref, second_ref, later_ref, fc1_ref, fc2_ref, source_ref, total_ref, bias_buf, qkv_ref, context_ref, all_buf,
      load_sem, move_send, move_recv, tp_send, tp_recv, row_send, row_recv, pair_send, pair_recv, spread_sem, ring_send, ring_recv) = refs
     mine = lax.axis_index('tp')
     me = lax.axis_index('ep')
@@ -149,18 +149,34 @@
     pairs = [(own_ref.at[0], view(me).at[mine])]
     pairs += [(bias, whole.at[mine]) for bias, whole in zip(biases, (b_query_ref, b_value_ref, b_fc1_ref, b_exp_ref))]
     pairs += [(own_ref.at[1 + index], later_ref.at[index, mine]) for index in range(later_ref.shape[0])]
+    near = (1, tp_size - 1)
     gathers = []
     for index, (src, dst) in enumerate(pairs):
+        far = range(2, tp_size - 1) if 0 < index <= len(biases) else ()
         gathers.append([pltpu.make_async_copy(src, dst, tp_send.at[index, 0])] + [pltpu.make_async_remote_copy(
             src_ref=src, dst_ref=dst, send_sem=tp_send.at[index, distance], recv_sem=tp_recv.at[index, distance],
-            device_id={'tp': away('tp', tp_size, distance)}, device_id_type=MESH) for distance in (1, tp_size - 1, *range(2, tp_size - 1))])
-    load_x = pltpu.make_async_copy(x_ref.at[pl.ds(mine * own_rows, own_rows)], hidden_ref, load_sem)
+            device_id={'tp': away('tp', tp_size, distance)}, device_id_type=MESH) for distance in (*near, *far)])
+
+    def relay(index, where):
+        half = own_ref.shape[1] // 2
+        copies = []
+        for way, distance in enumerate(near):
+            piece = where(away('tp', tp_size, tp_size - distance)).at[pl.ds(way * half, half)]
+            copies.append(pltpu.make_async_remote_copy(
+                src_ref=piece, dst_ref=piece, send_sem=tp_send.at[index, 2 + 2 * way], recv_sem=tp_recv.at[index, 2 + 2 * way],
+                device_id={'tp': away('tp', tp_size, distance)}, device_id_type=MESH))
+        return copies
+
+    load_x = pltpu.make_async_copy(x_ref.at[pl.ds(mine * own_rows, own_rows)], hidden_ref, load_sem.at[0])
+    keep_other = pltpu.make_async_copy(other_ref, other_out, load_sem.at[1])
+    keep_hidden = pltpu.make_async_copy(hidden_ref, hidden_out, load_sem.at[2])
     load_x.start()
     enter([('tp', tp_size), ('ep', ep_size)])
     for copies in gathers:
         for copy in copies:
             copy.start()
-    for copy in moves:
+    one = tp_size - 1
+    for copy in moves[-one:]:
         copy.start()
 
     cores = 2
@@ -180,10 +196,24 @@
 
     for copy in gathers[0]:
         copy.wait()
+    first_relay = relay(0, lambda part: view(me).at[part])
+    for copy in first_relay:
+        copy.start()
+    for copies in gathers[1:]:
+        for copy in copies:
+            copy.wait()
+    later_relays = [relay(1 + len(biases) + index, lambda part, index=index: later_ref.at[index, part]) for index in range(later_ref.shape[0])]
+    for copies in later_relays:
+        for copy in copies:
+            copy.start()
+    for copy in moves[:-one]:
+        copy.start()
+    for copy in first_relay:
+        copy.wait()
     for step in steps:
         along(step).start()
     across(0).start()
-    for copies in gathers[1:]:
+    for copies in later_relays:
         for copy in copies:
             copy.wait()
     views = [lambda part: fc1_ref.at[:, part], lambda part: fc2_ref.at[:, part], by_kind(second_ref, ep_size)]
@@ -312,6 +342,8 @@
     for copy in spreads[2]:
         copy.wait()
     attention(1, second_ref)
+    keep_hidden.start()
+    keep_other.start()
 
     token = lax.broadcasted_iota(jnp.int32, (1, size), 1)
     slot_count, _ = o_ref.shape
@@ -357,7 +389,7 @@
         return carry
 
     lax.fori_loop(0, count, drain, 0)
-    for copy in moves:
+    for copy in [*moves, keep_hidden, keep_other]:
         copy.wait()
 
 
@@ -378,16 +410,16 @@
     moved = landings(tp_size, w_in, pieces)
     b_exp = jax.ShapeDtypeStruct((tp_size,) + biases[3].shape, F32)
     pack = vmem(packs, tp_size, per, cut, width)
-    piece_dma, gather_dma, ring_dma = DMA((len(pieces), tp_size - 1)), DMA((packs + len(biases), tp_size)), DMA((own_rows, tp_size - 1, count))
+    piece_dma, gather_dma, ring_dma = DMA((len(pieces), tp_size - 1)), DMA((packs + len(biases), tp_size + 1)), DMA((own_rows, tp_size - 1, count))
     return pl.pallas_call(
         functools.partial(front_body, tp_size, ep_size, pieces, own_experts, head_dim),
-        out_shape=(jax.ShapeDtypeStruct((2 * rows * seq // 128, 128), jnp.int32), jax.ShapeDtypeStruct((slots, 1), jnp.int32), jax.ShapeDtypeStruct((own_rows, seq, width), BF16),
-                   jax.ShapeDtypeStruct((slots, width), BF16), b_exp, *moved),
-        in_specs=[SMEM_SPEC] + [VMEM_SPEC] * 5 + [HBM_SPEC] * (4 + len(biases)), out_specs=[VMEM_SPEC] * 4 + [HBM_SPEC] * (1 + len(pieces)),
-        scratch_shapes=[vmem(tp_size, *biases[0].shape, dtype=F32), vmem(tp_size, *biases[1].shape, dtype=F32), vmem(tp_size, *biases[2].shape, dtype=F32), pack, pack,
+        out_shape=(jax.ShapeDtypeStruct((2 * rows * seq // 128, 128), jnp.int32), jax.ShapeDtypeStruct((slots, width), BF16), jax.ShapeDtypeStruct((slots, 1), jnp.int32),
+                   jax.ShapeDtypeStruct((own_rows, seq, width), BF16), b_exp, *moved),
+        in_specs=[SMEM_SPEC] + [VMEM_SPEC] * 5 + [HBM_SPEC] * (4 + len(biases)), out_specs=[VMEM_SPEC] * 2 + [HBM_SPEC] * (3 + len(pieces)),
+        scratch_shapes=[vmem(slots, 1, dtype=jnp.int32), vmem(own_rows, seq, width), vmem(tp_size, *biases[0].shape, dtype=F32), vmem(tp_size, *biases[1].shape, dtype=F32), vmem(tp_size, *biases[2].shape, dtype=F32), pack, pack,
                         vmem(packs - 1, tp_size, cut, width), vmem(tp_size, ep_size, cut, width), vmem(tp_size, ep_size, cut, width), vmem(slots, 1, dtype=jnp.int32),
                         vmem(3 * capacity, num_experts, dtype=F32), vmem(1, 3 * width, dtype=F32), vmem(seq, 3 * width), vmem(size, width),
-                        vmem(tp_size, own_rows, count, size, width), DMA, piece_dma, piece_dma, gather_dma, gather_dma] + [DMA((ep_size,))] * 4
+                        vmem(tp_size, own_rows, count, size, width), DMA((3,)), piece_dma, piece_dma, gather_dma, gather_dma] + [DMA((ep_size,))] * 4
                        + [DMA((2, packs - 1, ep_size)), ring_dma, ring_dma],
         compiler_params=settings(call_id, 62), cost_estimate=cost(100), name='front')(lens, index, gain, shift, b_out, b_fc2, x, w_in, w_out, own, *biases)
 
@@ -608,11 +640,12 @@
         load.start()
     enter([('tp', tp_size)])
     wide_ref[slots] = jnp.zeros(wide_ref.shape[1:], F32)
+    flat_ref = wide_ref.reshape((slots + 1) * 8, lanes)
 
     def widen(index, carry):
         at = span(index, piece)
         for column, cols in enumerate(columns):
-            wide_ref[at, column, :] = slots_buf[at, cols].astype(F32) * gates_ref[at, :]
+            flat_ref[pl.ds(index * (piece * 8) + column, piece, stride=8), :] = slots_buf[at, cols].astype(F32) * gates_ref[at, :]
         return carry
 
     for part, load in enumerate(loads):
@@ -749,7 +782,7 @@
         early, late = [[piece(code) for code in codes] for codes in plan]
         weights = w_exp_in, w_exp_out
         biases = b_query.transpose(1, 0, 2), b_value.transpose(1, 0, 2), b_fc1.reshape(-1, 128), b_exp_in
-        table, other, hidden, dispatch, b_exp_in, *moved = front(
+        table, dispatch, other, hidden, b_exp_in, *moved = front(
             src_len, expert_idx.transpose(0, 2, 1), ln_gain, ln_bias, b_attn_out, b_fc2.reshape(-1, 128), x, *weights, own, biases, num_experts, capacity, head_dim, tp_size, ep_size, early, 0)
         dispatch = dispatch.reshape(own_experts, ep_size, capacity, width)
         outputs, gates = experts(dispatch, moved, *weights, b_exp_in, b_exp_out, w_router, other, tp_size, ep_size, early, late, 1)

time: 811 us -> 800 us (0.986)
  Pallas kernels: 795 us -> 783 us
where the time goes in v8:
time: 800 us; the launch traced here: 799 us
  Pallas kernels  783 us (98%)
  local copies, waits for them, and re-layouts  13.5 us (2%)
    pallas_call x1, Pallas kernels, front(): pl.pallas_call(functools.partial(front_body, tp_size, ep_size, pieces, ow...  413 us
    pallas_call x1, Pallas kernels, finish(): pl.pallas_call(functools.partial(finish_body, tp_size, count), out_shape=...  217 us
    pallas_call x1, Pallas kernels, experts(): pl.pallas_call(body, out_shape=(jax.ShapeDtypeStruct(dispatch.shape, BF16...  154 us

profile of v8, /device:TPU:97, one launch (start us, length us, event | category | flops | bytes accessed | tf_op | source)
XLA Modules:
  0.0 799.3 jit_solution(10064838849164949991)
XLA Ops:
  0.0 0.0 copy-start
  0.0 0.0 copy-start.3
  0.0 0.0 copy-start.2
  0.0 1.4 copy-done
  1.4 0.0 copy-start.4
  1.5 0.1 constant_dynamic-slice_fusion
  1.6 0.1 copy.23
  1.7 1.1 fusion.8
  2.8 0.0 copy-done.2
  2.9 0.0 copy-done.3
  2.9 0.0 copy-done.4
  3.0 1.2 dynamic-slice_bitcast_fusion
  4.2 0.3 fusion.7
  4.5 0.9 pad_maximum_fusion.own_ref
  5.4 413.0 %front.1 = (s32[128,128]{1,0:T(8,128)}, bf16[4096,768]{1,0:T(8,128)(2,1)}, s32[4096,1]{1,0:T(8,128)}, bf16[2,1024,768]{2,1,0:T(8,128)(2,1)}, f32[4,16,768]{2,1,0...) custom-call(s32[8]{0:T(128)} %lens_ref.1, ...), custom_call_target="tpu_custom_call" | custom-call | flops 99999997952 | bytes 10000000 | tf_op jit(solution)/shard_map/front/pallas_call | solution.py:414
  418.4 153.8 %experts.1 = (bf16[4,8,128,768]{3,2,1,0:T(8,128)(2,1)}, f32[4096,1]{1,0:T(8,128)}) custom-call(bf16[4,8,128,768]{3,2,1,0:T(8,128)(2,1)} %bitcast.54, bf16[3,768,768]{2,1,0:T(8,128)(2,1)} %get-tuple-element.20.refs_0_, bf16[3,768,768]{2,1,0:T(8,128)(2,1)} %get-tuple-element.21.refs_1_, bf16[3,768,768]{2,1,0:T(8,128)(2,1)} %get-tuple-element.22.refs_2_, ...), custom_call_target="tpu_custom_call" | custom-call | flops 30000001024 | bytes 10000000 | tf_op jit(solution)/shard_map/experts/pallas_call | solution.py:592
  572.1 216.6 %finish.1 = bf16[8192,768]{1,0:T(8,128)(2,1)} custom-call(s32[16384]{0:T(1024)} %bitcast.57, f32[4096,1]{1,0:T(8,128)} %get-tuple-element.28.gates_ref, bf16[4096,768]{1,0:T(8,128)(2,1)} %bitcast.55, bf16[2048,768]{1,0:T(8,128)(2,1)} %bitcast.56), custom_call_target="tpu_custom_call" | custom-call | flops 99999997952 | bytes 10000000 | tf_op jit(solution)/shard_map/finish/pallas_call | solution.py:744
  788.7 0.0 copy-start.1
  788.7 10.6 %copy.25 = bf16[8,1024,768]{2,1,0:T(8,128)(2,1)} copy(bf16[8,1024,768]{2,1,0:T(8,128)(2,1)} %bitcast.39) | data formatting | bytes 25165824
  799.3 0.0 copy-done.1
  (3 shorter events, 0.1 us)
Async XLA Ops:
  0.0 1.4 copy-start
  0.0 2.9 copy-start.3
  0.0 2.8 copy-start.2
  1.4 1.5 copy-start.4
  788.7 10.6 %copy-start.1 = (bf16[768,768]{1,0:T(8,128)(2,1)S(1)}, bf16[768,768]{1,0:T(8,128)(2,1)}, u32[]{:S(2)}) copy-start(bf16[768,768]{1,0:T(8,128)(2,1)} %param.33) | copy-start | bytes 3538948

commit v9 on v8

--- a/solution.py
+++ b/solution.py
@@ -176,7 +176,7 @@
         for copy in copies:
             copy.start()
     one = tp_size - 1
-    for copy in moves[-one:]:
+    for copy in moves[:one]:
         copy.start()
 
     cores = 2
@@ -206,7 +206,7 @@
     for copies in later_relays:
         for copy in copies:
             copy.start()
-    for copy in moves[:-one]:
+    for copy in moves[one:-one]:
         copy.start()
     for copy in first_relay:
         copy.wait()
@@ -342,8 +342,6 @@
     for copy in spreads[2]:
         copy.wait()
     attention(1, second_ref)
-    keep_hidden.start()
-    keep_other.start()
 
     token = lax.broadcasted_iota(jnp.int32, (1, size), 1)
     slot_count, _ = o_ref.shape
@@ -370,6 +368,8 @@
         return carry
 
     lax.fori_loop(1, count, own, 0)
+    keep_hidden.start()
+    keep_other.start()
     for hop in range(1, tp_size):
         def arrive(index, carry):
             chunks = [behind(way, hop) for way in range(ways)]
@@ -381,6 +381,9 @@
             return carry
 
         lax.fori_loop(0, count, arrive, 0)
+        if hop == hops - 1:
+            for copy in moves[-one:]:
+                copy.start()
 
     def drain(index, carry):
         for way in range(ways):
@@ -424,8 +427,8 @@
         compiler_params=settings(call_id, 62), cost_estimate=cost(100), name='front')(lens, index, gain, shift, b_out, b_fc2, x, w_in, w_out, own, *biases)
 
 
-def experts_body(tp_size, ep_size, early, late, dispatch_ref, early_refs, w_in_ref, w_out_ref, b_in_ref, b_out_ref, w_router_ref, other_ref, returned_ref, gates_ref,
-                 sent_buf, arrived_ref, parts_buf, own_buf, out_buf, local_sem, send_sem, recv_sem, back_send, back_recv, move_send, move_recv):
+def experts_body(tp_size, ep_size, early, late, dispatch_ref, early_refs, w_in_ref, w_out_ref, b_in_ref, b_out_ref, w_router_ref, other_in, returned_ref, gates_out,
+                 other_ref, gates_ref, sent_buf, arrived_ref, parts_buf, own_buf, out_buf, local_sem, send_sem, recv_sem, back_send, back_recv, move_send, move_recv):
     chunks, _, slots, width = arrived_ref.shape
     me = lax.axis_index('ep')
     mine = lax.axis_index('tp')
@@ -469,7 +472,11 @@
     def load(chunk):
         return pltpu.make_async_copy(dispatch_ref.at[chunk], sent_buf.at[chunk % 2], local_sem.at[5, chunk % 2])
 
+    load_other = pltpu.make_async_copy(other_in, other_ref, local_sem.at[5, 2])
+    keep_gates = pltpu.make_async_copy(gates_ref, gates_out, local_sem.at[5, 3])
     load(0).start()
+    load_other.start()
+    load_other.wait()
     for chunk in range(chunks):
         if chunk + 1 < chunks:
             load(chunk + 1).start()
@@ -568,6 +575,7 @@
                 device_id={'ep': peer}, device_id_type=MESH))
         backs[chunk].append(pltpu.make_async_copy(out_buf.at[slot, me], returned_ref.at[chunk, me], local_sem.at[4, chunk]))
 
+    keep_gates.start()
     for chunk in range(chunks):
         for distance in range(1, ep_size):
             sends[chunk, distance].wait_send()
@@ -580,6 +588,7 @@
     for piece in late:
         for copy in moves[piece]:
             copy.wait_send()
+    keep_gates.wait()
 
 
 def experts(dispatch, early_weights, w_in, w_out, b_in, b_out, w_router, other, tp_size, ep_size, early, late, call_id):
@@ -591,8 +600,8 @@
 
     return pl.pallas_call(
         body, out_shape=(jax.ShapeDtypeStruct(dispatch.shape, BF16), jax.ShapeDtypeStruct(other.shape, F32)),
-        in_specs=[HBM_SPEC] * (3 + len(early)) + [VMEM_SPEC] * 4, out_specs=(HBM_SPEC, VMEM_SPEC),
-        scratch_shapes=[pltpu.VMEM((2,) + dispatch.shape[1:], BF16), pltpu.VMEM(dispatch.shape, BF16), pltpu.VMEM((2 * chunks, tp_size - 1, width, hidden), BF16),
+        in_specs=[HBM_SPEC] * (3 + len(early)) + [VMEM_SPEC] * 3 + [HBM_SPEC], out_specs=(HBM_SPEC, HBM_SPEC),
+        scratch_shapes=[pltpu.VMEM(other.shape, jnp.int32), pltpu.VMEM(other.shape, F32), pltpu.VMEM((2,) + dispatch.shape[1:], BF16), pltpu.VMEM(dispatch.shape, BF16), pltpu.VMEM((2 * chunks, tp_size - 1, width, hidden), BF16),
                         pltpu.VMEM((chunks, 2, width, hidden), BF16), pltpu.VMEM((2, ep_size, slots, width), BF16),
                         DMA((6, max(chunks, len(early)))), DMA((chunks, ep_size)), DMA((chunks, ep_size)), DMA((chunks, ep_size)), DMA((chunks, ep_size)),
                         DMA((len(late), tp_size - 1)), DMA((len(late), tp_size - 1))],
@@ -601,7 +610,7 @@
         name='experts')(dispatch, *early_weights, w_in, w_out, b_in, b_out, w_router, other)
 
 
-def finish_body(tp_size, count, table_ref, gates_ref, outputs_ref, hidden_ref, o_ref, slots_buf, wide_ref, stage_ref, first_buf, hidden_buf, sum_buf, own_buf,
+def finish_body(tp_size, count, table_in, gates_in, outputs_ref, hidden_ref, o_ref, table_ref, gates_ref, slots_buf, wide_ref, stage_ref, first_buf, hidden_buf, sum_buf, own_buf,
                 load_sem, slots_sem, sum_send, sum_recv, out_send, out_recv):
     me = lax.axis_index('tp')
     own_tokens, width = hidden_ref.shape
@@ -636,7 +645,9 @@
     piece = min(128, part_slots)
     loads = [pltpu.make_async_copy(outputs_ref.at[span(part, part_slots)], slots_buf.at[span(part, part_slots)], slots_sem.at[part]) for part in range(parts)]
     load_hidden = pltpu.make_async_copy(hidden_ref, hidden_buf, load_sem.at[2])
-    for load in loads + [load_hidden]:
+    load_gates = pltpu.make_async_copy(gates_in, gates_ref, load_sem.at[3])
+    load_table = pltpu.make_async_copy(table_in, table_ref, load_sem.at[4])
+    for load in [load_gates, *loads, load_table, load_hidden]:
         load.start()
     enter([('tp', tp_size)])
     wide_ref[slots] = jnp.zeros(wide_ref.shape[1:], F32)
@@ -648,6 +659,7 @@
             flat_ref[pl.ds(index * (piece * 8) + column, piece, stride=8), :] = slots_buf[at, cols].astype(F32) * gates_ref[at, :]
         return carry
 
+    load_gates.wait()
     for part, load in enumerate(loads):
         load.wait()
         lax.fori_loop(part * (part_slots // piece), (part + 1) * (part_slots // piece), widen, 0)
@@ -673,10 +685,10 @@
             combine(way, behind(way, 1), index)
             for column, cols in enumerate(columns):
                 first_buf[way, index, :, cols] = staged(way, column).astype(BF16)
-        for way in range(2):
             send_sum(way, 0, index, first_buf.at[way, index]).start()
         return carry
 
+    load_table.wait()
     lax.fori_loop(0, count, first, 0)
     load_hidden.wait()
 
@@ -743,9 +755,9 @@
 
     return pl.pallas_call(
         functools.partial(finish_body, tp_size, count), out_shape=jax.ShapeDtypeStruct((tp_size * own_tokens, width), BF16),
-        in_specs=[SMEM_SPEC, VMEM_SPEC, HBM_SPEC, HBM_SPEC], out_specs=HBM_SPEC,
-        scratch_shapes=[vmem(slots, width), vmem(slots + 1, 8, 128, dtype=F32), vmem(2, size * 8, 128, dtype=F32), vmem(*pieces), vmem(own_tokens, width),
-                        vmem(2, hops, *pieces[1:]), vmem(*pieces), DMA((3,)), DMA((4,)), ring, ring, ring, ring],
+        in_specs=[HBM_SPEC] * 4, out_specs=HBM_SPEC,
+        scratch_shapes=[pltpu.SMEM(table.shape, jnp.int32), vmem(slots, 1, dtype=F32), vmem(slots, width), vmem(slots + 1, 8, 128, dtype=F32), vmem(2, size * 8, 128, dtype=F32), vmem(*pieces), vmem(own_tokens, width),
+                        vmem(2, hops, *pieces[1:]), vmem(*pieces), DMA((5,)), DMA((4,)), ring, ring, ring, ring],
         compiler_params=settings(call_id), cost_estimate=cost(100), name='finish')(table, gates, outputs, hidden)
 
 
@@ -778,7 +790,7 @@
             size = width // 3 if part else width
             return chunk, which, sum(part) * size, size
 
-        plan = ['00', '01', '10', '11', '20', '210'], ['211', '212', '30', '310', '311', '312']
+        plan = ['210', '00', '01', '10', '11', '200', '201', '202'], ['211', '212', '30', '310', '311', '312']
         early, late = [[piece(code) for code in codes] for codes in plan]
         weights = w_exp_in, w_exp_out
         biases = b_query.transpose(1, 0, 2), b_value.transpose(1, 0, 2), b_fc1.reshape(-1, 128), b_exp_in

time: 800 us -> 800 us (level)
  no operation moved by 1% of the time
where the time goes in v9:
time: 800 us
  Pallas kernels  783 us (98%)
  local copies, waits for them, and re-layouts  14.3 us (2%)
    pallas_call x1, Pallas kernels, front(): pl.pallas_call(functools.partial(front_body, tp_size, ep_size, pieces, ow...  418 us
    pallas_call x1, Pallas kernels, finish(): pl.pallas_call(functools.partial(finish_body, tp_size, count), out_shape=...  214 us
    pallas_call x1, Pallas kernels, experts(): pl.pallas_call(body, out_shape=(jax.ShapeDtypeStruct(dispatch.shape, BF16...  151 us

profile of v9, /device:TPU:97, one launch (start us, length us, event | category | flops | bytes accessed | tf_op | source)
XLA Modules:
  0.0 799.9 jit_solution(14510999437114630582)
XLA Ops:
  0.0 0.0 copy-start
  0.0 0.0 copy-start.2
  0.0 1.3 copy-done
  1.3 0.1 constant_dynamic-slice_fusion
  1.4 0.1 copy.23
  1.5 0.0 copy-start.3
  1.6 1.2 fusion.8
  2.7 0.0 copy-done.2
  2.7 0.0 copy-start.4
  2.8 0.0 copy-done.3
  2.8 1.0 copy-done.4
  3.8 1.2 dynamic-slice_bitcast_fusion
  5.0 0.3 fusion.7
  5.3 0.9 pad_maximum_fusion.own_ref
  6.2 417.6 %front.1 = (s32[128,128]{1,0:T(8,128)}, bf16[4096,768]{1,0:T(8,128)(2,1)}, s32[4096,1]{1,0:T(8,128)}, bf16[2,1024,768]{2,1,0:T(8,128)(2,1)}, f32[4,16,768]{2,1,0...) custom-call(s32[8]{0:T(128)} %lens_ref.1, ...), custom_call_target="tpu_custom_call" | custom-call | flops 99999997952 | bytes 10000000 | tf_op jit(solution)/shard_map/front/pallas_call | solution.py:417
  423.8 151.2 %experts.1 = (bf16[4,8,128,768]{3,2,1,0:T(8,128)(2,1)}, f32[4096,1]{1,0:T(8,128)}) custom-call(bf16[4,8,128,768]{3,2,1,0:T(8,128)(2,1)} %bitcast.54, bf16[3,768,256]{2,1,0:T(8,128)(2,1)} %get-tuple-element.22.refs_0_, bf16[3,768,768]{2,1,0:T(8,128)(2,1)} %get-tuple-element.23.refs_1_, bf16[3,768,768]{2,1,0:T(8,128)(2,1)} %get-tuple-element.24.refs_2_, ...), custom_call_target="tpu_custom_call" | custom-call | flops 30000001024 | bytes 10000000 | tf_op jit(solution)/shard_map/experts/pallas_call | solution.py:601
  575.0 214.3 %finish.1 = bf16[8192,768]{1,0:T(8,128)(2,1)} custom-call(s32[16384]{0:T(1024)} %bitcast.57, f32[4096,1]{1,0:T(8,128)} %get-tuple-element.32.gates_in, bf16[4096,768]{1,0:T(8,128)(2,1)} %bitcast.55, bf16[2048,768]{1,0:T(8,128)(2,1)} %bitcast.56), custom_call_target="tpu_custom_call" | custom-call | flops 99999997952 | bytes 10000000 | tf_op jit(solution)/shard_map/finish/pallas_call | solution.py:756
  789.3 0.0 copy-start.1
  789.3 10.6 %copy.25 = bf16[8,1024,768]{2,1,0:T(8,128)(2,1)} copy(bf16[8,1024,768]{2,1,0:T(8,128)(2,1)} %bitcast.39) | data formatting | bytes 25165824
  799.9 0.0 copy-done.1
  (3 shorter events, 0.1 us)
Async XLA Ops:
  0.0 1.3 copy-start
  0.0 2.7 copy-start.2
  1.5 1.2 copy-start.3
  2.7 1.1 copy-start.4
  789.3 10.6 %copy-start.1 = (bf16[768,768]{1,0:T(8,128)(2,1)S(1)}, bf16[768,768]{1,0:T(8,128)(2,1)}, u32[]{:S(2)}) copy-start(bf16[768,768]{1,0:T(8,128)(2,1)} %param.33) | copy-start | bytes 3538948

commit v10 on v9

--- a/solution.py
+++ b/solution.py
@@ -118,13 +118,21 @@
         count = lax.fori_loop(0, rows * per_row, block, count)
 
 
-def spread(ep_size, src_ref, view, sems):
+def spread(ep_size, src_ref, view, sems, landed=False):
+    cores = 2
     me = lax.axis_index('ep')
-    send_sem, recv_sem = sems
-    copies = [pltpu.make_async_remote_copy(
-        src_ref=src_ref, dst_ref=view(me), send_sem=send_sem.at[distance], recv_sem=recv_sem.at[distance],
-        device_id={'ep': away('ep', ep_size, distance)}, device_id_type=MESH) for distance in range(1, ep_size)]
-    return copies + [pltpu.make_async_copy(src_ref, view(me), send_sem.at[0])]
+    count = ep_size // cores
+
+    def send(src, dst, slot, device):
+        return pltpu.make_async_remote_copy(src_ref=src, dst_ref=dst, send_sem=sems[0].at[slot], recv_sem=sems[1].at[slot], device_id={'ep': device}, device_id_type=MESH)
+
+    along = [send(src_ref, view(me), step, away('ep', ep_size, cores * step)) for step in range(1, count)]
+    across = []
+    for step in range(count):
+        part = view(away('ep', ep_size, ep_size - cores * step))
+        across.append(send(part if step else src_ref, part, count + step, me + 1 - cores * lax.rem(me, cores)))
+    kept = [] if landed else [pltpu.make_async_copy(src_ref, view(me), sems[0].at[0])]
+    return along, across, kept
 
 
 def by_kind(ref, ep_size):
@@ -137,7 +145,7 @@
     table_ref, o_ref, other_out, hidden_out, b_exp_ref, *refs = refs
     moved_refs, refs = refs[:len(pieces)], refs[len(pieces):]
     (other_ref, hidden_ref, b_query_ref, b_value_ref, b_fc1_ref, first_ref, second_ref, later_ref, fc1_ref, fc2_ref, source_ref, total_ref, bias_buf, qkv_ref, context_ref, all_buf,
-     load_sem, move_send, move_recv, tp_send, tp_recv, row_send, row_recv, pair_send, pair_recv, spread_sem, ring_send, ring_recv) = refs
+     load_sem, move_send, move_recv, tp_send, tp_recv, spread_sem, ring_send, ring_recv) = refs
     mine = lax.axis_index('tp')
     me = lax.axis_index('ep')
     own_rows, seq, width = hidden_ref.shape
@@ -179,21 +187,10 @@
     for copy in moves[:one]:
         copy.start()
 
-    cores = 2
-    steps = range(1, ep_size // cores)
-    other_core = me + 1 - cores * lax.rem(me, cores)
-
-    def along(step):
-        return pltpu.make_async_remote_copy(
-            src_ref=view(me), dst_ref=view(me), send_sem=row_send.at[step], recv_sem=row_recv.at[step],
-            device_id={'ep': away('ep', ep_size, cores * step)}, device_id_type=MESH)
-
-    def across(step):
-        part = view(away('ep', ep_size, ep_size - cores * step))
-        return pltpu.make_async_remote_copy(
-            src_ref=part, dst_ref=part, send_sem=pair_send.at[step], recv_sem=pair_recv.at[step],
-            device_id={'ep': other_core}, device_id_type=MESH)
-
+    def sems(index):
+        return spread_sem.at[0, index], spread_sem.at[1, index]
+
+    along, across, _ = spread(ep_size, view(me), view, sems(0), True)
     for copy in gathers[0]:
         copy.wait()
     first_relay = relay(0, lambda part: view(me).at[part])
@@ -210,16 +207,15 @@
         copy.start()
     for copy in first_relay:
         copy.wait()
-    for step in steps:
-        along(step).start()
-    across(0).start()
+    for copy in [*along, across[0]]:
+        copy.start()
     for copies in later_relays:
         for copy in copies:
             copy.wait()
     views = [lambda part: fc1_ref.at[:, part], lambda part: fc2_ref.at[:, part], by_kind(second_ref, ep_size)]
-    spreads = [spread(ep_size, later_ref.at[index], where, (spread_sem.at[0, index], spread_sem.at[1, index])) for index, where in enumerate(views)]
-    for copies in spreads:
-        for copy in copies:
+    spreads = [spread(ep_size, later_ref.at[index], where, sems(1 + index)) for index, where in enumerate(views)]
+    for later_along, later_across, kept in spreads:
+        for copy in [*later_along, later_across[0], *kept]:
             copy.start()
 
     route_tables(own_experts, tp_size, ep_size, lens_ref, index_ref, table_ref, total_ref)
@@ -237,12 +233,12 @@
         other_ref[at, :] = other
         return carry
 
-    for step in steps:
-        along(step).wait()
-        across(step).start()
+    for copy, onward in zip(along, across[1:]):
+        copy.wait()
+        onward.start()
     lax.fori_loop(0, own_experts * ep_size, take, 0)
-    for step in range(ep_size // cores):
-        across(step).wait()
+    for copy in across:
+        copy.wait()
     load_x.wait()
 
     hops = tp_size - 1
@@ -319,8 +315,14 @@
 
     attention(0, first_ref)
 
-    for copies in spreads[:2]:
-        for copy in copies:
+    for later_along, later_across, kept in spreads:
+        for copy, onward in zip(later_along, later_across[1:]):
+            copy.wait()
+            onward.start()
+        for copy in kept:
+            copy.wait()
+    for _, later_across, _ in spreads[:2]:
+        for copy in later_across:
             copy.wait()
 
     def as_row(ref):
@@ -339,7 +341,7 @@
         return carry
 
     lax.fori_loop(0, own_rows * blocks, dense, 0)
-    for copy in spreads[2]:
+    for copy in spreads[2][1]:
         copy.wait()
     attention(1, second_ref)
 
@@ -422,8 +424,7 @@
         scratch_shapes=[vmem(slots, 1, dtype=jnp.int32), vmem(own_rows, seq, width), vmem(tp_size, *biases[0].shape, dtype=F32), vmem(tp_size, *biases[1].shape, dtype=F32), vmem(tp_size, *biases[2].shape, dtype=F32), pack, pack,
                         vmem(packs - 1, tp_size, cut, width), vmem(tp_size, ep_size, cut, width), vmem(tp_size, ep_size, cut, width), vmem(slots, 1, dtype=jnp.int32),
                         vmem(3 * capacity, num_experts, dtype=F32), vmem(1, 3 * width, dtype=F32), vmem(seq, 3 * width), vmem(size, width),
-                        vmem(tp_size, own_rows, count, size, width), DMA((3,)), piece_dma, piece_dma, gather_dma, gather_dma] + [DMA((ep_size,))] * 4
-                       + [DMA((2, packs - 1, ep_size)), ring_dma, ring_dma],
+                        vmem(tp_size, own_rows, count, size, width), DMA((3,)), piece_dma, piece_dma, gather_dma, gather_dma, DMA((2, packs, ep_size)), ring_dma, ring_dma],
         compiler_params=settings(call_id, 62), cost_estimate=cost(100), name='front')(lens, index, gain, shift, b_out, b_fc2, x, w_in, w_out, own, *biases)
 
 

time: 800 us -> 791 us (0.989)
  Pallas kernels: 783 us -> 774 us
    pallas_call x1, Pallas kernels: 418 us -> 408 us  [front(): pl.pallas_call(functools.partial(front_body, tp_size, ep_size, pieces, ow...]
where the time goes in v10:
time: 791 us
  Pallas kernels  774 us (98%)
  local copies, waits for them, and re-layouts  14.3 us (2%)
    pallas_call x1, Pallas kernels, front(): pl.pallas_call(functools.partial(front_body, tp_size, ep_size, pieces, ow...  408 us
    pallas_call x1, Pallas kernels, finish(): pl.pallas_call(functools.partial(finish_body, tp_size, count), out_shape=...  216 us
    pallas_call x1, Pallas kernels, experts(): pl.pallas_call(body, out_shape=(jax.ShapeDtypeStruct(dispatch.shape, BF16...  151 us

profile of v10, /device:TPU:97, one launch (start us, length us, event | category | flops | bytes accessed | tf_op | source)
XLA Modules:
  0.0 791.0 jit_solution(4171668036462991611)
XLA Ops:
  0.0 0.0 copy-start
  0.0 0.0 copy-start.2
  0.0 1.3 copy-done
  1.3 0.1 constant_dynamic-slice_fusion
  1.4 0.1 copy.23
  1.5 0.0 copy-start.3
  1.6 1.2 fusion.8
  2.7 0.0 copy-done.2
  2.7 0.0 copy-start.4
  2.8 0.0 copy-done.3
  2.8 1.0 copy-done.4
  3.8 1.2 dynamic-slice_bitcast_fusion
  5.0 0.3 fusion.7
  5.3 0.9 pad_maximum_fusion.own_ref
  6.2 407.7 %front.1 = (s32[128,128]{1,0:T(8,128)}, bf16[4096,768]{1,0:T(8,128)(2,1)}, s32[4096,1]{1,0:T(8,128)}, bf16[2,1024,768]{2,1,0:T(8,128)(2,1)}, f32[4,16,768]{2,1,0...) custom-call(s32[8]{0:T(128)} %lens_ref.1, ...), custom_call_target="tpu_custom_call" | custom-call | flops 99999997952 | bytes 10000000 | tf_op jit(solution)/shard_map/front/pallas_call | solution.py:419
  414.0 150.6 %experts.1 = (bf16[4,8,128,768]{3,2,1,0:T(8,128)(2,1)}, f32[4096,1]{1,0:T(8,128)}) custom-call(bf16[4,8,128,768]{3,2,1,0:T(8,128)(2,1)} %bitcast.54, bf16[3,768,256]{2,1,0:T(8,128)(2,1)} %get-tuple-element.22.refs_0_, bf16[3,768,768]{2,1,0:T(8,128)(2,1)} %get-tuple-element.23.refs_1_, bf16[3,768,768]{2,1,0:T(8,128)(2,1)} %get-tuple-element.24.refs_2_, ...), custom_call_target="tpu_custom_call" | custom-call | flops 30000001024 | bytes 10000000 | tf_op jit(solution)/shard_map/experts/pallas_call | solution.py:602
  564.5 215.9 %finish.1 = bf16[8192,768]{1,0:T(8,128)(2,1)} custom-call(s32[16384]{0:T(1024)} %bitcast.57, f32[4096,1]{1,0:T(8,128)} %get-tuple-element.32.gates_in, bf16[4096,768]{1,0:T(8,128)(2,1)} %bitcast.55, bf16[2048,768]{1,0:T(8,128)(2,1)} %bitcast.56), custom_call_target="tpu_custom_call" | custom-call | flops 99999997952 | bytes 10000000 | tf_op jit(solution)/shard_map/finish/pallas_call | solution.py:757
  780.5 0.0 copy-start.1
  780.5 10.6 %copy.25 = bf16[8,1024,768]{2,1,0:T(8,128)(2,1)} copy(bf16[8,1024,768]{2,1,0:T(8,128)(2,1)} %bitcast.39) | data formatting | bytes 25165824
  791.0 0.0 copy-done.1
  (3 shorter events, 0.1 us)
Async XLA Ops:
  0.0 1.3 copy-start
  0.0 2.7 copy-start.2
  1.5 1.2 copy-start.3
  2.7 1.1 copy-start.4
  780.5 10.6 %copy-start.1 = (bf16[768,768]{1,0:T(8,128)(2,1)S(1)}, bf16[768,768]{1,0:T(8,128)(2,1)}, u32[]{:S(2)}) copy-start(bf16[768,768]{1,0:T(8,128)(2,1)} %param.33) | copy-start | bytes 3538948

commit v11 on v10

--- a/solution.py
+++ b/solution.py
@@ -142,9 +142,9 @@
 
 def front_body(tp_size, ep_size, pieces, own_experts, head_dim, lens_ref, index_ref, gain_ref, shift_ref, b_out_ref, b_fc2_ref, x_ref, w_in_ref, w_out_ref, own_ref, *refs):
     biases, refs = refs[:4], refs[4:]
-    table_ref, o_ref, other_out, hidden_out, b_exp_ref, *refs = refs
+    table_ref, o_out, other_out, hidden_out, b_exp_ref, *refs = refs
     moved_refs, refs = refs[:len(pieces)], refs[len(pieces):]
-    (other_ref, hidden_ref, b_query_ref, b_value_ref, b_fc1_ref, first_ref, second_ref, later_ref, fc1_ref, fc2_ref, source_ref, total_ref, bias_buf, qkv_ref, context_ref, all_buf,
+    (o_ref, other_ref, hidden_ref, b_query_ref, b_value_ref, b_fc1_ref, first_ref, second_ref, later_ref, fc1_ref, fc2_ref, source_ref, total_ref, bias_buf, qkv_ref, context_ref, all_buf,
      load_sem, move_send, move_recv, tp_send, tp_recv, spread_sem, ring_send, ring_recv) = refs
     mine = lax.axis_index('tp')
     me = lax.axis_index('ep')
@@ -178,6 +178,7 @@
     load_x = pltpu.make_async_copy(x_ref.at[pl.ds(mine * own_rows, own_rows)], hidden_ref, load_sem.at[0])
     keep_other = pltpu.make_async_copy(other_ref, other_out, load_sem.at[1])
     keep_hidden = pltpu.make_async_copy(hidden_ref, hidden_out, load_sem.at[2])
+    keep_rows = pltpu.make_async_copy(o_ref, o_out, load_sem.at[3])
     load_x.start()
     enter([('tp', tp_size), ('ep', ep_size)])
     for copies in gathers:
@@ -394,7 +395,8 @@
         return carry
 
     lax.fori_loop(0, count, drain, 0)
-    for copy in [*moves, keep_hidden, keep_other]:
+    keep_rows.start()
+    for copy in [*moves, keep_hidden, keep_other, keep_rows]:
         copy.wait()
 
 
@@ -420,11 +422,11 @@
         functools.partial(front_body, tp_size, ep_size, pieces, own_experts, head_dim),
         out_shape=(jax.ShapeDtypeStruct((2 * rows * seq // 128, 128), jnp.int32), jax.ShapeDtypeStruct((slots, width), BF16), jax.ShapeDtypeStruct((slots, 1), jnp.int32),
                    jax.ShapeDtypeStruct((own_rows, seq, width), BF16), b_exp, *moved),
-        in_specs=[SMEM_SPEC] + [VMEM_SPEC] * 5 + [HBM_SPEC] * (4 + len(biases)), out_specs=[VMEM_SPEC] * 2 + [HBM_SPEC] * (3 + len(pieces)),
-        scratch_shapes=[vmem(slots, 1, dtype=jnp.int32), vmem(own_rows, seq, width), vmem(tp_size, *biases[0].shape, dtype=F32), vmem(tp_size, *biases[1].shape, dtype=F32), vmem(tp_size, *biases[2].shape, dtype=F32), pack, pack,
+        in_specs=[SMEM_SPEC] + [VMEM_SPEC] * 5 + [HBM_SPEC] * (4 + len(biases)), out_specs=[VMEM_SPEC] + [HBM_SPEC] * (4 + len(pieces)),
+        scratch_shapes=[vmem(slots, width), vmem(slots, 1, dtype=jnp.int32), vmem(own_rows, seq, width), vmem(tp_size, *biases[0].shape, dtype=F32), vmem(tp_size, *biases[1].shape, dtype=F32), vmem(tp_size, *biases[2].shape, dtype=F32), pack, pack,
                         vmem(packs - 1, tp_size, cut, width), vmem(tp_size, ep_size, cut, width), vmem(tp_size, ep_size, cut, width), vmem(slots, 1, dtype=jnp.int32),
                         vmem(3 * capacity, num_experts, dtype=F32), vmem(1, 3 * width, dtype=F32), vmem(seq, 3 * width), vmem(size, width),
-                        vmem(tp_size, own_rows, count, size, width), DMA((3,)), piece_dma, piece_dma, gather_dma, gather_dma, DMA((2, packs, ep_size)), ring_dma, ring_dma],
+                        vmem(tp_size, own_rows, count, size, width), DMA((4,)), piece_dma, piece_dma, gather_dma, gather_dma, DMA((2, packs, ep_size)), ring_dma, ring_dma],
         compiler_params=settings(call_id, 62), cost_estimate=cost(100), name='front')(lens, index, gain, shift, b_out, b_fc2, x, w_in, w_out, own, *biases)
 
 

time: 791 us -> 789 us (level)
  no operation moved by 1% of the time
where the time goes in v11:
time: 789 us
  Pallas kernels  772 us (98%)
  local copies, waits for them, and re-layouts  14.3 us (2%)
    pallas_call x1, Pallas kernels, front(): pl.pallas_call(functools.partial(front_body, tp_size, ep_size, pieces, ow...  406 us
    pallas_call x1, Pallas kernels, finish(): pl.pallas_call(functools.partial(finish_body, tp_size, count), out_shape=...  216 us
    pallas_call x1, Pallas kernels, experts(): pl.pallas_call(body, out_shape=(jax.ShapeDtypeStruct(dispatch.shape, BF16...  151 us

profile of v11, /device:TPU:97, one launch (start us, length us, event | category | flops | bytes accessed | tf_op | source)
XLA Modules:
  0.0 789.0 jit_solution(12421509629154426483)
XLA Ops:
  0.0 0.0 copy-start
  0.0 0.0 copy-start.2
  0.0 1.3 copy-done
  1.3 0.1 constant_dynamic-slice_fusion
  1.4 0.1 copy.23
  1.5 0.0 copy-start.3
  1.6 1.2 fusion.8
  2.7 0.0 copy-done.2
  2.7 0.0 copy-start.4
  2.8 0.0 copy-done.3
  2.8 1.0 copy-done.4
  3.8 1.2 dynamic-slice_bitcast_fusion
  5.0 0.3 fusion.7
  5.3 0.9 pad_maximum_fusion.own_ref
  6.2 405.7 %front.1 = (s32[128,128]{1,0:T(8,128)}, bf16[4096,768]{1,0:T(8,128)(2,1)}, s32[4096,1]{1,0:T(8,128)}, bf16[2,1024,768]{2,1,0:T(8,128)(2,1)}, f32[4,16,768]{2,1,0...) custom-call(s32[8]{0:T(128)} %lens_ref.1, ...), custom_call_target="tpu_custom_call" | custom-call | flops 99999997952 | bytes 10000000 | tf_op jit(solution)/shard_map/front/pallas_call | solution.py:421
  411.9 150.6 %experts.1 = (bf16[4,8,128,768]{3,2,1,0:T(8,128)(2,1)}, f32[4096,1]{1,0:T(8,128)}) custom-call(bf16[4,8,128,768]{3,2,1,0:T(8,128)(2,1)} %bitcast.54, bf16[3,768,256]{2,1,0:T(8,128)(2,1)} %get-tuple-element.22.refs_0_, bf16[3,768,768]{2,1,0:T(8,128)(2,1)} %get-tuple-element.23.refs_1_, bf16[3,768,768]{2,1,0:T(8,128)(2,1)} %get-tuple-element.24.refs_2_, ...), custom_call_target="tpu_custom_call" | custom-call | flops 30000001024 | bytes 10000000 | tf_op jit(solution)/shard_map/experts/pallas_call | solution.py:604
  562.5 215.9 %finish.1 = bf16[8192,768]{1,0:T(8,128)(2,1)} custom-call(s32[16384]{0:T(1024)} %bitcast.57, f32[4096,1]{1,0:T(8,128)} %get-tuple-element.32.gates_in, bf16[4096,768]{1,0:T(8,128)(2,1)} %bitcast.55, bf16[2048,768]{1,0:T(8,128)(2,1)} %bitcast.56), custom_call_target="tpu_custom_call" | custom-call | flops 99999997952 | bytes 10000000 | tf_op jit(solution)/shard_map/finish/pallas_call | solution.py:759
  778.4 0.0 copy-start.1
  778.4 10.6 %copy.25 = bf16[8,1024,768]{2,1,0:T(8,128)(2,1)} copy(bf16[8,1024,768]{2,1,0:T(8,128)(2,1)} %bitcast.39) | data formatting | bytes 25165824
  789.0 0.0 copy-done.1
  (3 shorter events, 0.1 us)
Async XLA Ops:
  0.0 1.3 copy-start
  0.0 2.7 copy-start.2
  1.5 1.2 copy-start.3
  2.7 1.1 copy-start.4
  778.4 10.6 %copy-start.1 = (bf16[768,768]{1,0:T(8,128)(2,1)S(1)}, bf16[768,768]{1,0:T(8,128)(2,1)}, u32[]{:S(2)}) copy-start(bf16[768,768]{1,0:T(8,128)(2,1)} %param.33) | copy-start | bytes 3538948
